TPU v7x, 8 devices: a whole 2x2x1 slice. The times are simulated.
8 devices in a mesh: row: 4 (over z, y, x), col: 2 (over core).
Axes of the slice: x: 2, y: 2, z: 1, core: 2. Of those that a mesh axis runs over, the one named last changes fastest.
Arguments:
- w_in: float32 [4, 2, 2, 1024, 4096], P('row', 'col')
- w_out: float32 [4, 2, 2, 4096, 1024], P('row', 'col')
- inputs: bfloat16 [4, 2, 4, 2048, 1024], P('row', 'col')
- targets: bfloat16 [4, 2, 4, 2048, 1024], P('row', 'col')
Outputs:
- output 1: float32 [4, 2, 2, 1024, 4096], P('row', 'col')
- output 2: float32 [4, 2, 2, 4096, 1024], P('row', 'col')
All inputs are finite; a program needn't handle non-finite values.
Results may differ from a plain program's by a relative error of at most 0.001.
Values are sent between devices in bfloat16 or wider.
A program may use at most 1 GiB of HBM per device.

v0:
```python
import jax
import jax.numpy as jnp
from jax import lax
from jax.sharding import PartitionSpec as P

LR_SCALE = 0.8
EPS = 1e-6
INV_SQRT2 = 0.7071067811865476
INV_SQRT_2PI = 0.3989422804014327
CONTRACT_ROWS = (((0,), (0,)), ((), ()))
CONTRACT_LAST = (((1,), (1,)), ((), ()))


def rms_norm(rows):
    return rows * lax.rsqrt(jnp.mean(rows * rows, axis=-1, keepdims=True) + EPS)


def rms_back(rows, grad_norm):
    inv_rms = lax.rsqrt(jnp.mean(rows * rows, axis=-1, keepdims=True) + EPS)
    row_dot = jnp.mean(rows * grad_norm, axis=-1, keepdims=True)
    return inv_rms * grad_norm - rows * (inv_rms * inv_rms * inv_rms) * row_dot


def gelu_exact(pre_act):
    return 0.5 * pre_act * (1.0 + lax.erf(pre_act * INV_SQRT2))


def gelu_slope(pre_act):
    return 0.5 * (1.0 + lax.erf(pre_act * INV_SQRT2)) + pre_act * jnp.exp(-0.5 * pre_act * pre_act) * INV_SQRT_2PI


def device_grads(w_in, w_out, rows_in, rows_tgt):
    layer_count = w_in.shape[0]
    hidden = rows_in
    saved_acts = []
    for layer_idx in range(layer_count):
        w1_bf = w_in[layer_idx].astype(jnp.bfloat16)
        w2_bf = w_out[layer_idx].astype(jnp.bfloat16)
        h_f32 = hidden.astype(jnp.float32)
        normed = rms_norm(h_f32).astype(jnp.bfloat16)
        pre_act = jnp.dot(normed, w1_bf, preferred_element_type=jnp.float32)
        act_bf = gelu_exact(pre_act).astype(jnp.bfloat16)
        hidden = (h_f32 + jnp.dot(act_bf, w2_bf, preferred_element_type=jnp.float32)).astype(jnp.bfloat16)
        saved_acts.append((w1_bf, w2_bf, h_f32, normed, pre_act, act_bf))
    grad_h = (hidden.astype(jnp.float32) - rows_tgt.astype(jnp.float32)) * (2.0 / rows_tgt.size)
    grads_in = [None] * layer_count
    grads_out = [None] * layer_count
    for layer_idx in reversed(range(layer_count)):
        w1_bf, w2_bf, h_f32, normed, pre_act, act_bf = saved_acts[layer_idx]
        grad_bf = grad_h.astype(jnp.bfloat16)
        grads_out[layer_idx] = lax.dot_general(act_bf, grad_bf, CONTRACT_ROWS, preferred_element_type=jnp.float32)
        d_pre = (lax.dot_general(grad_bf, w2_bf, CONTRACT_LAST, preferred_element_type=jnp.float32) * gelu_slope(pre_act)).astype(jnp.bfloat16)
        grads_in[layer_idx] = lax.dot_general(normed, d_pre, CONTRACT_ROWS, preferred_element_type=jnp.float32)
        if layer_idx > 0:
            grad_h = grad_h + rms_back(h_f32, lax.dot_general(d_pre, w1_bf, CONTRACT_LAST, preferred_element_type=jnp.float32))
    return jnp.stack(grads_in), jnp.stack(grads_out)


def solution(mesh):
    row_size = mesh.shape["row"]
    col_size = mesh.shape["col"]
    neighbour_moves = [
        ("col", [(src_idx, (src_idx + 1) % col_size) for src_idx in range(col_size)]),
        ("col", [(src_idx, (src_idx - 1) % col_size) for src_idx in range(col_size)]),
        ("row", [(src_idx, (src_idx + 1) % row_size) for src_idx in range(row_size)]),
        ("row", [(src_idx, (src_idx - 1) % row_size) for src_idx in range(row_size)]),
    ]

    def neighbour_mix(params):
        wire_copy = params.astype(jnp.bfloat16)
        mix_sum = params
        for axis_name, pair_list in neighbour_moves:
            mix_sum = mix_sum + lax.ppermute(wire_copy, axis_name, pair_list).astype(jnp.float32)
        return mix_sum / 5.0

    def device_program(w_in, w_out, inputs, targets):
        cur_in = w_in[0, 0]
        cur_out = w_out[0, 0]
        rows_all = inputs[0, 0]
        tgt_all = targets[0, 0]
        learn_rate = LR_SCALE / cur_in.shape[0]
        for window_idx in range(rows_all.shape[0] // 2):
            step_a = 2 * window_idx
            g_a_in, g_a_out = device_grads(cur_in, cur_out, rows_all[step_a], tgt_all[step_a])
            g_b_in, g_b_out = device_grads(cur_in - learn_rate * g_a_in, cur_out - learn_rate * g_a_out,
                                           rows_all[step_a + 1], tgt_all[step_a + 1])
            mixed_in = neighbour_mix(cur_in)
            mixed_out = neighbour_mix(cur_out)
            cur_in = mixed_in - learn_rate * (g_a_in + g_b_in)
            cur_out = mixed_out - learn_rate * (g_a_out + g_b_out)
        return cur_in[None, None], cur_out[None, None]

    block_spec = P("row", "col")
    return jax.shard_map(device_program, mesh=mesh,
                         in_specs=(block_spec, block_spec, block_spec, block_spec),
                         out_specs=(block_spec, block_spec), check_vma=False)
```

profile of v0, /device:TPU:0, one launch (start us, length us, event | category | flops | bytes accessed | tf_op | source)
XLA Modules:
  0.0 3230.9 jit_solution(7627753254003721555)
XLA Ops:
  0.6 35.5 %bitcast_convert_fusion.1 = (bf16[2,1024,4096]{2,1,0:T(8,128)(2,1)}, bf16[1,1,2,1024,4096]{4,3,2,1,0:T(8,128)(2,1)}) fusion(f32[1,1,2,1024,4096]{4,3,2,1,0:T(8,128)} %param.4), kind=kLoop, calls=%fused_computation.94 | loop fusion | flops 16777216 | bytes 67108864 | tf_op jit(solution)/shard_map/convert_element_type | solution.py:70
  42.4 11.9 bitcast_convert_fusion
  58.6 12.3 fusion.241
  70.8 6.5 copy.22
  80.5 30.3 multiply_convert_fusion.7
  110.8 24.5 fusion.120
  135.9 30.6 multiply_convert_fusion.6
  166.5 24.1 fusion.122
  190.6 12.2 fusion.240
  209.4 36.4 %fusion.9 = bf16[2048,4096]{1,0:T(8,128)(2,1)} fusion(f32[2048,4096]{1,0:T(8,128)} %get-tuple-element.31, bf16[1,1,2,4096,1024]{4,3,2,1,0:T(8,128)(2,1)} %get-tuple-element.7, bf16[2048,1024]{0,1:T(8,128)(2,1)} %fusion.122, bf16[1,1,1,2048,1024]{3,4,2,1,0:T(8,128)(2,1)} %copy.23), kind=kOutput, calls=%fused_computation.21 | convolution fusion | flops 17274241024 | bytes 67108864 | tf_op jit(solution)/shard_map/dot_general | solution.py:52
  245.8 23.4 convolution_bitcast_fusion.11
  269.2 23.5 fusion.127
  292.7 24.1 convolution_bitcast_fusion.9
  316.8 6.7 fusion.126
  323.5 24.0 convolution_bitcast_fusion.10
  347.5 34.0 %fusion.15.clone.7 = bf16[2048,4096]{1,0:T(8,128)(2,1)} fusion(f32[2048,4096]{1,0:T(8,128)} %get-tuple-element.27, bf16[2048,1024]{0,1:T(8,128)(2,1)S(1)} %copy-done.28, bf16[1,1,2,4096,1024]{4,3,2,1,0:T(8,128)(2,1)S(1)} %bitcast.345), kind=kOutput, calls=%fused_computation.27.clone.clone.clone.clone.clone.2 | convolution fusion | flops 17263755264 | bytes 62914560 | tf_op jit(solution)/shard_map/dot_general | solution.py:52
  381.5 22.2 fusion.100
  413.4 27.8 fusion.71
  441.2 30.6 multiply_convert_fusion.5
  471.8 27.5 fusion.70
  499.2 23.5 fusion.128
  523.5 29.8 multiply_convert_fusion.4
  553.3 23.9 fusion.130
  583.8 36.2 %fusion.21 = bf16[2048,4096]{1,0:T(8,128)(2,1)} fusion(f32[2048,4096]{1,0:T(8,128)} %get-tuple-element.39, bf16[2,4096,1024]{2,1,0:T(8,128)(2,1)} %fusion.70, bf16[2048,1024]{0,1:T(8,128)(2,1)} %fusion.130, bf16[1,1,1,2048,1024]{3,4,2,1,0:T(8,128)(2,1)} %copy.25), kind=kOutput, calls=%fused_computation.33 | convolution fusion | flops 17274241024 | bytes 67108864 | tf_op jit(solution)/shard_map/dot_general | solution.py:52
  619.9 23.3 fusion.135
  643.3 22.9 convolution_bitcast_fusion.8
  700.6 36.4 %fusion.27.clone.7 = bf16[2048,4096]{1,0:T(8,128)(2,1)} fusion(f32[2048,4096]{1,0:T(8,128)} %get-tuple-element.35, bf16[2048,1024]{0,1:T(8,128)(2,1)} %fusion.134, bf16[2,4096,1024]{2,1,0:T(8,128)(2,1)} %fusion.70), kind=kOutput, calls=%fused_computation.39.clone.clone.clone.clone.clone.2 | convolution fusion | flops 17263755264 | bytes 62914560 | tf_op jit(solution)/shard_map/dot_general | solution.py:52
  737.0 22.6 fusion.101
  761.1 22.7 convolution_bitcast_fusion.7
  783.8 23.0 convolution_bitcast_fusion.6
  806.8 64.8 %fusion.238 = (bf16[2,1024,4096]{2,1,0:T(8,128)(2,1)}, f32[2,1024,4096]{2,1,0:T(8,128)}) fusion(f32[1,1024,4096]{2,1,0:T(8,128)} %convolution_bitcast_fusion.8, f32[1,1024,4096]{2,1,0:T(8,128)} %fusion.101, f32[1,1024,4096]{2,1,0:T(8,128)} %convolution_bitcast_fusion.11, f32[1,1024,4096]{2,1,0:T(8,128)} %fusion.100, ...), kind=kLoop, calls=%fused_computation.331 | loop fusion | flops 117440512 | bytes 201326592 | tf_op jit(solution)/shard_map/convert_element_type | solution.py:70
  871.6 29.4 multiply_convert_fusion.3
  901.0 219.1 %collective-permute-done.8 = bf16[2,4096,1024]{2,1,0:T(8,128)(2,1)} collective-permute-done((bf16[2,4096,1024]{2,1,0:T(8,128)(2,1)}, bf16[2,4096,1024]{2,1,0:T(8,128)(2,1)}, u32[]{:S(2)}, u32[]{:S(2)}) %collective-permute-start.8) | collective-permute-done | bytes 16777248 | tf_op jit(solution)/shard_map/ppermute | solution.py:73
  1120.1 359.6 %collective-permute-done.7 = bf16[2,4096,1024]{2,1,0:T(8,128)(2,1)} collective-permute-done((bf16[2,4096,1024]{2,1,0:T(8,128)(2,1)}, bf16[2,4096,1024]{2,1,0:T(8,128)(2,1)}, u32[]{:S(2)}, u32[]{:S(2)}) %collective-permute-start.7) | collective-permute-done | bytes 16777248 | tf_op jit(solution)/shard_map/ppermute | solution.py:73
  1479.7 64.8 %fusion.236 = (bf16[2,4096,1024]{2,1,0:T(8,128)(2,1)}, f32[2,4096,1024]{2,1,0:T(8,128)}) fusion(f32[1,4096,1024]{2,1,0:T(8,128)} %convolution_bitcast_fusion.6, f32[1,4096,1024]{2,1,0:T(8,128)} %convolution_bitcast_fusion.7, f32[1,4096,1024]{2,1,0:T(8,128)} %convolution_bitcast_fusion.9, f32[1,4096,1024]{2,1,0:T(8,128)} %convolution_bitcast_fusion.10, ...), kind=kLoop, calls=%fused_computation.330 | loop fusion | flops 117440512 | bytes 201326592 | tf_op jit(solution)/shard_map/convert.14
  1544.5 24.7 fusion.136
  1569.8 30.5 multiply_convert_fusion.2
  1600.3 24.0 fusion.138
  1624.4 36.0 %fusion.42 = bf16[2048,4096]{1,0:T(8,128)(2,1)} fusion(f32[2048,4096]{1,0:T(8,128)} %get-tuple-element.47, bf16[2,4096,1024]{2,1,0:T(8,128)(2,1)} %get-tuple-element.2, bf16[2048,1024]{0,1:T(8,128)(2,1)} %fusion.138, bf16[1,1,1,2048,1024]{3,4,2,1,0:T(8,128)(2,1)} %copy.27), kind=kOutput, calls=%fused_computation.54 | convolution fusion | flops 17274241024 | bytes 67108864 | tf_op jit(solution)/shard_map/dot_general | solution.py:52
  1660.4 23.6 convolution_bitcast_fusion.5
  1684.0 23.3 fusion.143
  1707.3 24.1 convolution_bitcast_fusion.3
  1735.6 7.1 fusion.142
  1742.7 24.5 convolution_bitcast_fusion.4
  1767.3 33.7 %fusion.48.clone.4 = bf16[2048,4096]{1,0:T(8,128)(2,1)S(1)} fusion(f32[2048,4096]{1,0:T(8,128)} %get-tuple-element.43, bf16[2048,1024]{0,1:T(8,128)(2,1)S(1)} %copy-done.29, bf16[2,4096,1024]{2,1,0:T(8,128)(2,1)} %get-tuple-element.2), kind=kOutput, calls=%fused_computation.60.clone.clone.clone.clone.clone | convolution fusion | flops 17263755264 | bytes 62914560 | tf_op jit(solution)/shard_map/dot_general | solution.py:52
  1801.0 20.7 fusion.102
  1821.7 27.8 subtract_convert_fusion.1
  1849.5 30.2 multiply_convert_fusion.1
  1879.7 27.5 subtract_convert_fusion
  1907.2 23.7 fusion.144
  1931.0 30.3 multiply_convert_fusion
  1961.4 24.3 fusion.146
  1985.7 36.0 %fusion.54 = bf16[2048,4096]{1,0:T(8,128)(2,1)} fusion(f32[2048,4096]{1,0:T(8,128)} %get-tuple-element.55, bf16[2,4096,1024]{2,1,0:T(8,128)(2,1)} %subtract_convert_fusion, bf16[2048,1024]{0,1:T(8,128)(2,1)} %fusion.146, bf16[1,1,1,2048,1024]{3,4,2,1,0:T(8,128)(2,1)} %copy.29), kind=kOutput, calls=%fused_computation.66 | convolution fusion | flops 17274241024 | bytes 67108864 | tf_op jit(solution)/shard_map/dot_general | solution.py:52
  2021.6 23.5 fusion.151
  2051.1 36.9 %fusion.60.clone.4 = bf16[2048,4096]{1,0:T(8,128)(2,1)} fusion(f32[2048,4096]{1,0:T(8,128)} %get-tuple-element.51, bf16[2048,1024]{0,1:T(8,128)(2,1)S(1)} %fusion.150, bf16[2,4096,1024]{2,1,0:T(8,128)(2,1)} %subtract_convert_fusion), kind=kOutput, calls=%fused_computation.72.clone.clone.clone.clone.clone | convolution fusion | flops 17263755264 | bytes 62914560 | tf_op jit(solution)/shard_map/dot_general | solution.py:52
  2094.5 22.4 convolution_bitcast_fusion.2
  2116.9 22.4 fusion.103
  2139.3 22.7 convolution_bitcast_fusion.1
  2162.0 23.0 convolution_bitcast_fusion
  2185.0 268.7 %collective-permute-done.4 = bf16[2,1024,4096]{2,1,0:T(8,128)(2,1)} collective-permute-done((bf16[2,1024,4096]{2,1,0:T(8,128)(2,1)}, bf16[2,1024,4096]{2,1,0:T(8,128)(2,1)}, u32[]{:S(2)}, u32[]{:S(2)}) %collective-permute-start.4) | collective-permute-done | bytes 16777248 | tf_op jit(solution)/shard_map/ppermute | solution.py:73
  2453.7 59.0 %fusion.32 = f32[1,1,2,1024,4096]{4,3,2,1,0:T(8,128)} fusion(f32[2,1024,4096]{2,1,0:T(8,128)} %get-tuple-element.5, f32[1,1024,4096]{2,1,0:T(8,128)} %convolution_bitcast_fusion.2, f32[1,1024,4096]{2,1,0:T(8,128)} %fusion.103, bf16[2,1024,4096]{2,1,0:T(8,128)(2,1)} %collective-permute-done.5, bf16[2,1024,4096]{2,1,0:T(8,128)(2,1)} %collective-permute-done.4, ...), kind=kLoop, calls=%fused_computation.44 | loop fusion | flops 109051904 | bytes 184549376 | tf_op jit(solution)/shard_map/broadcast_in_dim | solution.py:91
  2512.7 300.8 %collective-permute-done.11 = bf16[2,4096,1024]{2,1,0:T(8,128)(2,1)} collective-permute-done((bf16[2,4096,1024]{2,1,0:T(8,128)(2,1)}, bf16[2,4096,1024]{2,1,0:T(8,128)(2,1)}, u32[]{:S(2)}, u32[]{:S(2)}) %collective-permute-start.11) | collective-permute-done | bytes 16777248 | tf_op jit(solution)/shard_map/ppermute | solution.py:73
  2813.6 357.6 %collective-permute-done.10 = bf16[2,4096,1024]{2,1,0:T(8,128)(2,1)} collective-permute-done((bf16[2,4096,1024]{2,1,0:T(8,128)(2,1)}, bf16[2,4096,1024]{2,1,0:T(8,128)(2,1)}, u32[]{:S(2)}, u32[]{:S(2)}) %collective-permute-start.10) | collective-permute-done | bytes 16777248 | tf_op jit(solution)/shard_map/ppermute | solution.py:73
  3171.2 59.3 %fusion.65 = f32[1,1,2,4096,1024]{4,3,2,1,0:T(8,128)} fusion(f32[2,4096,1024]{2,1,0:T(8,128)} %get-tuple-element.3, f32[1,4096,1024]{2,1,0:T(8,128)} %convolution_bitcast_fusion, f32[1,4096,1024]{2,1,0:T(8,128)} %convolution_bitcast_fusion.1, bf16[2,4096,1024]{2,1,0:T(8,128)(2,1)} %collective-permute-done.11, ...), kind=kLoop, calls=%fused_computation.77 | loop fusion | flops 109051904 | bytes 184549376 | tf_op jit(solution)/shard_map/broadcast_in_dim | solution.py:91
  (135 shorter events, 90.7 us)
Async XLA Ops:
  0.6 41.8 %copy-start = (f32[1,1,2,4096,1024]{4,3,2,1,0:T(8,128)S(1)}, f32[1,1,2,4096,1024]{4,3,2,1,0:T(8,128)}, u32[]{:S(2)}) copy-start(f32[1,1,2,4096,1024]{4,3,2,1,0:T(8,128)} %param.5) | copy-start | bytes 100663296
  36.2 723.4 %collective-permute-start.2 = (bf16[2,1024,4096]{2,1,0:T(8,128)(2,1)}, bf16[2,1024,4096]{2,1,0:T(8,128)(2,1)}, u32[]{:S(2)}, u32[]{:S(2)}) collective-permute-start(bf16[2,1024,4096]{2,1,0:T(8,128)(2,1)} %get-tuple-element.8), channel_id=1, source_target_pairs={{0,6},{2,0},{4,2},{6,4},{1,7},{3,1},{5,3},{7,5}} | collective-permute-start | bytes 50331656 | tf_op jit(solution)/shard_map/ppermute | solution.py:73
  40.4 766.3 %collective-permute-start.1 = (bf16[2,1024,4096]{2,1,0:T(8,128)(2,1)}, bf16[2,1024,4096]{2,1,0:T(8,128)(2,1)}, u32[]{:S(2)}, u32[]{:S(2)}) collective-permute-start(bf16[2,1024,4096]{2,1,0:T(8,128)(2,1)} %get-tuple-element.8), channel_id=1, source_target_pairs={{0,2},{2,4},{4,6},{6,0},{1,3},{3,5},{5,7},{7,1}} | collective-permute-start | bytes 50331656 | tf_op jit(solution)/shard_map/ppermute | solution.py:73
  40.5 766.3 %collective-permute-start = (bf16[2,1024,4096]{2,1,0:T(8,128)(2,1)}, bf16[2,1024,4096]{2,1,0:T(8,128)(2,1)}, u32[]{:S(2)}, u32[]{:S(2)}) collective-permute-start(bf16[2,1024,4096]{2,1,0:T(8,128)(2,1)} %get-tuple-element.8), channel_id=1, source_target_pairs={{0,1},{1,0},{2,3},{3,2},{4,5},{5,4},{6,7},{7,6}} | collective-permute-start | bytes 50331656 | tf_op jit(solution)/shard_map/ppermute | solution.py:73
  54.3 1065.8 %collective-permute-start.8 = (bf16[2,4096,1024]{2,1,0:T(8,128)(2,1)}, bf16[2,4096,1024]{2,1,0:T(8,128)(2,1)}, u32[]{:S(2)}, u32[]{:S(2)}) collective-permute-start(bf16[2,4096,1024]{2,1,0:T(8,128)(2,1)} %get-tuple-element.6), channel_id=1, source_target_pairs={{0,6},{2,0},{4,2},{6,4},{1,7},{3,1},{5,3},{7,5}} | collective-permute-start | bytes 50331656 | tf_op jit(solution)/shard_map/ppermute | solution.py:73
  58.6 1421.2 %collective-permute-start.7 = (bf16[2,4096,1024]{2,1,0:T(8,128)(2,1)}, bf16[2,4096,1024]{2,1,0:T(8,128)(2,1)}, u32[]{:S(2)}, u32[]{:S(2)}) collective-permute-start(bf16[2,4096,1024]{2,1,0:T(8,128)(2,1)} %get-tuple-element.6), channel_id=1, source_target_pairs={{0,2},{2,4},{4,6},{6,0},{1,3},{3,5},{5,7},{7,1}} | collective-permute-start | bytes 50331656 | tf_op jit(solution)/shard_map/ppermute | solution.py:73
  80.4 30.4 copy-start.37
  80.5 30.4 copy-start.11
  135.9 30.6 copy-start.22
  269.2 23.5 copy-start.6
  292.7 24.1 copy-start.23
  292.7 24.1 copy-start.31
  316.8 30.7 slice-start
  323.5 24.0 slice-start.1
  323.5 24.0 slice-start.2
  323.5 24.0 slice-start.3
  323.5 24.0 copy-start.28
  347.5 34.0 %copy-start.12 = (bf16[1,1,1,2048,1024]{3,4,2,1,0:T(8,128)(2,1)S(1)}, bf16[1,1,1,2048,1024]{3,4,2,1,0:T(8,128)(2,1)}, u32[]{:S(2)}) copy-start(bf16[1,1,1,2048,1024]{3,4,2,1,0:T(8,128)(2,1)} %copy.22) | copy-start | bytes 12582916
  347.5 34.0 %copy-start.38 = (f32[2048]{0:T(1024)S(1)}, f32[2048]{0:T(1024)}, u32[]{:S(2)}) copy-start(f32[2048]{0:T(1024)} %copy-done.37) | copy-start | bytes 24580
  413.4 27.8 copy-start.39
  522.8 30.5 copy-start.24
  619.9 23.4 copy-start.25
  643.3 23.0 copy-start.4
  643.3 23.0 copy-start.14
  643.3 23.0 copy-start.32
  700.6 36.4 %copy-start.13 = (bf16[1,1,1,2048,1024]{3,4,2,1,0:T(8,128)(2,1)S(1)}, bf16[1,1,1,2048,1024]{3,4,2,1,0:T(8,128)(2,1)}, u32[]{:S(2)}) copy-start(bf16[1,1,1,2048,1024]{3,4,2,1,0:T(8,128)(2,1)} %copy.24) | copy-start | bytes 12582916
  700.6 36.4 %copy-start.40 = (f32[2048]{0:T(1024)S(1)}, f32[2048]{0:T(1024)}, u32[]{:S(2)}) copy-start(f32[2048]{0:T(1024)} %copy-done.39) | copy-start | bytes 24580
  737.0 22.6 copy-start.7
  737.0 24.1 copy-start.19
  759.6 720.2 %collective-permute-start.6 = (bf16[2,4096,1024]{2,1,0:T(8,128)(2,1)}, bf16[2,4096,1024]{2,1,0:T(8,128)(2,1)}, u32[]{:S(2)}, u32[]{:S(2)}) collective-permute-start(bf16[2,4096,1024]{2,1,0:T(8,128)(2,1)} %get-tuple-element.6), channel_id=1, source_target_pairs={{0,1},{1,0},{2,3},{3,2},{4,5},{5,4},{6,7},{7,6}} | collective-permute-start | bytes 50331656 | tf_op jit(solution)/shard_map/ppermute | solution.py:73
  759.6 112.0 %copy-start.35 = (f32[2048]{0:T(1024)}, f32[2048]{0:T(1024)S(1)}, u32[]{:S(2)}) copy-start(f32[2048]{0:T(1024)S(1)} %add_rsqrt_fusion.3) | copy-start | bytes 24580
  761.1 22.7 copy-start.5
  761.1 22.7 copy-start.15
  806.8 64.8 %copy-start.9 = (bf16[1,1,1,2048,1024]{3,4,2,1,0:T(8,128)(2,1)S(1)}, bf16[1,1,1,2048,1024]{3,4,2,1,0:T(8,128)(2,1)}, u32[]{:S(2)}) copy-start(bf16[1,1,1,2048,1024]{3,4,2,1,0:T(8,128)(2,1)} %copy.26) | copy-start | bytes 12582916
  1569.8 30.5 copy-start.16
  1684.0 23.3 copy-start.3
  1707.3 28.3 copy-start.17
  1707.3 28.3 copy-start.30
  1731.4 363.1 %collective-permute-start.5 = (bf16[2,1024,4096]{2,1,0:T(8,128)(2,1)}, bf16[2,1024,4096]{2,1,0:T(8,128)(2,1)}, u32[]{:S(2)}, u32[]{:S(2)}) collective-permute-start(bf16[2,1024,4096]{2,1,0:T(8,128)(2,1)} %get-tuple-element.4), channel_id=1, source_target_pairs={{0,6},{2,0},{4,2},{6,4},{1,7},{3,1},{5,3},{7,5}} | collective-permute-start | bytes 50331656 | tf_op jit(solution)/shard_map/ppermute | solution.py:73
  1732.6 721.1 %collective-permute-start.4 = (bf16[2,1024,4096]{2,1,0:T(8,128)(2,1)}, bf16[2,1024,4096]{2,1,0:T(8,128)(2,1)}, u32[]{:S(2)}, u32[]{:S(2)}) collective-permute-start(bf16[2,1024,4096]{2,1,0:T(8,128)(2,1)} %get-tuple-element.4), channel_id=1, source_target_pairs={{0,2},{2,4},{4,6},{6,0},{1,3},{3,5},{5,7},{7,1}} | collective-permute-start | bytes 50331656 | tf_op jit(solution)/shard_map/ppermute | solution.py:73
  1733.4 720.3 %collective-permute-start.3 = (bf16[2,1024,4096]{2,1,0:T(8,128)(2,1)}, bf16[2,1024,4096]{2,1,0:T(8,128)(2,1)}, u32[]{:S(2)}, u32[]{:S(2)}) collective-permute-start(bf16[2,1024,4096]{2,1,0:T(8,128)(2,1)} %get-tuple-element.4), channel_id=1, source_target_pairs={{0,1},{1,0},{2,3},{3,2},{4,5},{5,4},{6,7},{7,6}} | collective-permute-start | bytes 50331656 | tf_op jit(solution)/shard_map/ppermute | solution.py:73
  1733.4 1080.1 %collective-permute-start.11 = (bf16[2,4096,1024]{2,1,0:T(8,128)(2,1)}, bf16[2,4096,1024]{2,1,0:T(8,128)(2,1)}, u32[]{:S(2)}, u32[]{:S(2)}) collective-permute-start(bf16[2,4096,1024]{2,1,0:T(8,128)(2,1)} %get-tuple-element.2), channel_id=1, source_target_pairs={{0,6},{2,0},{4,2},{6,4},{1,7},{3,1},{5,3},{7,5}} | collective-permute-start | bytes 50331656 | tf_op jit(solution)/shard_map/ppermute | solution.py:73
  1735.5 1435.6 %collective-permute-start.10 = (bf16[2,4096,1024]{2,1,0:T(8,128)(2,1)}, bf16[2,4096,1024]{2,1,0:T(8,128)(2,1)}, u32[]{:S(2)}, u32[]{:S(2)}) collective-permute-start(bf16[2,4096,1024]{2,1,0:T(8,128)(2,1)} %get-tuple-element.2), channel_id=1, source_target_pairs={{0,2},{2,4},{4,6},{6,0},{1,3},{3,5},{5,7},{7,1}} | collective-permute-start | bytes 50331656 | tf_op jit(solution)/shard_map/ppermute | solution.py:73
  1742.7 24.6 copy-start.29
  1767.3 33.7 %copy-start.10 = (bf16[1,1,1,2048,1024]{3,4,2,1,0:T(8,128)(2,1)S(1)}, bf16[1,1,1,2048,1024]{3,4,2,1,0:T(8,128)(2,1)}, u32[]{:S(2)}) copy-start(bf16[1,1,1,2048,1024]{3,4,2,1,0:T(8,128)(2,1)} %copy.26) | copy-start | bytes 12582916
  1767.3 33.7 %copy-start.36 = (f32[2048]{0:T(1024)S(1)}, f32[2048]{0:T(1024)}, u32[]{:S(2)}) copy-start(f32[2048]{0:T(1024)} %copy-done.35) | copy-start | bytes 24580
  1821.7 27.8 copy-start.33
  1931.0 30.4 copy-start.20
  2021.6 23.5 copy-start.1
  2051.1 37.0 %copy-start.26 = (bf16[2048,1024]{0,1:T(8,128)(2,1)}, bf16[2048,1024]{0,1:T(8,128)(2,1)S(1)}, u32[]{:S(2)}) copy-start(bf16[2048,1024]{0,1:T(8,128)(2,1)S(1)} %fusion.150) | copy-start | bytes 12582916
  2051.1 43.4 %copy-start.21 = (bf16[2048,1024]{0,1:T(8,128)(2,1)S(1)}, bf16[2048,1024]{0,1:T(8,128)(2,1)}, u32[]{:S(2)}) copy-start(bf16[2048,1024]{0,1:T(8,128)(2,1)} %copy-done.20) | copy-start | bytes 12582916
  2088.1 28.8 copy-start.8
  2088.1 28.8 copy-start.34
  2094.5 1076.7 %collective-permute-start.9 = (bf16[2,4096,1024]{2,1,0:T(8,128)(2,1)}, bf16[2,4096,1024]{2,1,0:T(8,128)(2,1)}, u32[]{:S(2)}, u32[]{:S(2)}) collective-permute-start(bf16[2,4096,1024]{2,1,0:T(8,128)(2,1)} %get-tuple-element.2), channel_id=1, source_target_pairs={{0,1},{1,0},{2,3},{3,2},{4,5},{5,4},{6,7},{7,6}} | collective-permute-start | bytes 50331656 | tf_op jit(solution)/shard_map/ppermute | solution.py:73
  2116.9 22.4 copy-start.27
  2139.3 22.7 copy-start.2
  2139.3 22.7 copy-start.18
where the time goes:
time: 3240 us; the launch traced here: 3230 us
  waiting for transfers between devices  1510 us (47%)
  matrix products  1180 us (36%)
  other arithmetic  443 us (14%)
  local copies, waits for them, and re-layouts  78.8 us (2%)
    ppermute x12, waiting for transfers between devices, neighbour_mix(): lax.ppermute(wire_copy, axis_name, pair_list).astype(jnp.float32)  1510 us
    dot_general x8, matrix products, device_grads(): lax.dot_general(grad_bf, w2_bf, CONTRACT_LAST, preferred_element_type=jnp...  286 us
    dot_general x8, matrix products, device_grads(): pre_act = jnp.dot(normed, w1_bf, preferred_element_type=jnp.float32)  242 us
    dot_general x8, matrix products, device_grads(): jnp.dot(act_bf, w2_bf, preferred_element_type=jnp.float32)  193 us
    dot_general x8, matrix products, device_grads(): lax.dot_general(act_bf, grad_bf, CONTRACT_ROWS, preferred_element_type=jn...  188 us
    dot_general x8, matrix products, device_grads(): lax.dot_general(normed, d_pre, CONTRACT_ROWS, preferred_element_type=jnp....  180 us
    another operation x5, other arithmetic  175 us
    broadcast_in_dim x2, other arithmetic, device_program(): return (cur_in[None, None], cur_out[None, None])  118 us
  transfers between devices with their start and end apart: 12, of which 6 were waited for; matrix products, arithmetic and copies ran while one was open for 42% of the time, Pallas kernels for 0%

commit v1 on v0

v1 whole, which is shorter than its diff:
```python
import functools

import jax
import jax.numpy as jnp
from jax import lax
from jax.experimental import pallas as pl
from jax.experimental.pallas import tpu as pltpu
from jax.sharding import PartitionSpec as P


LR_SCALE = 0.8
EPS = 1e-6
INV_SQRT2 = 0.7071067811865476
INV_SQRT_2PI = 0.3989422804014327
F32 = jnp.float32
BF16 = jnp.bfloat16
CONTRACT_ROWS = (((0,), (0,)), ((), ()))
CONTRACT_LAST = (((1,), (1,)), ((), ()))
VMEM_LIMIT = 63 * 1024 * 1024
TILE = 512
SLAB = 256
FWD_BLOCK = 512
BWD_BLOCK = 256
CHUNKS = 4
ANY = pl.BlockSpec(memory_space=pl.ANY)


def params_of(axes=1, limit=VMEM_LIMIT):
    return pltpu.CompilerParams(dimension_semantics=("arbitrary",) * axes, vmem_limit_bytes=limit)


def inv_rms_of(rows):
    return lax.rsqrt(jnp.mean(rows * rows, axis=-1, keepdims=True) + EPS)


def slabs(count, body):
    lax.fori_loop(0, count, lambda i, c: (body(pl.ds(pl.multiple_of(i * SLAB, SLAB), SLAB)), c)[1], 0)


def fwd_kernel(last, scale, t, *refs):
    if last:
        h_ref, w1_ref, w2_ref, tgt_hbm, act_ref, slope_ref, ut_hbm, hout_hbm, g_hbm, u_s, ut_s, acc, h_s, g_s, tgt_s, sems = refs
    else:
        h_ref, w1_ref, w2_ref, act_ref, slope_ref, ut_hbm, hout_hbm, u_s, ut_s, acc, h_s, sems = refs
    step = pl.program_id(0)
    rows_total = h_ref.shape[0]
    ut_copy = pltpu.make_async_copy(ut_s, ut_hbm, sems.at[0])
    hout_copy = pltpu.make_async_copy(h_s, hout_hbm, sems.at[1])
    if last:
        tgt_copy = pltpu.make_async_copy(tgt_hbm.at[0, 0, t], tgt_s, sems.at[2])
        g_copy = pltpu.make_async_copy(g_s, g_hbm, sems.at[3])

    @pl.when(step == 0)
    def _():
        if last:
            tgt_copy.start()

        for i in range(rows_total // SLAB):
            rows = pl.ds(i * SLAB, SLAB)
            h = h_ref[rows, :].astype(F32)
            u = h * inv_rms_of(h)
            u_s[rows, :] = u.astype(BF16)
            ut_s[:, rows] = u.T.astype(BF16)
            acc[rows, :] = jnp.zeros_like(h)
        ut_copy.start()

    for i in range(rows_total // TILE):
        rows = pl.ds(i * TILE, TILE)
        z = jnp.dot(u_s[rows, :], w1_ref[...], preferred_element_type=F32)
        half = 0.5 * (1.0 + lax.erf(z * INV_SQRT2))
        act = (z * half).astype(BF16)
        act_ref[rows, :] = act
        slope_ref[rows, :] = half + z * jnp.exp(-0.5 * z * z) * INV_SQRT_2PI
        acc[rows, :] += jnp.dot(act, w2_ref[...], preferred_element_type=F32)

    @pl.when(step == pl.num_programs(0) - 1)
    def _():
        if last:
            tgt_copy.wait()

        def finish(rows):
            h = (h_ref[rows, :].astype(F32) + acc[rows, :]).astype(BF16)
            h_s[rows, :] = h
            if last:
                g_s[rows, :] = ((h.astype(F32) - tgt_s[rows, :].astype(F32)) * scale).astype(BF16)

        slabs(rows_total // SLAB, finish)
        hout_copy.start()
        if last:
            g_copy.start()
        ut_copy.wait()
        hout_copy.wait()
        if last:
            g_copy.wait()


def forward(h, h_spec, w1, w2, target=None, scale=None, t=None):
    depth, ff = w1.shape
    rows = h.shape[-2]
    last = target is not None
    block = FWD_BLOCK
    in_specs = [
        h_spec or pl.BlockSpec((rows, depth), lambda j: (0, 0), pipeline_mode=pl.Buffered(1)),
        pl.BlockSpec((depth, block), lambda j: (0, j)),
        pl.BlockSpec((block, depth), lambda j: (j, 0)),
    ]
    out_shape = [
        jax.ShapeDtypeStruct((rows, ff), BF16),
        jax.ShapeDtypeStruct((rows, ff), F32),
        jax.ShapeDtypeStruct((depth, rows), BF16),
        jax.ShapeDtypeStruct((rows, depth), BF16),
    ]
    out_specs = [
        pl.BlockSpec((rows, block), lambda j: (0, j)),
        pl.BlockSpec((rows, block), lambda j: (0, j)),
        ANY,
        ANY,
    ]
    scratch = [
        pltpu.VMEM((rows, depth), BF16),
        pltpu.VMEM((depth, rows), BF16),
        pltpu.VMEM((rows, depth), F32),
        pltpu.VMEM((rows, depth), BF16),
    ]
    args = [h, w1, w2]
    if last:
        args.append(target)
        in_specs.append(ANY)
        out_shape.append(jax.ShapeDtypeStruct((rows, depth), BF16))
        out_specs.append(ANY)
        scratch += [pltpu.VMEM((rows, depth), BF16), pltpu.VMEM((rows, depth), BF16)]
    scratch.append(pltpu.SemaphoreType.DMA((4,)))
    return pl.pallas_call(
        functools.partial(fwd_kernel, last, scale, t),
        grid=(ff // block,),
        in_specs=in_specs, out_specs=out_specs, out_shape=out_shape, scratch_shapes=scratch,
        compiler_params=params_of(),
        cost_estimate=pl.CostEstimate(flops=4 * rows * depth * ff, bytes_accessed=rows * ff * 6 + depth * ff * 4,
                                      transcendentals=2 * rows * ff),
    )(*args)


def bwd_kernel(deep, second, scale, rate, t, *refs):
    refs = list(refs)
    g_ref, ut_ref, act_ref, slope_ref, w2_ref = refs[:5]
    rest = refs[5:]
    if deep:
        w1_ref, h_hbm, hl_hbm, tgt_hbm = rest[:4]
        rest = rest[4:]
    old1_ref, old2_ref = rest[:2]
    rest = rest[2:]
    d1_ref, d2_ref = rest[:2]
    rest = rest[2:]
    if not second:
        q1_ref, q2_ref = rest[:2]
        rest = rest[2:]
    if deep:
        gout_hbm = rest[0]
        rest = rest[1:]
    s_s = rest[0]
    if deep:
        acc, h_s, hl_s, tgt_s, gout_s, sems = rest[1:]
    step = pl.program_id(0)
    rows_total = g_ref.shape[0]
    if deep:
        loads = [pltpu.make_async_copy(src, dst, sems.at[i])
                 for i, (src, dst) in enumerate(((h_hbm, h_s), (hl_hbm, hl_s), (tgt_hbm.at[0, 0, t], tgt_s)))]
        gout_copy = pltpu.make_async_copy(gout_s, gout_hbm, sems.at[3])

        @pl.when(step == 0)
        def _():
            for load in loads:
                load.start()
            slabs(rows_total // SLAB, lambda rows: acc.__setitem__((rows, slice(None)), jnp.zeros((SLAB, acc.shape[1]), F32)))

    for i in range(rows_total // TILE):
        rows = pl.ds(i * TILE, TILE)
        back = lax.dot_general(g_ref[rows, :], w2_ref[...], CONTRACT_LAST, preferred_element_type=F32)
        s_s[rows, :] = (back * slope_ref[rows, :]).astype(BF16)

    d2 = lax.dot_general(act_ref[...], g_ref[...], CONTRACT_ROWS, preferred_element_type=F32)
    d1 = jnp.dot(ut_ref[...], s_s[...], preferred_element_type=F32)
    if second:
        d2_ref[...] = old2_ref[...] + d2
        d1_ref[...] = old1_ref[...] + d1
    else:
        d2_ref[...] = d2
        d1_ref[...] = d1
        q2_ref[...] = (old2_ref[...] - rate * d2).astype(BF16)
        q1_ref[...] = (old1_ref[...] - rate * d1).astype(BF16)
    if deep:
        for i in range(rows_total // TILE):
            rows = pl.ds(i * TILE, TILE)
            acc[rows, :] += lax.dot_general(s_s[rows, :], w1_ref[...], CONTRACT_LAST, preferred_element_type=F32)

        @pl.when(step == pl.num_programs(0) - 1)
        def _():
            for load in loads:
                load.wait()

            def finish(rows):
                h = h_s[rows, :].astype(F32)
                grad = acc[rows, :]
                inv_rms = inv_rms_of(h)
                row_dot = jnp.mean(h * grad, axis=-1, keepdims=True)
                e = (hl_s[rows, :].astype(F32) - tgt_s[rows, :].astype(F32)) * scale
                e = e + (inv_rms * grad - h * (inv_rms * inv_rms * inv_rms) * row_dot)
                gout_s[rows, :] = e.astype(BF16)

            slabs(rows_total // SLAB, finish)
            gout_copy.start()
            gout_copy.wait()


def backward(g, ut, act, slope, w1, w2, old1, old2, second, rate, layer, deep=None, scale=None, t=None):
    rows, ff = act.shape
    depth = g.shape[1]
    is_deep = deep is not None
    block = BWD_BLOCK
    if second:
        old1_spec = pl.BlockSpec((depth, block), lambda j: (0, j))
        old2_spec = pl.BlockSpec((block, depth), lambda j: (j, 0))
    else:
        old1_spec = pl.BlockSpec((None, None, None, depth, block), lambda j: (0, 0, layer, 0, j))
        old2_spec = pl.BlockSpec((None, None, None, block, depth), lambda j: (0, 0, layer, j, 0))
    once = pl.Buffered(1)
    args = [g, ut, act, slope, w2]
    in_specs = [
        pl.BlockSpec((rows, depth), lambda j: (0, 0), pipeline_mode=once),
        pl.BlockSpec((depth, rows), lambda j: (0, 0), pipeline_mode=once),
        pl.BlockSpec((rows, block), lambda j: (0, j)),
        pl.BlockSpec((rows, block), lambda j: (0, j)),
        pl.BlockSpec((block, depth), lambda j: (j, 0)),
    ]
    if is_deep:
        args += [w1, *deep]
        in_specs += [pl.BlockSpec((depth, block), lambda j: (0, j)), ANY, ANY, ANY]
    args += [old1, old2]
    in_specs += [old1_spec, old2_spec]
    out_shape = [jax.ShapeDtypeStruct((depth, ff), F32), jax.ShapeDtypeStruct((ff, depth), F32)]
    out_specs = [pl.BlockSpec((depth, block), lambda j: (0, j)), pl.BlockSpec((block, depth), lambda j: (j, 0))]
    if not second:
        out_shape += [jax.ShapeDtypeStruct((depth, ff), BF16), jax.ShapeDtypeStruct((ff, depth), BF16)]
        out_specs += out_specs[:2]
    scratch = [pltpu.VMEM((rows, block), BF16)]
    if is_deep:
        out_shape.append(jax.ShapeDtypeStruct((rows, depth), BF16))
        out_specs.append(ANY)
        scratch += [pltpu.VMEM((rows, depth), F32)] + [pltpu.VMEM((rows, depth), BF16)] * 4 + [pltpu.SemaphoreType.DMA((4,))]
    return pl.pallas_call(
        functools.partial(bwd_kernel, is_deep, second, scale, rate, t),
        grid=(ff // block,),
        in_specs=in_specs, out_specs=out_specs, out_shape=out_shape, scratch_shapes=scratch,
        compiler_params=params_of(),
        cost_estimate=pl.CostEstimate(flops=(8 if is_deep else 6) * rows * depth * ff,
                                      bytes_accessed=rows * ff * 6 + depth * ff * 24, transcendentals=0),
    )(*args)


def chunk_specs(shape, layer, part, steps):
    rows, cols = shape
    band = rows // CHUNKS // steps
    first = part * steps
    return (pl.BlockSpec((None, None, None, band, cols), lambda j: (0, 0, layer, first + j, 0)),
            pl.BlockSpec((band, cols), lambda j: (first + j, 0)),
            pl.BlockSpec((band, cols), lambda j: (j, 0)))


def cast_kernel(has_prev, p_ref, *refs):
    whole_ref, wire_ref = refs[1:] if has_prev else refs
    value = p_ref[...].astype(BF16)
    whole_ref[...] = value
    wire_ref[...] = value


def cast_chunk(p, layer, part, prev):
    shape = p.shape[-2:]
    steps = 2
    param_spec, layer_spec, wire_spec = chunk_specs(shape, layer, part, steps)
    return pl.pallas_call(
        functools.partial(cast_kernel, prev is not None),
        grid=(steps,),
        in_specs=[param_spec] + ([ANY] if prev is not None else []),
        out_specs=[layer_spec, wire_spec],
        out_shape=[jax.ShapeDtypeStruct(shape, BF16), jax.ShapeDtypeStruct((shape[0] // CHUNKS, shape[1]), BF16)],
        input_output_aliases={1: 0} if prev is not None else {},
        compiler_params=params_of(),
        cost_estimate=pl.CostEstimate(flops=10 ** 9, bytes_accessed=8 * shape[0] * shape[1] // CHUNKS, transcendentals=0),
    )(*([p] + ([prev] if prev is not None else [])))


def mix_kernel(rate, n_prev, final, par_ref, p_ref, grad_ref, col_ref, near_ref, far_ref, *refs):
    refs = refs[n_prev:]
    near = near_ref[...].astype(F32)
    far = far_ref[...].astype(F32)
    even = par_ref[0] == 0
    col = col_ref[...].astype(F32)
    mix = p_ref[...] + col + col
    mix = mix + jnp.where(even, far, near)
    mix = mix + jnp.where(even, near, far)
    new = mix / 5.0 - rate * grad_ref[...]
    refs[0][...] = new
    if not final:
        value = new.astype(BF16)
        refs[1][...] = value
        refs[2][...] = value


def mix_chunk(par, p, grad, col, near, far, layer, part, rate, prev_param, prev_layer, final):
    shape = p.shape[-2:]
    steps = 4
    param_spec, layer_spec, wire_spec = chunk_specs(shape, layer, part, steps)
    args = [par, p, grad, col, near, far]
    in_specs = [pl.BlockSpec(memory_space=pltpu.SMEM), param_spec, layer_spec, layer_spec, wire_spec, wire_spec]
    aliases = {}
    out_shape = [jax.ShapeDtypeStruct(p.shape, F32)]
    out_specs = [param_spec]
    if not final:
        out_shape += [jax.ShapeDtypeStruct(shape, BF16), jax.ShapeDtypeStruct((shape[0] // CHUNKS, shape[1]), BF16)]
        out_specs += [layer_spec, wire_spec]
    n_prev = 0
    for prev, out_idx in ((prev_param, 0), (None if final else prev_layer, 1)):
        if prev is not None:
            aliases[len(args)] = out_idx
            args.append(prev)
            in_specs.append(ANY)
            n_prev += 1
    return pl.pallas_call(
        functools.partial(mix_kernel, rate, n_prev, final),
        grid=(steps,),
        in_specs=in_specs, out_specs=out_specs, out_shape=out_shape,
        input_output_aliases=aliases,
        compiler_params=params_of(),
        cost_estimate=pl.CostEstimate(flops=10 ** 9, bytes_accessed=20 * shape[0] * shape[1] // CHUNKS, transcendentals=0),
    )(*args)


def solution(mesh):
    row_size = mesh.shape["row"]
    col_size = mesh.shape["col"]
    layers, windows = 2, 2
    near_pairs = [(i, i ^ 1) for i in range(row_size)]
    far_pairs = [(i, i ^ 2) for i in range(row_size)]
    col_pairs = [(i, (i + 1) % col_size) for i in range(col_size)]
    total = 2 * layers * CHUNKS

    def locate(i):
        return i // (2 * CHUNKS), (i // CHUNKS) % 2, i % CHUNKS

    def device_program(w_in, w_out, inputs, targets):
        batch, depth = inputs.shape[-2:]
        scale = 2.0 / (batch * depth)
        rate = LR_SCALE / layers
        par = (lax.axis_index("row") % 2).astype(jnp.int32).reshape(1)
        row_spec = lambda t: pl.BlockSpec((None, None, None, batch, depth), lambda j: (0, 0, t, 0, 0), pipeline_mode=pl.Buffered(1))

        def send(i, wire, weights):
            near = lax.ppermute(wire, "row", near_pairs)
            far = lax.ppermute(near, "row", far_pairs)
            cols = None
            if i % CHUNKS == CHUNKS - 1:
                layer, kind, _ = locate(i)
                cols = lax.ppermute(weights[layer][kind], "col", col_pairs)
            return near, far, cols

        def fwd(layer, h, weights, t):
            spec = row_spec(t) if layer == 0 else None
            if layer == layers - 1:
                return forward(h, spec, *weights[layer], target=targets, scale=scale, t=t)
            return forward(h, spec, *weights[layer])

        def grads(step, weights, t, olds, head=None):
            outs = head or run_forward(weights, t)
            g = outs[-1][4]
            found = [None] * layers
            for layer in reversed(range(layers)):
                act, slope, ut = outs[layer][:3]
                deep = (outs[layer - 1][3], outs[layer][3], targets) if layer else None
                res = backward(g, ut, act, slope,
                             *weights[layer], *olds[layer], step == 1, rate, layer, deep, scale, t)
                if layer:
                    g = res[-1]
                found[layer] = res
            return found

        def run_forward(weights, t):
            outs, h = [], inputs
            for layer in range(layers):
                outs.append(fwd(layer, h, weights, t))
                h = outs[-1][3]
            return outs

        params = [w_in, w_out]
        weights = [[None, None] for _ in range(layers)]
        moved = []
        for i in range(total):
            layer, kind, part = locate(i)
            weights[layer][kind], wire = cast_chunk(params[kind], layer, part, weights[layer][kind])
            moved.append(send(i, wire, weights))
        head = run_forward(weights, 0)
        for window in range(windows):
            final = window == windows - 1
            step_a = 2 * window
            first = grads(0, weights, step_a, [params] * layers, head)
            second = grads(1, [r[2:4] for r in first], step_a + 1, [r[:2] for r in first])
            new_params = [None, None]
            new_weights = [[None, None] for _ in range(layers)]
            new_moved, head = [], []
            for i in range(total):
                layer, kind, part = locate(i)
                near, far, _ = moved[i]
                cols = moved[i - i % CHUNKS + CHUNKS - 1][2]
                res = mix_chunk(par, params[kind], second[layer][kind], cols, near, far,
                             layer, part, rate, new_params[kind], new_weights[layer][kind], final)
                new_params[kind] = res[0]
                if not final:
                    new_weights[layer][kind] = res[1]
                    new_moved.append(send(i, res[2], new_weights))
                    if i % (2 * CHUNKS) == 2 * CHUNKS - 1:
                        h = inputs if layer == 0 else head[-1][3]
                        head.append(fwd(layer, h, new_weights, step_a + 2))
            params, weights, moved = new_params, new_weights, new_moved
        return params[0], params[1]

    block_spec = P("row", "col")
    return jax.shard_map(device_program, mesh=mesh, in_specs=(block_spec,) * 4, out_specs=(block_spec,) * 2, check_vma=False)
```

time: 3240 us -> 2680 us (0.83)
  Pallas kernels: 0 us -> 1390 us
  matrix products: 1180 us -> 0 us
  other arithmetic: 443 us -> 0 us
  waiting for transfers between devices: 1510 us -> 1200 us
  local copies, waits for them, and re-layouts: 78.8 us -> 0 us
  starting transfers between devices: 12.8 us -> 79.6 us
    pallas_call x0 -> x64, Pallas kernels: none -> 1390 us  [the longest x8 608 us: backward(): pl.pallas_call(functools.partial(bwd_kernel, is_deep, second, scale, rate...]
    dot_general x44 -> x0, matrix products: 1180 us -> none  [the longest x8 286 us: device_grads(): lax.dot_general(grad_bf, w2_bf, CONTRACT_LAST, preferred_element_type=jnp...]
    ppermute x12 -> x72, waiting for transfers between devices: 1510 us -> 1200 us  [the longest x32 805 us: send(): near = lax.ppermute(wire, 'row', near_pairs)]
    another operation x5 -> x0, other arithmetic: 175 us -> none
    convert_element_type x7 -> x0, other arithmetic: 137 us -> none  [the longest x3 112 us: neighbour_mix(): wire_copy = params.astype(jnp.bfloat16)]
    broadcast_in_dim x2 -> x0, other arithmetic: 118 us -> none  [device_program(): return (cur_in[None, None], cur_out[None, None])]
    ppermute x12 -> x72, starting transfers between devices: 12.8 us -> 79.6 us  [the longest x32 45.1 us: send(): near = lax.ppermute(wire, 'row', near_pairs)]
    unnamed x98 -> x0, local copies, waits for them, and re-layouts: 54.4 us -> none
  transfers between devices with their start and end apart: 12 -> 72, of which waited for: 6 -> 30; matrix products, arithmetic and copies ran while one was open for 42% -> 0% of each run, Pallas kernels for 0% -> 52%
where the time goes in v1:
time: 2680 us; the launch traced here: 2670 us
  Pallas kernels  1390 us (52%)
  waiting for transfers between devices  1200 us (45%)
  starting transfers between devices  79.6 us (3%)
    ppermute x32, waiting for transfers between devices, send(): near = lax.ppermute(wire, 'row', near_pairs)  805 us
    pallas_call x8, Pallas kernels, backward(): pl.pallas_call(functools.partial(bwd_kernel, is_deep, second, scale, rate...  608 us
    pallas_call x8, Pallas kernels, forward(): pl.pallas_call(functools.partial(fwd_kernel, last, scale, t), grid=(ff //...  450 us
    ppermute x32, waiting for transfers between devices, send(): far = lax.ppermute(near, 'row', far_pairs)  396 us
    pallas_call x32, Pallas kernels, mix_chunk(): pl.pallas_call(functools.partial(mix_kernel, rate, n_prev, final), grid=(...  270 us
    pallas_call x16, Pallas kernels, cast_chunk(): pl.pallas_call(functools.partial(cast_kernel, prev is not None), grid=(st...  60.2 us
  transfers between devices with their start and end apart: 72, of which 30 were waited for; matrix products, arithmetic and copies ran while one was open for 0% of the time, Pallas kernels for 52%

profile of v1, /device:TPU:0, one launch (start us, length us, event | category | flops | bytes accessed | tf_op | source)
XLA Modules:
  0.0 2668.3 jit_solution(18073687727369105889)
XLA Ops:
  68.2 54.7 %shard_map.67 = (bf16[2048,4096]{1,0:T(8,128)(2,1)}, f32[2048,4096]{1,0:T(8,128)}, bf16[1024,2048]{1,0:T(8,128)(2,1)}, bf16[2048,1024]{1,0:T(8,128)(2,1)}) custom-call(bf16[1,1,4,2048,1024]{4,3,2,1,0:T(8,128)(2,1)} %refs_0_.7, bf16[1024,4096]{1,0:T(8,128)(2,1)} %get-tuple-element.149.refs_1_, bf16[4096,1024]{1,0:T(8,128)(2,1)} %get-tuple-element.153.refs_2_.refs_4_), custom_call_target="tpu_custom_call" | custom-call | flops 34359738368 | bytes 67108864 | tf_op jit(solution)/shard_map/pallas_call | solution.py:133
  125.0 19.3 collective-permute-done.21.near_ref
  146.4 42.9 %collective-permute-done.19.near_ref = bf16[1024,1024]{1,0:T(8,128)(2,1)} collective-permute-done((bf16[1024,1024]{1,0:T(8,128)(2,1)}, bf16[1024,1024]{1,0:T(8,128)(2,1)}, u32[]{:S(2)}, u32[]{:S(2)}) %collective-permute-start.19) | collective-permute-done | bytes 2097184 | tf_op jit(solution)/shard_map/ppermute | solution.py:358
  191.3 42.9 %collective-permute-done.34.near_ref = bf16[1024,1024]{1,0:T(8,128)(2,1)} collective-permute-done((bf16[1024,1024]{1,0:T(8,128)(2,1)}, bf16[1024,1024]{1,0:T(8,128)(2,1)}, u32[]{:S(2)}, u32[]{:S(2)}) %collective-permute-start.34) | collective-permute-done | bytes 2097184 | tf_op jit(solution)/shard_map/ppermute | solution.py:358
  236.3 57.8 %shard_map.76 = (bf16[2048,4096]{1,0:T(8,128)(2,1)}, f32[2048,4096]{1,0:T(8,128)}, bf16[1024,2048]{1,0:T(8,128)(2,1)}, bf16[2048,1024]{1,0:T(8,128)(2,1)}, bf16[2048,1024]{1,0:T(8,128)(2,1)}) custom-call(bf16[2048,1024]{1,0:T(8,128)(2,1)} %get-tuple-element.154.refs_0_.refs_6_, bf16[1024,4096]{1,0:T(8,128)(2,1)} %get-tuple-element.158.refs_1_.refs_5_, ...), custom_call_target="tpu_custom_call" | custom-call | flops 34359738368 | bytes 67108864 | tf_op jit(solution)/shard_map/pallas_call | solution.py:133
  294.1 30.0 %collective-permute-done.30.near_ref = bf16[1024,1024]{1,0:T(8,128)(2,1)} collective-permute-done((bf16[1024,1024]{1,0:T(8,128)(2,1)}, bf16[1024,1024]{1,0:T(8,128)(2,1)}, u32[]{:S(2)}, u32[]{:S(2)}) %collective-permute-start.30) | collective-permute-done | bytes 2097184 | tf_op jit(solution)/shard_map/ppermute | solution.py:358
  326.2 42.9 %collective-permute-done.28.near_ref = bf16[1024,1024]{1,0:T(8,128)(2,1)} collective-permute-done((bf16[1024,1024]{1,0:T(8,128)(2,1)}, bf16[1024,1024]{1,0:T(8,128)(2,1)}, u32[]{:S(2)}, u32[]{:S(2)}) %collective-permute-start.28) | collective-permute-done | bytes 2097184 | tf_op jit(solution)/shard_map/ppermute | solution.py:358
  371.1 42.9 %collective-permute-done.16.near_ref = bf16[256,4096]{1,0:T(8,128)(2,1)} collective-permute-done((bf16[256,4096]{1,0:T(8,128)(2,1)}, bf16[256,4096]{1,0:T(8,128)(2,1)}, u32[]{:S(2)}, u32[]{:S(2)}) %collective-permute-start.16) | collective-permute-done | bytes 2097184 | tf_op jit(solution)/shard_map/ppermute | solution.py:358
  416.0 42.9 %collective-permute-done.14.near_ref = bf16[256,4096]{1,0:T(8,128)(2,1)} collective-permute-done((bf16[256,4096]{1,0:T(8,128)(2,1)}, bf16[256,4096]{1,0:T(8,128)(2,1)}, u32[]{:S(2)}, u32[]{:S(2)}) %collective-permute-start.14) | collective-permute-done | bytes 2097184 | tf_op jit(solution)/shard_map/ppermute | solution.py:358
  461.0 88.9 %shard_map.77 = (f32[1024,4096]{1,0:T(8,128)}, f32[4096,1024]{1,0:T(8,128)}, bf16[1024,4096]{1,0:T(8,128)(2,1)}, bf16[4096,1024]{1,0:T(8,128)(2,1)}, bf16[2048,1024]{1,0:T(8,128)(2,1)}) custom-call(bf16[2048,1024]{1,0:T(8,128)(2,1)} %get-tuple-element.163.refs_0_, bf16[1024,2048]{1,0:T(8,128)(2,1)} %get-tuple-element.164.refs_1_, ...), custom_call_target="tpu_custom_call" | custom-call | flops 68719476736 | bytes 150994944 | tf_op jit(solution)/shard_map/pallas_call | solution.py:250
  552.0 41.8 %collective-permute-done.7.near_ref = bf16[256,4096]{1,0:T(8,128)(2,1)} collective-permute-done((bf16[256,4096]{1,0:T(8,128)(2,1)}, bf16[256,4096]{1,0:T(8,128)(2,1)}, u32[]{:S(2)}, u32[]{:S(2)}) %collective-permute-start.7) | collective-permute-done | bytes 2097184 | tf_op jit(solution)/shard_map/ppermute | solution.py:358
  595.8 42.9 %collective-permute-done.5.near_ref = bf16[256,4096]{1,0:T(8,128)(2,1)} collective-permute-done((bf16[256,4096]{1,0:T(8,128)(2,1)}, bf16[256,4096]{1,0:T(8,128)(2,1)}, u32[]{:S(2)}, u32[]{:S(2)}) %collective-permute-start.5) | collective-permute-done | bytes 2097184 | tf_op jit(solution)/shard_map/ppermute | solution.py:358
  640.8 42.9 %collective-permute-done.3.near_ref = bf16[256,4096]{1,0:T(8,128)(2,1)} collective-permute-done((bf16[256,4096]{1,0:T(8,128)(2,1)}, bf16[256,4096]{1,0:T(8,128)(2,1)}, u32[]{:S(2)}, u32[]{:S(2)}) %collective-permute-start.3) | collective-permute-done | bytes 2097184 | tf_op jit(solution)/shard_map/ppermute | solution.py:358
  685.7 63.4 %shard_map.78 = (f32[1024,4096]{1,0:T(8,128)}, f32[4096,1024]{1,0:T(8,128)}, bf16[1024,4096]{1,0:T(8,128)(2,1)}, bf16[4096,1024]{1,0:T(8,128)(2,1)}) custom-call(bf16[2048,1024]{1,0:T(8,128)(2,1)} %get-tuple-element.168.refs_0_, bf16[1024,2048]{1,0:T(8,128)(2,1)} %get-tuple-element.169.refs_1_, bf16[2048,4096]{1,0:T(8,128)(2,1)} %get-tuple-element.170.refs_2_, ...), custom_call_target="tpu_custom_call" | custom-call | flops 51539607552 | bytes 150994944 | tf_op jit(solution)/shard_map/pallas_call | solution.py:250
  753.2 54.9 %shard_map.79 = (bf16[2048,4096]{1,0:T(8,128)(2,1)}, f32[2048,4096]{1,0:T(8,128)}, bf16[1024,2048]{1,0:T(8,128)(2,1)}, bf16[2048,1024]{1,0:T(8,128)(2,1)}) custom-call(bf16[1,1,4,2048,1024]{4,3,2,1,0:T(8,128)(2,1)} %refs_0_.7, bf16[1024,4096]{1,0:T(8,128)(2,1)} %get-tuple-element.172.refs_1_, bf16[4096,1024]{1,0:T(8,128)(2,1)} %get-tuple-element.173.refs_2_.refs_4_), custom_call_target="tpu_custom_call" | custom-call | flops 34359738368 | bytes 67108864 | tf_op jit(solution)/shard_map/pallas_call | solution.py:133
  808.2 34.7 %collective-permute-done.33.far_ref = bf16[1024,1024]{1,0:T(8,128)(2,1)} collective-permute-done((bf16[1024,1024]{1,0:T(8,128)(2,1)}, bf16[1024,1024]{1,0:T(8,128)(2,1)}, u32[]{:S(2)}, u32[]{:S(2)}) %collective-permute-start.33) | collective-permute-done | bytes 2097184 | tf_op jit(solution)/shard_map/ppermute | solution.py:359
  842.9 44.9 %collective-permute-done.31.far_ref = bf16[1024,1024]{1,0:T(8,128)(2,1)} collective-permute-done((bf16[1024,1024]{1,0:T(8,128)(2,1)}, bf16[1024,1024]{1,0:T(8,128)(2,1)}, u32[]{:S(2)}, u32[]{:S(2)}) %collective-permute-start.31) | collective-permute-done | bytes 2097184 | tf_op jit(solution)/shard_map/ppermute | solution.py:359
  887.8 44.9 %collective-permute-done.29.far_ref = bf16[1024,1024]{1,0:T(8,128)(2,1)} collective-permute-done((bf16[1024,1024]{1,0:T(8,128)(2,1)}, bf16[1024,1024]{1,0:T(8,128)(2,1)}, u32[]{:S(2)}, u32[]{:S(2)}) %collective-permute-start.29) | collective-permute-done | bytes 2097184 | tf_op jit(solution)/shard_map/ppermute | solution.py:359
  932.8 44.9 %collective-permute-done.17.far_ref = bf16[256,4096]{1,0:T(8,128)(2,1)} collective-permute-done((bf16[256,4096]{1,0:T(8,128)(2,1)}, bf16[256,4096]{1,0:T(8,128)(2,1)}, u32[]{:S(2)}, u32[]{:S(2)}) %collective-permute-start.17) | collective-permute-done | bytes 2097184 | tf_op jit(solution)/shard_map/ppermute | solution.py:359
  977.7 57.5 %shard_map.80 = (bf16[2048,4096]{1,0:T(8,128)(2,1)}, f32[2048,4096]{1,0:T(8,128)}, bf16[1024,2048]{1,0:T(8,128)(2,1)}, bf16[2048,1024]{1,0:T(8,128)(2,1)}, bf16[2048,1024]{1,0:T(8,128)(2,1)}) custom-call(bf16[2048,1024]{1,0:T(8,128)(2,1)} %get-tuple-element.174.refs_0_.refs_6_, bf16[1024,4096]{1,0:T(8,128)(2,1)} %get-tuple-element.175.refs_1_.refs_5_, ...), custom_call_target="tpu_custom_call" | custom-call | flops 34359738368 | bytes 67108864 | tf_op jit(solution)/shard_map/pallas_call | solution.py:133
  1035.3 29.3 %collective-permute-done.13.far_ref = bf16[256,4096]{1,0:T(8,128)(2,1)} collective-permute-done((bf16[256,4096]{1,0:T(8,128)(2,1)}, bf16[256,4096]{1,0:T(8,128)(2,1)}, u32[]{:S(2)}, u32[]{:S(2)}) %collective-permute-start.13) | collective-permute-done | bytes 2097184 | tf_op jit(solution)/shard_map/ppermute | solution.py:359
  1064.7 88.5 %shard_map.81 = (f32[1024,4096]{1,0:T(8,128)}, f32[4096,1024]{1,0:T(8,128)}, bf16[2048,1024]{1,0:T(8,128)(2,1)}) custom-call(bf16[2048,1024]{1,0:T(8,128)(2,1)} %get-tuple-element.177.refs_0_, bf16[1024,2048]{1,0:T(8,128)(2,1)} %get-tuple-element.178.refs_1_, bf16[2048,4096]{1,0:T(8,128)(2,1)} %get-tuple-element.179.refs_2_, ...), custom_call_target="tpu_custom_call" | custom-call | flops 68719476736 | bytes 150994944 | tf_op jit(solution)/shard_map/pallas_call | solution.py:250
  1157.3 63.1 %shard_map.82 = (f32[1024,4096]{1,0:T(8,128)}, f32[4096,1024]{1,0:T(8,128)}) custom-call(bf16[2048,1024]{1,0:T(8,128)(2,1)} %get-tuple-element.189.refs_0_, bf16[1024,2048]{1,0:T(8,128)(2,1)} %get-tuple-element.190.refs_1_, bf16[2048,4096]{1,0:T(8,128)(2,1)} %get-tuple-element.191.refs_2_, f32[2048,4096]{1,0:T(8,128)} %get-tuple-element.192.refs_3_, ...), custom_call_target="tpu_custom_call" | custom-call | flops 51539607552 | bytes 150994944 | tf_op jit(solution)/shard_map/pallas_call | solution.py:250
  1220.4 9.1 shard_map.91
  1229.5 9.1 shard_map.92
  1238.6 9.1 shard_map.93
  1247.7 9.1 shard_map.94
  1256.8 9.1 shard_map.96
  1265.9 9.1 shard_map.97
  1275.0 9.1 shard_map.98
  1284.0 9.1 shard_map.99
  1293.1 9.3 shard_map.83
  1302.4 9.1 shard_map.84
  1311.5 9.0 shard_map.85
  1320.5 9.0 shard_map.86
  1331.6 9.1 shard_map.87
  1342.6 9.1 shard_map.88
  1351.9 9.1 shard_map.89
  1362.9 9.0 shard_map.90
  1371.9 54.8 %shard_map.95 = (bf16[2048,4096]{1,0:T(8,128)(2,1)}, f32[2048,4096]{1,0:T(8,128)}, bf16[1024,2048]{1,0:T(8,128)(2,1)}, bf16[2048,1024]{1,0:T(8,128)(2,1)}) custom-call(bf16[1,1,4,2048,1024]{4,3,2,1,0:T(8,128)(2,1)} %refs_0_.7, bf16[1024,4096]{1,0:T(8,128)(2,1)} %get-tuple-element.214.refs_1_, bf16[4096,1024]{1,0:T(8,128)(2,1)} %get-tuple-element.226.refs_2_.refs_4_), custom_call_target="tpu_custom_call" | custom-call | flops 34359738368 | bytes 67108864 | tf_op jit(solution)/shard_map/pallas_call | solution.py:133
  1428.8 39.5 %collective-permute-done.66.near_ref = bf16[1024,1024]{1,0:T(8,128)(2,1)} collective-permute-done((bf16[1024,1024]{1,0:T(8,128)(2,1)}, bf16[1024,1024]{1,0:T(8,128)(2,1)}, u32[]{:S(2)}, u32[]{:S(2)}) %collective-permute-start.66) | collective-permute-done | bytes 2097184 | tf_op jit(solution)/shard_map/ppermute | solution.py:358
  1470.1 43.1 %collective-permute-done.64.near_ref = bf16[1024,1024]{1,0:T(8,128)(2,1)} collective-permute-done((bf16[1024,1024]{1,0:T(8,128)(2,1)}, bf16[1024,1024]{1,0:T(8,128)(2,1)}, u32[]{:S(2)}, u32[]{:S(2)}) %collective-permute-start.64) | collective-permute-done | bytes 2097184 | tf_op jit(solution)/shard_map/ppermute | solution.py:358
  1515.1 43.1 %collective-permute-done.61.near_ref = bf16[1024,1024]{1,0:T(8,128)(2,1)} collective-permute-done((bf16[1024,1024]{1,0:T(8,128)(2,1)}, bf16[1024,1024]{1,0:T(8,128)(2,1)}, u32[]{:S(2)}, u32[]{:S(2)}) %collective-permute-start.61) | collective-permute-done | bytes 2097184 | tf_op jit(solution)/shard_map/ppermute | solution.py:358
  1560.0 57.4 %shard_map.100 = (bf16[2048,4096]{1,0:T(8,128)(2,1)}, f32[2048,4096]{1,0:T(8,128)}, bf16[1024,2048]{1,0:T(8,128)(2,1)}, bf16[2048,1024]{1,0:T(8,128)(2,1)}, bf16[2048,1024]{1,0:T(8,128)(2,1)}) custom-call(bf16[2048,1024]{1,0:T(8,128)(2,1)} %get-tuple-element.227.refs_0_.refs_6_, bf16[1024,4096]{1,0:T(8,128)(2,1)} %get-tuple-element.228.refs_1_.refs_5_, ...), custom_call_target="tpu_custom_call" | custom-call | flops 34359738368 | bytes 67108864 | tf_op jit(solution)/shard_map/pallas_call | solution.py:133
  1617.6 30.4 %collective-permute-done.57.near_ref = bf16[1024,1024]{1,0:T(8,128)(2,1)} collective-permute-done((bf16[1024,1024]{1,0:T(8,128)(2,1)}, bf16[1024,1024]{1,0:T(8,128)(2,1)}, u32[]{:S(2)}, u32[]{:S(2)}) %collective-permute-start.57) | collective-permute-done | bytes 2097184 | tf_op jit(solution)/shard_map/ppermute | solution.py:358
  1649.9 43.1 %collective-permute-done.55.near_ref = bf16[1024,1024]{1,0:T(8,128)(2,1)} collective-permute-done((bf16[1024,1024]{1,0:T(8,128)(2,1)}, bf16[1024,1024]{1,0:T(8,128)(2,1)}, u32[]{:S(2)}, u32[]{:S(2)}) %collective-permute-start.55) | collective-permute-done | bytes 2097184 | tf_op jit(solution)/shard_map/ppermute | solution.py:358
  1694.8 43.1 %collective-permute-done.52.near_ref = bf16[256,4096]{1,0:T(8,128)(2,1)} collective-permute-done((bf16[256,4096]{1,0:T(8,128)(2,1)}, bf16[256,4096]{1,0:T(8,128)(2,1)}, u32[]{:S(2)}, u32[]{:S(2)}) %collective-permute-start.52) | collective-permute-done | bytes 2097184 | tf_op jit(solution)/shard_map/ppermute | solution.py:358
  1739.8 43.1 %collective-permute-done.50.near_ref = bf16[256,4096]{1,0:T(8,128)(2,1)} collective-permute-done((bf16[256,4096]{1,0:T(8,128)(2,1)}, bf16[256,4096]{1,0:T(8,128)(2,1)}, u32[]{:S(2)}, u32[]{:S(2)}) %collective-permute-start.50) | collective-permute-done | bytes 2097184 | tf_op jit(solution)/shard_map/ppermute | solution.py:358
  1784.7 89.0 %shard_map.101 = (f32[1024,4096]{1,0:T(8,128)}, f32[4096,1024]{1,0:T(8,128)}, bf16[1024,4096]{1,0:T(8,128)(2,1)}, bf16[4096,1024]{1,0:T(8,128)(2,1)}, bf16[2048,1024]{1,0:T(8,128)(2,1)}) custom-call(bf16[2048,1024]{1,0:T(8,128)(2,1)} %get-tuple-element.242.refs_0_, bf16[1024,2048]{1,0:T(8,128)(2,1)} %get-tuple-element.243.refs_1_, ...), custom_call_target="tpu_custom_call" | custom-call | flops 68719476736 | bytes 150994944 | tf_op jit(solution)/shard_map/pallas_call | solution.py:250
  1875.8 41.8 %collective-permute-done.43.near_ref = bf16[256,4096]{1,0:T(8,128)(2,1)} collective-permute-done((bf16[256,4096]{1,0:T(8,128)(2,1)}, bf16[256,4096]{1,0:T(8,128)(2,1)}, u32[]{:S(2)}, u32[]{:S(2)}) %collective-permute-start.43) | collective-permute-done | bytes 2097184 | tf_op jit(solution)/shard_map/ppermute | solution.py:358
  1919.6 43.0 %collective-permute-done.41.near_ref = bf16[256,4096]{1,0:T(8,128)(2,1)} collective-permute-done((bf16[256,4096]{1,0:T(8,128)(2,1)}, bf16[256,4096]{1,0:T(8,128)(2,1)}, u32[]{:S(2)}, u32[]{:S(2)}) %collective-permute-start.41) | collective-permute-done | bytes 2097184 | tf_op jit(solution)/shard_map/ppermute | solution.py:358
  1964.5 43.0 %collective-permute-done.39.near_ref = bf16[256,4096]{1,0:T(8,128)(2,1)} collective-permute-done((bf16[256,4096]{1,0:T(8,128)(2,1)}, bf16[256,4096]{1,0:T(8,128)(2,1)}, u32[]{:S(2)}, u32[]{:S(2)}) %collective-permute-start.39) | collective-permute-done | bytes 2097184 | tf_op jit(solution)/shard_map/ppermute | solution.py:358
  2009.5 63.4 %shard_map.102 = (f32[1024,4096]{1,0:T(8,128)}, f32[4096,1024]{1,0:T(8,128)}, bf16[1024,4096]{1,0:T(8,128)(2,1)}, bf16[4096,1024]{1,0:T(8,128)(2,1)}) custom-call(bf16[2048,1024]{1,0:T(8,128)(2,1)} %get-tuple-element.248.refs_0_, bf16[1024,2048]{1,0:T(8,128)(2,1)} %get-tuple-element.249.refs_1_, bf16[2048,4096]{1,0:T(8,128)(2,1)} %get-tuple-element.250.refs_2_, ...), custom_call_target="tpu_custom_call" | custom-call | flops 51539607552 | bytes 150994944 | tf_op jit(solution)/shard_map/pallas_call | solution.py:250
  2077.1 55.2 %shard_map.103 = (bf16[2048,4096]{1,0:T(8,128)(2,1)}, f32[2048,4096]{1,0:T(8,128)}, bf16[1024,2048]{1,0:T(8,128)(2,1)}, bf16[2048,1024]{1,0:T(8,128)(2,1)}) custom-call(bf16[1,1,4,2048,1024]{4,3,2,1,0:T(8,128)(2,1)} %refs_0_.7, bf16[1024,4096]{1,0:T(8,128)(2,1)} %get-tuple-element.252.refs_1_, bf16[4096,1024]{1,0:T(8,128)(2,1)} %get-tuple-element.253.refs_2_.refs_4_), custom_call_target="tpu_custom_call" | custom-call | flops 34359738368 | bytes 67108864 | tf_op jit(solution)/shard_map/pallas_call | solution.py:133
  2132.3 34.3 %collective-permute-done.60.far_ref = bf16[1024,1024]{1,0:T(8,128)(2,1)} collective-permute-done((bf16[1024,1024]{1,0:T(8,128)(2,1)}, bf16[1024,1024]{1,0:T(8,128)(2,1)}, u32[]{:S(2)}, u32[]{:S(2)}) %collective-permute-start.60) | collective-permute-done | bytes 2097184 | tf_op jit(solution)/shard_map/ppermute | solution.py:359
  2166.7 44.9 %collective-permute-done.58.far_ref = bf16[1024,1024]{1,0:T(8,128)(2,1)} collective-permute-done((bf16[1024,1024]{1,0:T(8,128)(2,1)}, bf16[1024,1024]{1,0:T(8,128)(2,1)}, u32[]{:S(2)}, u32[]{:S(2)}) %collective-permute-start.58) | collective-permute-done | bytes 2097184 | tf_op jit(solution)/shard_map/ppermute | solution.py:359
  2211.6 44.9 %collective-permute-done.56.far_ref = bf16[1024,1024]{1,0:T(8,128)(2,1)} collective-permute-done((bf16[1024,1024]{1,0:T(8,128)(2,1)}, bf16[1024,1024]{1,0:T(8,128)(2,1)}, u32[]{:S(2)}, u32[]{:S(2)}) %collective-permute-start.56) | collective-permute-done | bytes 2097184 | tf_op jit(solution)/shard_map/ppermute | solution.py:359
  2256.7 44.8 %collective-permute-done.53.far_ref = bf16[256,4096]{1,0:T(8,128)(2,1)} collective-permute-done((bf16[256,4096]{1,0:T(8,128)(2,1)}, bf16[256,4096]{1,0:T(8,128)(2,1)}, u32[]{:S(2)}, u32[]{:S(2)}) %collective-permute-start.53) | collective-permute-done | bytes 2097184 | tf_op jit(solution)/shard_map/ppermute | solution.py:359
  2301.6 57.3 %shard_map.104 = (bf16[2048,4096]{1,0:T(8,128)(2,1)}, f32[2048,4096]{1,0:T(8,128)}, bf16[1024,2048]{1,0:T(8,128)(2,1)}, bf16[2048,1024]{1,0:T(8,128)(2,1)}, bf16[2048,1024]{1,0:T(8,128)(2,1)}) custom-call(bf16[2048,1024]{1,0:T(8,128)(2,1)} %get-tuple-element.254.refs_0_.refs_6_, bf16[1024,4096]{1,0:T(8,128)(2,1)} %get-tuple-element.255.refs_1_.refs_5_, ...), custom_call_target="tpu_custom_call" | custom-call | flops 34359738368 | bytes 67108864 | tf_op jit(solution)/shard_map/pallas_call | solution.py:133
  2359.0 27.7 %collective-permute-done.49.far_ref = bf16[256,4096]{1,0:T(8,128)(2,1)} collective-permute-done((bf16[256,4096]{1,0:T(8,128)(2,1)}, bf16[256,4096]{1,0:T(8,128)(2,1)}, u32[]{:S(2)}, u32[]{:S(2)}) %collective-permute-start.49) | collective-permute-done | bytes 2097184 | tf_op jit(solution)/shard_map/ppermute | solution.py:359
  2388.5 88.2 %shard_map.105 = (f32[1024,4096]{1,0:T(8,128)}, f32[4096,1024]{1,0:T(8,128)}, bf16[2048,1024]{1,0:T(8,128)(2,1)}) custom-call(bf16[2048,1024]{1,0:T(8,128)(2,1)} %get-tuple-element.257.refs_0_, bf16[1024,2048]{1,0:T(8,128)(2,1)} %get-tuple-element.258.refs_1_, bf16[2048,4096]{1,0:T(8,128)(2,1)} %get-tuple-element.259.refs_2_, ...), custom_call_target="tpu_custom_call" | custom-call | flops 68719476736 | bytes 150994944 | tf_op jit(solution)/shard_map/pallas_call | solution.py:250
  2480.8 63.1 %shard_map.106 = (f32[1024,4096]{1,0:T(8,128)}, f32[4096,1024]{1,0:T(8,128)}) custom-call(bf16[2048,1024]{1,0:T(8,128)(2,1)} %get-tuple-element.269.refs_0_, bf16[1024,2048]{1,0:T(8,128)(2,1)} %get-tuple-element.270.refs_1_, bf16[2048,4096]{1,0:T(8,128)(2,1)} %get-tuple-element.271.refs_2_, f32[2048,4096]{1,0:T(8,128)} %get-tuple-element.272.refs_3_, ...), custom_call_target="tpu_custom_call" | custom-call | flops 51539607552 | bytes 150994944 | tf_op jit(solution)/shard_map/pallas_call | solution.py:250
  2613.5 8.0 shard_map.108.refs_0_
  2621.5 7.8 shard_map.109.refs_0_
  (144 shorter events, 248.2 us)
Async XLA Ops:
  4.4 118.6 %collective-permute-start.25 = (bf16[1024,1024]{1,0:T(8,128)(2,1)}, bf16[1024,1024]{1,0:T(8,128)(2,1)}, u32[]{:S(2)}, u32[]{:S(2)}) collective-permute-start(bf16[1024,1024]{1,0:T(8,128)(2,1)} %get-tuple-element.219), channel_id=1, source_target_pairs={{0,2},{2,0},{4,6},{6,4},{1,3},{3,1},{5,7},{7,5}} | collective-permute-start | bytes 6291464 | tf_op jit(solution)/shard_map/ppermute | solution.py:358
  11.4 111.6 %collective-permute-start.23 = (bf16[1024,1024]{1,0:T(8,128)(2,1)}, bf16[1024,1024]{1,0:T(8,128)(2,1)}, u32[]{:S(2)}, u32[]{:S(2)}) collective-permute-start(bf16[1024,1024]{1,0:T(8,128)(2,1)} %get-tuple-element.218), channel_id=1, source_target_pairs={{0,2},{2,0},{4,6},{6,4},{1,3},{3,1},{5,7},{7,5}} | collective-permute-start | bytes 6291464 | tf_op jit(solution)/shard_map/ppermute | solution.py:358
  15.2 129.2 %collective-permute-start.21 = (bf16[1024,1024]{1,0:T(8,128)(2,1)}, bf16[1024,1024]{1,0:T(8,128)(2,1)}, u32[]{:S(2)}, u32[]{:S(2)}) collective-permute-start(bf16[1024,1024]{1,0:T(8,128)(2,1)} %get-tuple-element.217), channel_id=1, source_target_pairs={{0,2},{2,0},{4,6},{6,4},{1,3},{3,1},{5,7},{7,5}} | collective-permute-start | bytes 6291464 | tf_op jit(solution)/shard_map/ppermute | solution.py:358
  21.0 168.3 %collective-permute-start.19 = (bf16[1024,1024]{1,0:T(8,128)(2,1)}, bf16[1024,1024]{1,0:T(8,128)(2,1)}, u32[]{:S(2)}, u32[]{:S(2)}) collective-permute-start(bf16[1024,1024]{1,0:T(8,128)(2,1)} %get-tuple-element.216), channel_id=1, source_target_pairs={{0,2},{2,0},{4,6},{6,4},{1,3},{3,1},{5,7},{7,5}} | collective-permute-start | bytes 6291464 | tf_op jit(solution)/shard_map/ppermute | solution.py:358
  24.7 209.6 %collective-permute-start.34 = (bf16[1024,1024]{1,0:T(8,128)(2,1)}, bf16[1024,1024]{1,0:T(8,128)(2,1)}, u32[]{:S(2)}, u32[]{:S(2)}) collective-permute-start(bf16[1024,1024]{1,0:T(8,128)(2,1)} %get-tuple-element.233), channel_id=1, source_target_pairs={{0,2},{2,0},{4,6},{6,4},{1,3},{3,1},{5,7},{7,5}} | collective-permute-start | bytes 6291464 | tf_op jit(solution)/shard_map/ppermute | solution.py:358
  123.0 171.1 %collective-permute-start.32 = (bf16[1024,1024]{1,0:T(8,128)(2,1)}, bf16[1024,1024]{1,0:T(8,128)(2,1)}, u32[]{:S(2)}, u32[]{:S(2)}) collective-permute-start(bf16[1024,1024]{1,0:T(8,128)(2,1)} %get-tuple-element.232), channel_id=1, source_target_pairs={{0,2},{2,0},{4,6},{6,4},{1,3},{3,1},{5,7},{7,5}} | collective-permute-start | bytes 6291464 | tf_op jit(solution)/shard_map/ppermute | solution.py:358
  123.0 201.1 %collective-permute-start.30 = (bf16[1024,1024]{1,0:T(8,128)(2,1)}, bf16[1024,1024]{1,0:T(8,128)(2,1)}, u32[]{:S(2)}, u32[]{:S(2)}) collective-permute-start(bf16[1024,1024]{1,0:T(8,128)(2,1)} %get-tuple-element.231), channel_id=1, source_target_pairs={{0,2},{2,0},{4,6},{6,4},{1,3},{3,1},{5,7},{7,5}} | collective-permute-start | bytes 6291464 | tf_op jit(solution)/shard_map/ppermute | solution.py:358
  144.4 224.7 %collective-permute-start.28 = (bf16[1024,1024]{1,0:T(8,128)(2,1)}, bf16[1024,1024]{1,0:T(8,128)(2,1)}, u32[]{:S(2)}, u32[]{:S(2)}) collective-permute-start(bf16[1024,1024]{1,0:T(8,128)(2,1)} %get-tuple-element.230), channel_id=1, source_target_pairs={{0,2},{2,0},{4,6},{6,4},{1,3},{3,1},{5,7},{7,5}} | collective-permute-start | bytes 6291464 | tf_op jit(solution)/shard_map/ppermute | solution.py:358
  189.3 224.7 %collective-permute-start.16 = (bf16[256,4096]{1,0:T(8,128)(2,1)}, bf16[256,4096]{1,0:T(8,128)(2,1)}, u32[]{:S(2)}, u32[]{:S(2)}) collective-permute-start(bf16[256,4096]{1,0:T(8,128)(2,1)} %get-tuple-element.199), channel_id=1, source_target_pairs={{0,2},{2,0},{4,6},{6,4},{1,3},{3,1},{5,7},{7,5}} | collective-permute-start | bytes 6291464 | tf_op jit(solution)/shard_map/ppermute | solution.py:358
  234.3 224.7 %collective-permute-start.14 = (bf16[256,4096]{1,0:T(8,128)(2,1)}, bf16[256,4096]{1,0:T(8,128)(2,1)}, u32[]{:S(2)}, u32[]{:S(2)}) collective-permute-start(bf16[256,4096]{1,0:T(8,128)(2,1)} %get-tuple-element.198), channel_id=1, source_target_pairs={{0,2},{2,0},{4,6},{6,4},{1,3},{3,1},{5,7},{7,5}} | collective-permute-start | bytes 6291464 | tf_op jit(solution)/shard_map/ppermute | solution.py:358
  294.1 255.8 %collective-permute-start.12 = (bf16[256,4096]{1,0:T(8,128)(2,1)}, bf16[256,4096]{1,0:T(8,128)(2,1)}, u32[]{:S(2)}, u32[]{:S(2)}) collective-permute-start(bf16[256,4096]{1,0:T(8,128)(2,1)} %get-tuple-element.197), channel_id=1, source_target_pairs={{0,2},{2,0},{4,6},{6,4},{1,3},{3,1},{5,7},{7,5}} | collective-permute-start | bytes 6291464 | tf_op jit(solution)/shard_map/ppermute | solution.py:358
  324.1 225.8 %collective-permute-start.10 = (bf16[256,4096]{1,0:T(8,128)(2,1)}, bf16[256,4096]{1,0:T(8,128)(2,1)}, u32[]{:S(2)}, u32[]{:S(2)}) collective-permute-start(bf16[256,4096]{1,0:T(8,128)(2,1)} %get-tuple-element.196), channel_id=1, source_target_pairs={{0,2},{2,0},{4,6},{6,4},{1,3},{3,1},{5,7},{7,5}} | collective-permute-start | bytes 6291464 | tf_op jit(solution)/shard_map/ppermute | solution.py:358
  369.1 224.7 %collective-permute-start.7 = (bf16[256,4096]{1,0:T(8,128)(2,1)}, bf16[256,4096]{1,0:T(8,128)(2,1)}, u32[]{:S(2)}, u32[]{:S(2)}) collective-permute-start(bf16[256,4096]{1,0:T(8,128)(2,1)} %get-tuple-element.188), channel_id=1, source_target_pairs={{0,2},{2,0},{4,6},{6,4},{1,3},{3,1},{5,7},{7,5}} | collective-permute-start | bytes 6291464 | tf_op jit(solution)/shard_map/ppermute | solution.py:358
  414.0 224.7 %collective-permute-start.5 = (bf16[256,4096]{1,0:T(8,128)(2,1)}, bf16[256,4096]{1,0:T(8,128)(2,1)}, u32[]{:S(2)}, u32[]{:S(2)}) collective-permute-start(bf16[256,4096]{1,0:T(8,128)(2,1)} %get-tuple-element.187), channel_id=1, source_target_pairs={{0,2},{2,0},{4,6},{6,4},{1,3},{3,1},{5,7},{7,5}} | collective-permute-start | bytes 6291464 | tf_op jit(solution)/shard_map/ppermute | solution.py:358
  459.0 224.7 %collective-permute-start.3 = (bf16[256,4096]{1,0:T(8,128)(2,1)}, bf16[256,4096]{1,0:T(8,128)(2,1)}, u32[]{:S(2)}, u32[]{:S(2)}) collective-permute-start(bf16[256,4096]{1,0:T(8,128)(2,1)} %get-tuple-element.186), channel_id=1, source_target_pairs={{0,2},{2,0},{4,6},{6,4},{1,3},{3,1},{5,7},{7,5}} | collective-permute-start | bytes 6291464 | tf_op jit(solution)/shard_map/ppermute | solution.py:358
  549.9 199.2 %collective-permute-start.1 = (bf16[256,4096]{1,0:T(8,128)(2,1)}, bf16[256,4096]{1,0:T(8,128)(2,1)}, u32[]{:S(2)}, u32[]{:S(2)}) collective-permute-start(bf16[256,4096]{1,0:T(8,128)(2,1)} %get-tuple-element.185), channel_id=1, source_target_pairs={{0,2},{2,0},{4,6},{6,4},{1,3},{3,1},{5,7},{7,5}} | collective-permute-start | bytes 6291464 | tf_op jit(solution)/shard_map/ppermute | solution.py:358
  550.0 199.2 %collective-permute-start.26 = (bf16[1024,1024]{1,0:T(8,128)(2,1)}, bf16[1024,1024]{1,0:T(8,128)(2,1)}, u32[]{:S(2)}, u32[]{:S(2)}) collective-permute-start(bf16[1024,1024]{1,0:T(8,128)(2,1)} %collective-permute-done.25.near_ref), channel_id=1, source_target_pairs={{0,4},{2,6},{4,0},{6,2},{1,5},{3,7},{5,1},{7,3}} | collective-permute-start | bytes 6291464 | tf_op jit(solution)/shard_map/ppermute | solution.py:359
  593.8 157.4 %collective-permute-start.24 = (bf16[1024,1024]{1,0:T(8,128)(2,1)}, bf16[1024,1024]{1,0:T(8,128)(2,1)}, u32[]{:S(2)}, u32[]{:S(2)}) collective-permute-start(bf16[1024,1024]{1,0:T(8,128)(2,1)} %collective-permute-done.23.near_ref), channel_id=1, source_target_pairs={{0,4},{2,6},{4,0},{6,2},{1,5},{3,7},{5,1},{7,3}} | collective-permute-start | bytes 6291464 | tf_op jit(solution)/shard_map/ppermute | solution.py:359
  638.7 112.5 %collective-permute-start.22 = (bf16[1024,1024]{1,0:T(8,128)(2,1)}, bf16[1024,1024]{1,0:T(8,128)(2,1)}, u32[]{:S(2)}, u32[]{:S(2)}) collective-permute-start(bf16[1024,1024]{1,0:T(8,128)(2,1)} %collective-permute-done.21.near_ref), channel_id=1, source_target_pairs={{0,4},{2,6},{4,0},{6,2},{1,5},{3,7},{5,1},{7,3}} | collective-permute-start | bytes 6291464 | tf_op jit(solution)/shard_map/ppermute | solution.py:359
  749.1 93.7 %collective-permute-start.33 = (bf16[1024,1024]{1,0:T(8,128)(2,1)}, bf16[1024,1024]{1,0:T(8,128)(2,1)}, u32[]{:S(2)}, u32[]{:S(2)}) collective-permute-start(bf16[1024,1024]{1,0:T(8,128)(2,1)} %collective-permute-done.32.near_ref), channel_id=1, source_target_pairs={{0,4},{2,6},{4,0},{6,2},{1,5},{3,7},{5,1},{7,3}} | collective-permute-start | bytes 6291464 | tf_op jit(solution)/shard_map/ppermute | solution.py:359
  751.1 136.7 %collective-permute-start.31 = (bf16[1024,1024]{1,0:T(8,128)(2,1)}, bf16[1024,1024]{1,0:T(8,128)(2,1)}, u32[]{:S(2)}, u32[]{:S(2)}) collective-permute-start(bf16[1024,1024]{1,0:T(8,128)(2,1)} %collective-permute-done.30.near_ref), channel_id=1, source_target_pairs={{0,4},{2,6},{4,0},{6,2},{1,5},{3,7},{5,1},{7,3}} | collective-permute-start | bytes 6291464 | tf_op jit(solution)/shard_map/ppermute | solution.py:359
  751.2 181.6 %collective-permute-start.29 = (bf16[1024,1024]{1,0:T(8,128)(2,1)}, bf16[1024,1024]{1,0:T(8,128)(2,1)}, u32[]{:S(2)}, u32[]{:S(2)}) collective-permute-start(bf16[1024,1024]{1,0:T(8,128)(2,1)} %collective-permute-done.28.near_ref), channel_id=1, source_target_pairs={{0,4},{2,6},{4,0},{6,2},{1,5},{3,7},{5,1},{7,3}} | collective-permute-start | bytes 6291464 | tf_op jit(solution)/shard_map/ppermute | solution.py:359
  753.2 224.5 %collective-permute-start.17 = (bf16[256,4096]{1,0:T(8,128)(2,1)}, bf16[256,4096]{1,0:T(8,128)(2,1)}, u32[]{:S(2)}, u32[]{:S(2)}) collective-permute-start(bf16[256,4096]{1,0:T(8,128)(2,1)} %collective-permute-done.16.near_ref), channel_id=1, source_target_pairs={{0,4},{2,6},{4,0},{6,2},{1,5},{3,7},{5,1},{7,3}} | collective-permute-start | bytes 6291464 | tf_op jit(solution)/shard_map/ppermute | solution.py:359
  808.2 347.0 %collective-permute-start.18 = (bf16[4096,1024]{1,0:T(8,128)(2,1)}, bf16[4096,1024]{1,0:T(8,128)(2,1)}, u32[]{:S(2)}, u32[]{:S(2)}) collective-permute-start(bf16[4096,1024]{1,0:T(8,128)(2,1)} %get-tuple-element.153.refs_2_.refs_4_), channel_id=1, source_target_pairs={{0,1},{1,0},{2,3},{3,2},{4,5},{5,4},{6,7},{7,6}} | collective-permute-start | bytes 25165832 | tf_op jit(solution)/shard_map/ppermute | solution.py:363
  842.9 312.4 %collective-permute-start.27 = (bf16[4096,1024]{1,0:T(8,128)(2,1)}, bf16[4096,1024]{1,0:T(8,128)(2,1)}, u32[]{:S(2)}, u32[]{:S(2)}) collective-permute-start(bf16[4096,1024]{1,0:T(8,128)(2,1)} %get-tuple-element.162.refs_2_.refs_4_), channel_id=1, source_target_pairs={{0,1},{1,0},{2,3},{3,2},{4,5},{5,4},{6,7},{7,6}} | collective-permute-start | bytes 25165832 | tf_op jit(solution)/shard_map/ppermute | solution.py:363
  887.8 269.4 %collective-permute-start.9 = (bf16[1024,4096]{1,0:T(8,128)(2,1)}, bf16[1024,4096]{1,0:T(8,128)(2,1)}, u32[]{:S(2)}, u32[]{:S(2)}) collective-permute-start(bf16[1024,4096]{1,0:T(8,128)(2,1)} %get-tuple-element.149.refs_1_), channel_id=1, source_target_pairs={{0,1},{1,0},{2,3},{3,2},{4,5},{5,4},{6,7},{7,6}} | collective-permute-start | bytes 25165832 | tf_op jit(solution)/shard_map/ppermute | solution.py:363
  932.8 102.5 %collective-permute-start.15 = (bf16[256,4096]{1,0:T(8,128)(2,1)}, bf16[256,4096]{1,0:T(8,128)(2,1)}, u32[]{:S(2)}, u32[]{:S(2)}) collective-permute-start(bf16[256,4096]{1,0:T(8,128)(2,1)} %collective-permute-done.14.near_ref), channel_id=1, source_target_pairs={{0,4},{2,6},{4,0},{6,2},{1,5},{3,7},{5,1},{7,3}} | collective-permute-start | bytes 6291464 | tf_op jit(solution)/shard_map/ppermute | solution.py:359
  1035.2 296.2 %collective-permute-start = (bf16[1024,4096]{1,0:T(8,128)(2,1)}, bf16[1024,4096]{1,0:T(8,128)(2,1)}, u32[]{:S(2)}, u32[]{:S(2)}) collective-permute-start(bf16[1024,4096]{1,0:T(8,128)(2,1)} %get-tuple-element.158.refs_1_.refs_5_), channel_id=1, source_target_pairs={{0,1},{1,0},{2,3},{3,2},{4,5},{5,4},{6,7},{7,6}} | collective-permute-start | bytes 25165832 | tf_op jit(solution)/shard_map/ppermute | solution.py:363
  1153.3 176.3 %collective-permute-start.8 = (bf16[256,4096]{1,0:T(8,128)(2,1)}, bf16[256,4096]{1,0:T(8,128)(2,1)}, u32[]{:S(2)}, u32[]{:S(2)}) collective-permute-start(bf16[256,4096]{1,0:T(8,128)(2,1)} %collective-permute-done.7.near_ref), channel_id=1, source_target_pairs={{0,4},{2,6},{4,0},{6,2},{1,5},{3,7},{5,1},{7,3}} | collective-permute-start | bytes 6291464 | tf_op jit(solution)/shard_map/ppermute | solution.py:359
  1155.2 185.5 %collective-permute-start.6 = (bf16[256,4096]{1,0:T(8,128)(2,1)}, bf16[256,4096]{1,0:T(8,128)(2,1)}, u32[]{:S(2)}, u32[]{:S(2)}) collective-permute-start(bf16[256,4096]{1,0:T(8,128)(2,1)} %collective-permute-done.5.near_ref), channel_id=1, source_target_pairs={{0,4},{2,6},{4,0},{6,2},{1,5},{3,7},{5,1},{7,3}} | collective-permute-start | bytes 6291464 | tf_op jit(solution)/shard_map/ppermute | solution.py:359
  1155.3 196.4 %collective-permute-start.4 = (bf16[256,4096]{1,0:T(8,128)(2,1)}, bf16[256,4096]{1,0:T(8,128)(2,1)}, u32[]{:S(2)}, u32[]{:S(2)}) collective-permute-start(bf16[256,4096]{1,0:T(8,128)(2,1)} %collective-permute-done.3.near_ref), channel_id=1, source_target_pairs={{0,4},{2,6},{4,0},{6,2},{1,5},{3,7},{5,1},{7,3}} | collective-permute-start | bytes 6291464 | tf_op jit(solution)/shard_map/ppermute | solution.py:359
  1157.2 203.8 %collective-permute-start.2 = (bf16[256,4096]{1,0:T(8,128)(2,1)}, bf16[256,4096]{1,0:T(8,128)(2,1)}, u32[]{:S(2)}, u32[]{:S(2)}) collective-permute-start(bf16[256,4096]{1,0:T(8,128)(2,1)} %collective-permute-done.1.near_ref), channel_id=1, source_target_pairs={{0,4},{2,6},{4,0},{6,2},{1,5},{3,7},{5,1},{7,3}} | collective-permute-start | bytes 6291464 | tf_op jit(solution)/shard_map/ppermute | solution.py:359
  1329.5 97.2 %collective-permute-start.70 = (bf16[1024,1024]{1,0:T(8,128)(2,1)}, bf16[1024,1024]{1,0:T(8,128)(2,1)}, u32[]{:S(2)}, u32[]{:S(2)}) collective-permute-start(bf16[1024,1024]{1,0:T(8,128)(2,1)} %get-tuple-element.289), channel_id=1, source_target_pairs={{0,2},{2,0},{4,6},{6,4},{1,3},{3,1},{5,7},{7,5}} | collective-permute-start | bytes 6291464 | tf_op jit(solution)/shard_map/ppermute | solution.py:358
  1331.4 95.5 %collective-permute-start.68 = (bf16[1024,1024]{1,0:T(8,128)(2,1)}, bf16[1024,1024]{1,0:T(8,128)(2,1)}, u32[]{:S(2)}, u32[]{:S(2)}) collective-permute-start(bf16[1024,1024]{1,0:T(8,128)(2,1)} %get-tuple-element.288), channel_id=1, source_target_pairs={{0,2},{2,0},{4,6},{6,4},{1,3},{3,1},{5,7},{7,5}} | collective-permute-start | bytes 6291464 | tf_op jit(solution)/shard_map/ppermute | solution.py:358
  1340.7 127.5 %collective-permute-start.66 = (bf16[1024,1024]{1,0:T(8,128)(2,1)}, bf16[1024,1024]{1,0:T(8,128)(2,1)}, u32[]{:S(2)}, u32[]{:S(2)}) collective-permute-start(bf16[1024,1024]{1,0:T(8,128)(2,1)} %get-tuple-element.287), channel_id=1, source_target_pairs={{0,2},{2,0},{4,6},{6,4},{1,3},{3,1},{5,7},{7,5}} | collective-permute-start | bytes 6291464 | tf_op jit(solution)/shard_map/ppermute | solution.py:358
  1351.7 161.5 %collective-permute-start.64 = (bf16[1024,1024]{1,0:T(8,128)(2,1)}, bf16[1024,1024]{1,0:T(8,128)(2,1)}, u32[]{:S(2)}, u32[]{:S(2)}) collective-permute-start(bf16[1024,1024]{1,0:T(8,128)(2,1)} %get-tuple-element.286), channel_id=1, source_target_pairs={{0,2},{2,0},{4,6},{6,4},{1,3},{3,1},{5,7},{7,5}} | collective-permute-start | bytes 6291464 | tf_op jit(solution)/shard_map/ppermute | solution.py:358
  1361.0 197.1 %collective-permute-start.61 = (bf16[1024,1024]{1,0:T(8,128)(2,1)}, bf16[1024,1024]{1,0:T(8,128)(2,1)}, u32[]{:S(2)}, u32[]{:S(2)}) collective-permute-start(bf16[1024,1024]{1,0:T(8,128)(2,1)} %get-tuple-element.284), channel_id=1, source_target_pairs={{0,2},{2,0},{4,6},{6,4},{1,3},{3,1},{5,7},{7,5}} | collective-permute-start | bytes 6291464 | tf_op jit(solution)/shard_map/ppermute | solution.py:358
  1426.7 190.7 %collective-permute-start.59 = (bf16[1024,1024]{1,0:T(8,128)(2,1)}, bf16[1024,1024]{1,0:T(8,128)(2,1)}, u32[]{:S(2)}, u32[]{:S(2)}) collective-permute-start(bf16[1024,1024]{1,0:T(8,128)(2,1)} %get-tuple-element.283), channel_id=1, source_target_pairs={{0,2},{2,0},{4,6},{6,4},{1,3},{3,1},{5,7},{7,5}} | collective-permute-start | bytes 6291464 | tf_op jit(solution)/shard_map/ppermute | solution.py:358
  1426.9 221.1 %collective-permute-start.57 = (bf16[1024,1024]{1,0:T(8,128)(2,1)}, bf16[1024,1024]{1,0:T(8,128)(2,1)}, u32[]{:S(2)}, u32[]{:S(2)}) collective-permute-start(bf16[1024,1024]{1,0:T(8,128)(2,1)} %get-tuple-element.282), channel_id=1, source_target_pairs={{0,2},{2,0},{4,6},{6,4},{1,3},{3,1},{5,7},{7,5}} | collective-permute-start | bytes 6291464 | tf_op jit(solution)/shard_map/ppermute | solution.py:358
  1468.3 224.7 %collective-permute-start.55 = (bf16[1024,1024]{1,0:T(8,128)(2,1)}, bf16[1024,1024]{1,0:T(8,128)(2,1)}, u32[]{:S(2)}, u32[]{:S(2)}) collective-permute-start(bf16[1024,1024]{1,0:T(8,128)(2,1)} %get-tuple-element.281), channel_id=1, source_target_pairs={{0,2},{2,0},{4,6},{6,4},{1,3},{3,1},{5,7},{7,5}} | collective-permute-start | bytes 6291464 | tf_op jit(solution)/shard_map/ppermute | solution.py:358
  1513.2 224.7 %collective-permute-start.52 = (bf16[256,4096]{1,0:T(8,128)(2,1)}, bf16[256,4096]{1,0:T(8,128)(2,1)}, u32[]{:S(2)}, u32[]{:S(2)}) collective-permute-start(bf16[256,4096]{1,0:T(8,128)(2,1)} %get-tuple-element.279), channel_id=1, source_target_pairs={{0,2},{2,0},{4,6},{6,4},{1,3},{3,1},{5,7},{7,5}} | collective-permute-start | bytes 6291464 | tf_op jit(solution)/shard_map/ppermute | solution.py:358
  1558.1 224.7 %collective-permute-start.50 = (bf16[256,4096]{1,0:T(8,128)(2,1)}, bf16[256,4096]{1,0:T(8,128)(2,1)}, u32[]{:S(2)}, u32[]{:S(2)}) collective-permute-start(bf16[256,4096]{1,0:T(8,128)(2,1)} %get-tuple-element.278), channel_id=1, source_target_pairs={{0,2},{2,0},{4,6},{6,4},{1,3},{3,1},{5,7},{7,5}} | collective-permute-start | bytes 6291464 | tf_op jit(solution)/shard_map/ppermute | solution.py:358
  1617.4 256.3 %collective-permute-start.48 = (bf16[256,4096]{1,0:T(8,128)(2,1)}, bf16[256,4096]{1,0:T(8,128)(2,1)}, u32[]{:S(2)}, u32[]{:S(2)}) collective-permute-start(bf16[256,4096]{1,0:T(8,128)(2,1)} %get-tuple-element.277), channel_id=1, source_target_pairs={{0,2},{2,0},{4,6},{6,4},{1,3},{3,1},{5,7},{7,5}} | collective-permute-start | bytes 6291464 | tf_op jit(solution)/shard_map/ppermute | solution.py:358
  1648.0 225.9 %collective-permute-start.46 = (bf16[256,4096]{1,0:T(8,128)(2,1)}, bf16[256,4096]{1,0:T(8,128)(2,1)}, u32[]{:S(2)}, u32[]{:S(2)}) collective-permute-start(bf16[256,4096]{1,0:T(8,128)(2,1)} %get-tuple-element.276), channel_id=1, source_target_pairs={{0,2},{2,0},{4,6},{6,4},{1,3},{3,1},{5,7},{7,5}} | collective-permute-start | bytes 6291464 | tf_op jit(solution)/shard_map/ppermute | solution.py:358
  1693.0 224.7 %collective-permute-start.43 = (bf16[256,4096]{1,0:T(8,128)(2,1)}, bf16[256,4096]{1,0:T(8,128)(2,1)}, u32[]{:S(2)}, u32[]{:S(2)}) collective-permute-start(bf16[256,4096]{1,0:T(8,128)(2,1)} %get-tuple-element.268), channel_id=1, source_target_pairs={{0,2},{2,0},{4,6},{6,4},{1,3},{3,1},{5,7},{7,5}} | collective-permute-start | bytes 6291464 | tf_op jit(solution)/shard_map/ppermute | solution.py:358
  1737.9 224.7 %collective-permute-start.41 = (bf16[256,4096]{1,0:T(8,128)(2,1)}, bf16[256,4096]{1,0:T(8,128)(2,1)}, u32[]{:S(2)}, u32[]{:S(2)}) collective-permute-start(bf16[256,4096]{1,0:T(8,128)(2,1)} %get-tuple-element.267), channel_id=1, source_target_pairs={{0,2},{2,0},{4,6},{6,4},{1,3},{3,1},{5,7},{7,5}} | collective-permute-start | bytes 6291464 | tf_op jit(solution)/shard_map/ppermute | solution.py:358
  1782.8 224.7 %collective-permute-start.39 = (bf16[256,4096]{1,0:T(8,128)(2,1)}, bf16[256,4096]{1,0:T(8,128)(2,1)}, u32[]{:S(2)}, u32[]{:S(2)}) collective-permute-start(bf16[256,4096]{1,0:T(8,128)(2,1)} %get-tuple-element.266), channel_id=1, source_target_pairs={{0,2},{2,0},{4,6},{6,4},{1,3},{3,1},{5,7},{7,5}} | collective-permute-start | bytes 6291464 | tf_op jit(solution)/shard_map/ppermute | solution.py:358
  1873.8 199.1 %collective-permute-start.37 = (bf16[256,4096]{1,0:T(8,128)(2,1)}, bf16[256,4096]{1,0:T(8,128)(2,1)}, u32[]{:S(2)}, u32[]{:S(2)}) collective-permute-start(bf16[256,4096]{1,0:T(8,128)(2,1)} %get-tuple-element.265), channel_id=1, source_target_pairs={{0,2},{2,0},{4,6},{6,4},{1,3},{3,1},{5,7},{7,5}} | collective-permute-start | bytes 6291464 | tf_op jit(solution)/shard_map/ppermute | solution.py:358
  1873.9 199.1 %collective-permute-start.71 = (bf16[1024,1024]{1,0:T(8,128)(2,1)}, bf16[1024,1024]{1,0:T(8,128)(2,1)}, u32[]{:S(2)}, u32[]{:S(2)}) collective-permute-start(bf16[1024,1024]{1,0:T(8,128)(2,1)} %collective-permute-done.70.near_ref), channel_id=1, source_target_pairs={{0,4},{2,6},{4,0},{6,2},{1,5},{3,7},{5,1},{7,3}} | collective-permute-start | bytes 6291464 | tf_op jit(solution)/shard_map/ppermute | solution.py:359
  1917.7 157.3 %collective-permute-start.69 = (bf16[1024,1024]{1,0:T(8,128)(2,1)}, bf16[1024,1024]{1,0:T(8,128)(2,1)}, u32[]{:S(2)}, u32[]{:S(2)}) collective-permute-start(bf16[1024,1024]{1,0:T(8,128)(2,1)} %collective-permute-done.68.near_ref), channel_id=1, source_target_pairs={{0,4},{2,6},{4,0},{6,2},{1,5},{3,7},{5,1},{7,3}} | collective-permute-start | bytes 6291464 | tf_op jit(solution)/shard_map/ppermute | solution.py:359
  1962.6 112.4 %collective-permute-start.67 = (bf16[1024,1024]{1,0:T(8,128)(2,1)}, bf16[1024,1024]{1,0:T(8,128)(2,1)}, u32[]{:S(2)}, u32[]{:S(2)}) collective-permute-start(bf16[1024,1024]{1,0:T(8,128)(2,1)} %collective-permute-done.66.near_ref), channel_id=1, source_target_pairs={{0,4},{2,6},{4,0},{6,2},{1,5},{3,7},{5,1},{7,3}} | collective-permute-start | bytes 6291464 | tf_op jit(solution)/shard_map/ppermute | solution.py:359
  2073.0 93.6 %collective-permute-start.60 = (bf16[1024,1024]{1,0:T(8,128)(2,1)}, bf16[1024,1024]{1,0:T(8,128)(2,1)}, u32[]{:S(2)}, u32[]{:S(2)}) collective-permute-start(bf16[1024,1024]{1,0:T(8,128)(2,1)} %collective-permute-done.59.near_ref), channel_id=1, source_target_pairs={{0,4},{2,6},{4,0},{6,2},{1,5},{3,7},{5,1},{7,3}} | collective-permute-start | bytes 6291464 | tf_op jit(solution)/shard_map/ppermute | solution.py:359
  2074.9 136.7 %collective-permute-start.58 = (bf16[1024,1024]{1,0:T(8,128)(2,1)}, bf16[1024,1024]{1,0:T(8,128)(2,1)}, u32[]{:S(2)}, u32[]{:S(2)}) collective-permute-start(bf16[1024,1024]{1,0:T(8,128)(2,1)} %collective-permute-done.57.near_ref), channel_id=1, source_target_pairs={{0,4},{2,6},{4,0},{6,2},{1,5},{3,7},{5,1},{7,3}} | collective-permute-start | bytes 6291464 | tf_op jit(solution)/shard_map/ppermute | solution.py:359
  2075.1 181.5 %collective-permute-start.56 = (bf16[1024,1024]{1,0:T(8,128)(2,1)}, bf16[1024,1024]{1,0:T(8,128)(2,1)}, u32[]{:S(2)}, u32[]{:S(2)}) collective-permute-start(bf16[1024,1024]{1,0:T(8,128)(2,1)} %collective-permute-done.55.near_ref), channel_id=1, source_target_pairs={{0,4},{2,6},{4,0},{6,2},{1,5},{3,7},{5,1},{7,3}} | collective-permute-start | bytes 6291464 | tf_op jit(solution)/shard_map/ppermute | solution.py:359
  2077.0 224.5 %collective-permute-start.53 = (bf16[256,4096]{1,0:T(8,128)(2,1)}, bf16[256,4096]{1,0:T(8,128)(2,1)}, u32[]{:S(2)}, u32[]{:S(2)}) collective-permute-start(bf16[256,4096]{1,0:T(8,128)(2,1)} %collective-permute-done.52.near_ref), channel_id=1, source_target_pairs={{0,4},{2,6},{4,0},{6,2},{1,5},{3,7},{5,1},{7,3}} | collective-permute-start | bytes 6291464 | tf_op jit(solution)/shard_map/ppermute | solution.py:359
  2132.3 344.8 %collective-permute-start.63 = (bf16[4096,1024]{1,0:T(8,128)(2,1)}, bf16[4096,1024]{1,0:T(8,128)(2,1)}, u32[]{:S(2)}, u32[]{:S(2)}) collective-permute-start(bf16[4096,1024]{1,0:T(8,128)(2,1)} %get-tuple-element.226.refs_2_.refs_4_), channel_id=1, source_target_pairs={{0,1},{1,0},{2,3},{3,2},{4,5},{5,4},{6,7},{7,6}} | collective-permute-start | bytes 25165832 | tf_op jit(solution)/shard_map/ppermute | solution.py:363
  2166.6 312.1 %collective-permute-start.54 = (bf16[4096,1024]{1,0:T(8,128)(2,1)}, bf16[4096,1024]{1,0:T(8,128)(2,1)}, u32[]{:S(2)}, u32[]{:S(2)}) collective-permute-start(bf16[4096,1024]{1,0:T(8,128)(2,1)} %get-tuple-element.241.refs_2_.refs_4_), channel_id=1, source_target_pairs={{0,1},{1,0},{2,3},{3,2},{4,5},{5,4},{6,7},{7,6}} | collective-permute-start | bytes 25165832 | tf_op jit(solution)/shard_map/ppermute | solution.py:363
  2211.6 267.5 %collective-permute-start.45 = (bf16[1024,4096]{1,0:T(8,128)(2,1)}, bf16[1024,4096]{1,0:T(8,128)(2,1)}, u32[]{:S(2)}, u32[]{:S(2)}) collective-permute-start(bf16[1024,4096]{1,0:T(8,128)(2,1)} %get-tuple-element.214.refs_1_), channel_id=1, source_target_pairs={{0,1},{1,0},{2,3},{3,2},{4,5},{5,4},{6,7},{7,6}} | collective-permute-start | bytes 25165832 | tf_op jit(solution)/shard_map/ppermute | solution.py:363
  2256.5 102.4 %collective-permute-start.51 = (bf16[256,4096]{1,0:T(8,128)(2,1)}, bf16[256,4096]{1,0:T(8,128)(2,1)}, u32[]{:S(2)}, u32[]{:S(2)}) collective-permute-start(bf16[256,4096]{1,0:T(8,128)(2,1)} %collective-permute-done.50.near_ref), channel_id=1, source_target_pairs={{0,4},{2,6},{4,0},{6,2},{1,5},{3,7},{5,1},{7,3}} | collective-permute-start | bytes 6291464 | tf_op jit(solution)/shard_map/ppermute | solution.py:359
  2359.0 278.0 %collective-permute-start.36 = (bf16[1024,4096]{1,0:T(8,128)(2,1)}, bf16[1024,4096]{1,0:T(8,128)(2,1)}, u32[]{:S(2)}, u32[]{:S(2)}) collective-permute-start(bf16[1024,4096]{1,0:T(8,128)(2,1)} %get-tuple-element.228.refs_1_.refs_5_), channel_id=1, source_target_pairs={{0,1},{1,0},{2,3},{3,2},{4,5},{5,4},{6,7},{7,6}} | collective-permute-start | bytes 25165832 | tf_op jit(solution)/shard_map/ppermute | solution.py:363
  2476.7 160.3 %collective-permute-start.44 = (bf16[256,4096]{1,0:T(8,128)(2,1)}, bf16[256,4096]{1,0:T(8,128)(2,1)}, u32[]{:S(2)}, u32[]{:S(2)}) collective-permute-start(bf16[256,4096]{1,0:T(8,128)(2,1)} %collective-permute-done.43.near_ref), channel_id=1, source_target_pairs={{0,4},{2,6},{4,0},{6,2},{1,5},{3,7},{5,1},{7,3}} | collective-permute-start | bytes 6291464 | tf_op jit(solution)/shard_map/ppermute | solution.py:359
  2477.0 167.7 %collective-permute-start.42 = (bf16[256,4096]{1,0:T(8,128)(2,1)}, bf16[256,4096]{1,0:T(8,128)(2,1)}, u32[]{:S(2)}, u32[]{:S(2)}) collective-permute-start(bf16[256,4096]{1,0:T(8,128)(2,1)} %collective-permute-done.41.near_ref), channel_id=1, source_target_pairs={{0,4},{2,6},{4,0},{6,2},{1,5},{3,7},{5,1},{7,3}} | collective-permute-start | bytes 6291464 | tf_op jit(solution)/shard_map/ppermute | solution.py:359
  2478.8 173.7 %collective-permute-start.40 = (bf16[256,4096]{1,0:T(8,128)(2,1)}, bf16[256,4096]{1,0:T(8,128)(2,1)}, u32[]{:S(2)}, u32[]{:S(2)}) collective-permute-start(bf16[256,4096]{1,0:T(8,128)(2,1)} %collective-permute-done.39.near_ref), channel_id=1, source_target_pairs={{0,4},{2,6},{4,0},{6,2},{1,5},{3,7},{5,1},{7,3}} | collective-permute-start | bytes 6291464 | tf_op jit(solution)/shard_map/ppermute | solution.py:359
  2479.1 181.2 %collective-permute-start.38 = (bf16[256,4096]{1,0:T(8,128)(2,1)}, bf16[256,4096]{1,0:T(8,128)(2,1)}, u32[]{:S(2)}, u32[]{:S(2)}) collective-permute-start(bf16[256,4096]{1,0:T(8,128)(2,1)} %collective-permute-done.37.near_ref), channel_id=1, source_target_pairs={{0,4},{2,6},{4,0},{6,2},{1,5},{3,7},{5,1},{7,3}} | collective-permute-start | bytes 6291464 | tf_op jit(solution)/shard_map/ppermute | solution.py:359
  (8 other events, 608.2 us)

commit v2 on v1

v2 whole, which is shorter than its diff:
```python
import functools

import jax
import jax.numpy as jnp
from jax import lax
from jax.experimental import pallas as pl
from jax.experimental.pallas import tpu as pltpu
from jax.sharding import PartitionSpec as P


LR_SCALE = 0.8
EPS = 1e-6
INV_SQRT2 = 0.7071067811865476
INV_SQRT_2PI = 0.3989422804014327
F32 = jnp.float32
BF16 = jnp.bfloat16
CONTRACT_ROWS = (((0,), (0,)), ((), ()))
CONTRACT_LAST = (((1,), (1,)), ((), ()))
VMEM_LIMIT = 63 * 1024 * 1024
TILE = 512
SLAB = 256
FWD_BLOCK = 512
BWD_BLOCK = 256
HID_TILE = 256
PARTS = 2
CHUNKS = 4
ANY = pl.BlockSpec(memory_space=pl.ANY)


def params_of(axes=1, limit=VMEM_LIMIT):
    return pltpu.CompilerParams(dimension_semantics=("arbitrary",) * axes, vmem_limit_bytes=limit)


def inv_rms_of(rows):
    return lax.rsqrt(jnp.mean(rows * rows, axis=-1, keepdims=True) + EPS)


def slabs(count, body):
    lax.fori_loop(0, count, lambda i, c: (body(pl.ds(pl.multiple_of(i * SLAB, SLAB), SLAB)), c)[1], 0)


def act_kernel(h_ref, w1_ref, act_ref, slope_ref, ut_hbm, u_s, ut_s, sem):
    step = pl.program_id(0)
    rows_total = h_ref.shape[0]
    ut_copy = pltpu.make_async_copy(ut_s, ut_hbm, sem)

    @pl.when(step == 0)
    def _():
        def normalize(rows):
            h = h_ref[rows, :].astype(F32)
            u = h * inv_rms_of(h)
            u_s[rows, :] = u.astype(BF16)
            ut_s[:, rows] = u.T.astype(BF16)

        slabs(rows_total // SLAB, normalize)
        ut_copy.start()

    for i in range(rows_total // TILE):
        rows = pl.ds(i * TILE, TILE)
        z = jnp.dot(u_s[rows, :], w1_ref[...], preferred_element_type=F32)
        half = 0.5 * (1.0 + lax.erf(z * INV_SQRT2))
        act_ref[rows, :] = (z * half).astype(BF16)
        slope_ref[rows, :] = half + z * jnp.exp(-0.5 * z * z) * INV_SQRT_2PI

    @pl.when(step == pl.num_programs(0) - 1)
    def _():
        ut_copy.wait()


def activate(h, t, w1):
    depth, ff = w1.shape
    rows = h.shape[-2]
    block = FWD_BLOCK
    once = pl.Buffered(1)
    if t is None:
        h_spec = pl.BlockSpec((rows, depth), lambda j: (0, 0), pipeline_mode=once)
    else:
        h_spec = pl.BlockSpec((None, None, None, rows, depth), lambda j: (0, 0, t, 0, 0), pipeline_mode=once)
    return pl.pallas_call(
        act_kernel,
        grid=(ff // block,),
        in_specs=[h_spec, pl.BlockSpec((depth, block), lambda j: (0, j))],
        out_specs=[pl.BlockSpec((rows, block), lambda j: (0, j)), pl.BlockSpec((rows, block), lambda j: (0, j)), ANY],
        out_shape=[jax.ShapeDtypeStruct((rows, ff), BF16), jax.ShapeDtypeStruct((rows, ff), F32),
                   jax.ShapeDtypeStruct((depth, rows), BF16)],
        scratch_shapes=[pltpu.VMEM((rows, depth), BF16), pltpu.VMEM((depth, rows), BF16), pltpu.SemaphoreType.DMA],
        compiler_params=params_of(),
        cost_estimate=pl.CostEstimate(flops=2 * rows * depth * ff, bytes_accessed=rows * ff * 6 + depth * ff * 2,
                                      transcendentals=2 * rows * ff),
    )(h, w1)


def hidden_kernel(last, scale, act_ref, w2_ref, h_ref, *refs):
    add = jnp.dot(act_ref[...], w2_ref[...], preferred_element_type=F32)
    h = (h_ref[...].astype(F32) + add).astype(BF16)
    if last:
        tgt_ref, hout_ref, g_ref = refs
        g_ref[...] = ((h.astype(F32) - tgt_ref[...].astype(F32)) * scale).astype(BF16)
    else:
        hout_ref, = refs
    hout_ref[...] = h


def hidden(act, w2, h, t, target, target_t, scale):
    ff, depth = w2.shape
    rows = act.shape[0]
    tile = HID_TILE
    plain = pl.BlockSpec((tile, depth), lambda i: (i, 0))
    of_step = lambda t: pl.BlockSpec((None, None, None, tile, depth), lambda i: (0, 0, t, i, 0))
    last = target is not None
    n_out = 2 if last else 1
    return pl.pallas_call(
        functools.partial(hidden_kernel, last, scale),
        grid=(rows // tile,),
        in_specs=[pl.BlockSpec((tile, ff), lambda i: (i, 0)),
                  pl.BlockSpec((ff, depth), lambda i: (0, 0), pipeline_mode=pl.Buffered(1)),
                  plain if t is None else of_step(t)] + ([of_step(target_t)] if last else []),
        out_specs=[plain] * n_out,
        out_shape=[jax.ShapeDtypeStruct((rows, depth), BF16)] * n_out,
        compiler_params=params_of(),
        cost_estimate=pl.CostEstimate(flops=2 * rows * depth * ff, bytes_accessed=rows * ff * 2 + depth * ff * 2,
                                      transcendentals=0),
    )(act, w2, h, *([target] if last else []))


def bwd_kernel(deep, second, part, scale, rate, t, n_prev, *refs):
    refs = list(refs)

    def take(count):
        taken = refs[:count]
        del refs[:count]
        return taken

    g_ref, ut_ref, act_ref, slope_ref, w2_ref = take(5)
    closing = deep and part == PARTS - 1
    if deep:
        w1_ref, = take(1)
    if deep and part:
        acc_in_hbm, = take(1)
    if closing:
        h_hbm, hl_hbm, tgt_hbm = take(3)
    old1_ref, old2_ref = take(2)
    take(n_prev)
    d1_ref, d2_ref = take(2)
    if not second:
        q1_ref, q2_ref = take(2)
    if deep:
        out_hbm, = take(1)
    s_s, = take(1)
    if deep:
        acc, sems = take(2)
    if closing:
        h_s, hl_s, tgt_s, gout_s = take(4)
    step = pl.program_id(0)
    rows_total = g_ref.shape[0]
    if deep:
        @pl.when(step == 0)
        def _():
            if part:
                acc_load = pltpu.make_async_copy(acc_in_hbm, acc, sems.at[0])
                acc_load.start()
                acc_load.wait()
            else:
                def clear(rows):
                    acc[rows, :] = jnp.zeros((SLAB, acc.shape[1]), F32)

                slabs(rows_total // SLAB, clear)
    if closing:
        loads = [pltpu.make_async_copy(src, dst, sems.at[i + 1])
                 for i, (src, dst) in enumerate(((h_hbm, h_s), (hl_hbm, hl_s), (tgt_hbm.at[0, 0, t], tgt_s)))]

        @pl.when(step == 0)
        def _():
            for load in loads:
                load.start()

    for i in range(rows_total // TILE):
        rows = pl.ds(i * TILE, TILE)
        back = lax.dot_general(g_ref[rows, :], w2_ref[...], CONTRACT_LAST, preferred_element_type=F32)
        s_s[rows, :] = (back * slope_ref[rows, :]).astype(BF16)

    d2 = lax.dot_general(act_ref[...], g_ref[...], CONTRACT_ROWS, preferred_element_type=F32)
    d1 = jnp.dot(ut_ref[...], s_s[...], preferred_element_type=F32)
    if second:
        d2_ref[...] = old2_ref[...] + d2
        d1_ref[...] = old1_ref[...] + d1
    else:
        d2_ref[...] = d2
        d1_ref[...] = d1
        q2_ref[...] = (old2_ref[...] - rate * d2).astype(BF16)
        q1_ref[...] = (old1_ref[...] - rate * d1).astype(BF16)
    if deep:
        for i in range(rows_total // TILE):
            rows = pl.ds(i * TILE, TILE)
            acc[rows, :] += lax.dot_general(s_s[rows, :], w1_ref[...], CONTRACT_LAST, preferred_element_type=F32)

        @pl.when(step == pl.num_programs(0) - 1)
        def _():
            out_copy = pltpu.make_async_copy(gout_s if closing else acc, out_hbm, sems.at[0])
            if closing:
                for load in loads:
                    load.wait()

                def finish(rows):
                    h = h_s[rows, :].astype(F32)
                    grad = acc[rows, :]
                    inv_rms = inv_rms_of(h)
                    row_dot = jnp.mean(h * grad, axis=-1, keepdims=True)
                    e = (hl_s[rows, :].astype(F32) - tgt_s[rows, :].astype(F32)) * scale
                    e = e + (inv_rms * grad - h * (inv_rms * inv_rms * inv_rms) * row_dot)
                    gout_s[rows, :] = e.astype(BF16)

                slabs(rows_total // SLAB, finish)
            out_copy.start()
            out_copy.wait()


def backward(part, g, ut, act, slope, w1, w2, old1, old2, prev, second, rate, layer, deep, scale, t):
    rows, ff = act.shape
    depth = g.shape[1]
    is_deep = deep is not None
    closing = is_deep and part == PARTS - 1
    block = BWD_BLOCK
    steps = ff // block // PARTS
    first = part * steps
    in_cols = pl.BlockSpec((depth, block), lambda j: (0, first + j))
    out_rows = pl.BlockSpec((block, depth), lambda j: (first + j, 0))
    wide = pl.BlockSpec((rows, block), lambda j: (0, first + j))
    if second:
        old_specs = [in_cols, out_rows]
    else:
        old_specs = [pl.BlockSpec((None, None, None, depth, block), lambda j: (0, 0, layer, 0, first + j)),
                     pl.BlockSpec((None, None, None, block, depth), lambda j: (0, 0, layer, first + j, 0))]
    once = pl.Buffered(1)
    args = [g, ut, act, slope, w2]
    in_specs = [pl.BlockSpec((rows, depth), lambda j: (0, 0), pipeline_mode=once),
                pl.BlockSpec((depth, rows), lambda j: (0, 0), pipeline_mode=once), wide, wide, out_rows]
    n_grads = 2 if second else 4
    if is_deep:
        args.append(w1)
        in_specs.append(in_cols)
    if is_deep and part:
        args.append(prev[-1])
        in_specs.append(ANY)
    if closing:
        args += list(deep)
        in_specs += [ANY] * 3
    args += [old1, old2]
    in_specs += old_specs
    aliases, n_prev = {}, 0
    if part:
        n_prev = n_grads
        for i in range(n_grads):
            aliases[len(args)] = i
            args.append(prev[i])
            in_specs.append(ANY)
    out_shape = [jax.ShapeDtypeStruct((depth, ff), F32), jax.ShapeDtypeStruct((ff, depth), F32)]
    out_specs = [in_cols, out_rows]
    if not second:
        out_shape += [jax.ShapeDtypeStruct((depth, ff), BF16), jax.ShapeDtypeStruct((ff, depth), BF16)]
        out_specs += [in_cols, out_rows]
    scratch = [pltpu.VMEM((rows, block), BF16)]
    if is_deep:
        out_shape.append(jax.ShapeDtypeStruct((rows, depth), BF16 if closing else F32))
        out_specs.append(ANY)
        scratch += [pltpu.VMEM((rows, depth), F32), pltpu.SemaphoreType.DMA((4,))]
    if closing:
        scratch += [pltpu.VMEM((rows, depth), BF16)] * 4
    return pl.pallas_call(
        functools.partial(bwd_kernel, is_deep, second, part, scale, rate, t, n_prev),
        grid=(steps,),
        in_specs=in_specs, out_specs=out_specs, out_shape=out_shape, scratch_shapes=scratch,
        input_output_aliases=aliases,
        compiler_params=params_of(),
        cost_estimate=pl.CostEstimate(flops=(8 if is_deep else 6) * rows * depth * ff // PARTS,
                                      bytes_accessed=(rows * ff * 6 + depth * ff * 24) // PARTS, transcendentals=0),
    )(*args)


def chunk_specs(shape, layer, part, steps):
    rows, cols = shape
    band = rows // CHUNKS // steps
    first = part * steps
    return (pl.BlockSpec((None, None, None, band, cols), lambda j: (0, 0, layer, first + j, 0)),
            pl.BlockSpec((band, cols), lambda j: (first + j, 0)),
            pl.BlockSpec((band, cols), lambda j: (j, 0)))


def cast_kernel(has_prev, p_ref, *refs):
    whole_ref, wire_ref = refs[1:] if has_prev else refs
    value = p_ref[...].astype(BF16)
    whole_ref[...] = value
    wire_ref[...] = value


def cast_chunk(p, layer, part, prev):
    shape = p.shape[-2:]
    steps = 2
    param_spec, layer_spec, wire_spec = chunk_specs(shape, layer, part, steps)
    return pl.pallas_call(
        functools.partial(cast_kernel, prev is not None),
        grid=(steps,),
        in_specs=[param_spec] + ([ANY] if prev is not None else []),
        out_specs=[layer_spec, wire_spec],
        out_shape=[jax.ShapeDtypeStruct(shape, BF16), jax.ShapeDtypeStruct((shape[0] // CHUNKS, shape[1]), BF16)],
        input_output_aliases={1: 0} if prev is not None else {},
        compiler_params=params_of(),
        cost_estimate=pl.CostEstimate(flops=10 ** 9, bytes_accessed=8 * shape[0] * shape[1] // CHUNKS, transcendentals=0),
    )(*([p] + ([prev] if prev is not None else [])))


def mix_kernel(rate, n_prev, final, par_ref, p_ref, grad_ref, col_ref, near_ref, far_ref, *refs):
    refs = refs[n_prev:]
    near = near_ref[...].astype(F32)
    far = far_ref[...].astype(F32)
    even = par_ref[0] == 0
    col = col_ref[...].astype(F32)
    mix = p_ref[...] + col + col
    mix = mix + jnp.where(even, far, near)
    mix = mix + jnp.where(even, near, far)
    new = mix / 5.0 - rate * grad_ref[...]
    refs[0][...] = new
    if not final:
        value = new.astype(BF16)
        refs[1][...] = value
        refs[2][...] = value


def mix_chunk(par, p, grad, col, near, far, layer, part, rate, prev_param, prev_layer, final):
    shape = p.shape[-2:]
    steps = 8
    param_spec, layer_spec, wire_spec = chunk_specs(shape, layer, part, steps)
    args = [par, p, grad, col, near, far]
    in_specs = [pl.BlockSpec(memory_space=pltpu.SMEM), param_spec, layer_spec, layer_spec, wire_spec, wire_spec]
    aliases = {}
    out_shape = [jax.ShapeDtypeStruct(p.shape, F32)]
    out_specs = [param_spec]
    if not final:
        out_shape += [jax.ShapeDtypeStruct(shape, BF16), jax.ShapeDtypeStruct((shape[0] // CHUNKS, shape[1]), BF16)]
        out_specs += [layer_spec, wire_spec]
    n_prev = 0
    for prev, out_idx in ((prev_param, 0), (None if final else prev_layer, 1)):
        if prev is not None:
            aliases[len(args)] = out_idx
            args.append(prev)
            in_specs.append(ANY)
            n_prev += 1
    return pl.pallas_call(
        functools.partial(mix_kernel, rate, n_prev, final),
        grid=(steps,),
        in_specs=in_specs, out_specs=out_specs, out_shape=out_shape,
        input_output_aliases=aliases,
        compiler_params=params_of(),
        cost_estimate=pl.CostEstimate(flops=10 ** 9, bytes_accessed=20 * shape[0] * shape[1] // CHUNKS, transcendentals=0),
    )(*args)


def solution(mesh):
    row_size = mesh.shape["row"]
    col_size = mesh.shape["col"]
    layers, windows = 2, 2
    near_pairs = [(i, i ^ 1) for i in range(row_size)]
    far_pairs = [(i, i ^ 2) for i in range(row_size)]
    col_pairs = [(i, (i + 1) % col_size) for i in range(col_size)]
    total = 2 * layers * CHUNKS

    def locate(i):
        return i // (2 * CHUNKS), (i // CHUNKS) % 2, i % CHUNKS

    def device_program(w_in, w_out, inputs, targets):
        batch, depth = inputs.shape[-2:]
        scale = 2.0 / (batch * depth)
        rate = LR_SCALE / layers
        par = (lax.axis_index("row") % 2).astype(jnp.int32).reshape(1)

        def send(i, wire, weights):
            near = lax.ppermute(wire, "row", near_pairs)
            far = lax.ppermute(near, "row", far_pairs)
            cols = None
            if i % CHUNKS == CHUNKS - 1:
                layer, kind, _ = locate(i)
                cols = lax.ppermute(weights[layer][kind], "col", col_pairs)
            return near, far, cols

        def fwd(layer, h, weights, t):
            w1, w2 = weights[layer]
            at = t if layer == 0 else None
            act, slope, ut = activate(h, at, w1)
            outs = hidden(act, w2, h, at, targets if layer == layers - 1 else None, t, scale)
            return (act, slope, ut, *outs)

        def run_forward(weights, t):
            outs, h = [], inputs
            for layer in range(layers):
                outs.append(fwd(layer, h, weights, t))
                h = outs[-1][3]
            return outs

        def grads(step, outs, weights, t, olds):
            g = outs[-1][4]
            found = [None] * layers
            for layer in reversed(range(layers)):
                act, slope, ut = outs[layer][:3]
                deep = (outs[layer - 1][3], outs[layer][3], targets) if layer else None
                res = None
                for part in range(PARTS):
                    res = backward(part, g, ut, act, slope,
                                 *weights[layer], *olds[layer], res, step == 1, rate, layer, deep, scale, t)
                if layer:
                    g = res[-1]
                found[layer] = res
            return found

        params = [w_in, w_out]
        weights = [[None, None] for _ in range(layers)]
        moved = []
        for i in range(total):
            layer, kind, part = locate(i)
            weights[layer][kind], wire = cast_chunk(params[kind], layer, part, weights[layer][kind])
            moved.append(send(i, wire, weights))
        head = run_forward(weights, 0)
        for window in range(windows):
            final = window == windows - 1
            step_a = 2 * window
            first = grads(0, head, weights, step_a, [params] * layers)
            moved_on = [r[2:4] for r in first]
            middle = run_forward(moved_on, step_a + 1)
            second = grads(1, middle, moved_on, step_a + 1, [r[:2] for r in first])
            new_params = [None, None]
            new_weights = [[None, None] for _ in range(layers)]
            new_moved, head = [], []
            for i in range(total):
                layer, kind, part = locate(i)
                near, far, _ = moved[i]
                cols = moved[i - i % CHUNKS + CHUNKS - 1][2]
                res = mix_chunk(par, params[kind], second[layer][kind], cols, near, far,
                             layer, part, rate, new_params[kind], new_weights[layer][kind], final)
                new_params[kind] = res[0]
                if not final:
                    new_weights[layer][kind] = res[1]
                    new_moved.append(send(i, res[2], new_weights))
                    if i % (2 * CHUNKS) == 2 * CHUNKS - 1:
                        h = inputs if layer == 0 else head[-1][3]
                        head.append(fwd(layer, h, new_weights, step_a + 2))
            params, weights, moved = new_params, new_weights, new_moved
        return params[0], params[1]

    block_spec = P("row", "col")
    return jax.shard_map(device_program, mesh=mesh, in_specs=(block_spec,) * 4, out_specs=(block_spec,) * 2, check_vma=False)
```

time: 2680 us -> 2650 us (0.989)
  waiting for transfers between devices: 1200 us -> 1010 us
  Pallas kernels: 1390 us -> 1570 us
    ppermute x32, waiting for transfers between devices: 805 us -> 670 us  [send(): near = lax.ppermute(wire, 'row', near_pairs)]
    pallas_call x16 -> x32, Pallas kernels: 1060 us -> 1190 us  [the longest x16 695 us: backward(): pl.pallas_call(functools.partial(bwd_kernel, is_deep, second, part, scale...]
    ppermute x32, waiting for transfers between devices: 396 us -> 336 us  [send(): far = lax.ppermute(near, 'row', far_pairs)]
    pallas_call x32, Pallas kernels: 270 us -> 321 us  [mix_chunk(): pl.pallas_call(functools.partial(mix_kernel, rate, n_prev, final), grid=(...]
  transfers between devices with their start and end apart: 72 -> 72, of which waited for: 30 -> 31; matrix products, arithmetic and copies ran while one was open for 0% -> 0% of each run, Pallas kernels for 52% -> 59%
where the time goes in v2:
time: 2650 us; the launch traced here: 2630 us
  Pallas kernels  1570 us (59%)
  waiting for transfers between devices  1010 us (38%)
  starting transfers between devices  59.4 us (2%)
    pallas_call x16, Pallas kernels, backward(): pl.pallas_call(functools.partial(bwd_kernel, is_deep, second, part, scale...  695 us
    ppermute x32, waiting for transfers between devices, send(): near = lax.ppermute(wire, 'row', near_pairs)  670 us
    ppermute x32, waiting for transfers between devices, send(): far = lax.ppermute(near, 'row', far_pairs)  336 us
    pallas_call x32, Pallas kernels, mix_chunk(): pl.pallas_call(functools.partial(mix_kernel, rate, n_prev, final), grid=(...  321 us
    pallas_call x8, Pallas kernels, activate(): pl.pallas_call(act_kernel, grid=(ff // block,), in_specs=[h_spec, pl.Bloc...  293 us
    pallas_call x8, Pallas kernels, hidden(): pl.pallas_call(functools.partial(hidden_kernel, last, scale), grid=(rows...  200 us
    pallas_call x16, Pallas kernels, cast_chunk(): pl.pallas_call(functools.partial(cast_kernel, prev is not None), grid=(st...  59.7 us
  transfers between devices with their start and end apart: 72, of which 31 were waited for; matrix products, arithmetic and copies ran while one was open for 0% of the time, Pallas kernels for 59%

profile of v2, /device:TPU:0, one launch (start us, length us, event | category | flops | bytes accessed | tf_op | source)
XLA Modules:
  0.0 2635.0 jit_solution(8980097048136792766)
XLA Ops:
  67.7 36.5 %shard_map.63 = (bf16[2048,4096]{1,0:T(8,128)(2,1)}, f32[2048,4096]{1,0:T(8,128)}, bf16[1024,2048]{1,0:T(8,128)(2,1)}) custom-call(bf16[1,1,4,2048,1024]{4,3,2,1,0:T(8,128)(2,1)} %h_ref.15, bf16[1024,4096]{1,0:T(8,128)(2,1)} %get-tuple-element.173.w1_ref), custom_call_target="tpu_custom_call" | custom-call | flops 17179869184 | bytes 58720256 | tf_op jit(solution)/shard_map/pallas_call | solution.py:79
  104.3 23.8 shard_map.68.h_ref.refs_7_
  128.1 36.5 %shard_map.73 = (bf16[2048,4096]{1,0:T(8,128)(2,1)}, f32[2048,4096]{1,0:T(8,128)}, bf16[1024,2048]{1,0:T(8,128)(2,1)}) custom-call(bf16[2048,1024]{1,0:T(8,128)(2,1)} %shard_map.68.h_ref.refs_7_, bf16[1024,4096]{1,0:T(8,128)(2,1)} %get-tuple-element.182.w1_ref.refs_5_), custom_call_target="tpu_custom_call" | custom-call | flops 17179869184 | bytes 58720256 | tf_op jit(solution)/shard_map/pallas_call | solution.py:79
  164.6 25.6 shard_map.78
  190.3 48.6 %shard_map.79 = (f32[1024,4096]{1,0:T(8,128)}, f32[4096,1024]{1,0:T(8,128)}, bf16[1024,4096]{1,0:T(8,128)(2,1)}, bf16[4096,1024]{1,0:T(8,128)(2,1)}, f32[2048,1024]{1,0:T(8,128)}) custom-call(bf16[2048,1024]{1,0:T(8,128)(2,1)} %get-tuple-element.188.refs_0_, bf16[1024,2048]{1,0:T(8,128)(2,1)} %get-tuple-element.189.refs_1_, ...), custom_call_target="tpu_custom_call" | custom-call | flops 34359738368 | bytes 75497472 | tf_op jit(solution)/shard_map/pallas_call | solution.py:269
  238.9 54.7 %shard_map.80 = (f32[1024,4096]{1,0:T(8,128)}, f32[4096,1024]{1,0:T(8,128)}, bf16[1024,4096]{1,0:T(8,128)(2,1)}, bf16[4096,1024]{1,0:T(8,128)(2,1)}, bf16[2048,1024]{1,0:T(8,128)(2,1)}) custom-call(bf16[2048,1024]{1,0:T(8,128)(2,1)} %get-tuple-element.188.refs_0_, ...), custom_call_target="tpu_custom_call", output_to_operand_aliasing={{0}: (12, {}), {1}: (13, {}), {2}: (14, {}), {3}: (15, {})} | custom-call | flops 34359738368 | bytes 75497472 | tf_op jit(solution)/shard_map/pallas_call | solution.py:269
  293.7 35.5 %shard_map.81 = (f32[1024,4096]{1,0:T(8,128)}, f32[4096,1024]{1,0:T(8,128)}, bf16[1024,4096]{1,0:T(8,128)(2,1)}, bf16[4096,1024]{1,0:T(8,128)(2,1)}) custom-call(bf16[2048,1024]{1,0:T(8,128)(2,1)} %get-tuple-element.197.refs_0_, bf16[1024,2048]{1,0:T(8,128)(2,1)} %get-tuple-element.198.refs_1_, bf16[2048,4096]{1,0:T(8,128)(2,1)} %get-tuple-element.174.act_ref.refs_2_, ...), custom_call_target="tpu_custom_call" | custom-call | flops 25769803776 | bytes 75497472 | tf_op jit(solution)/shard_map/pallas_call | solution.py:269
  331.3 35.3 %shard_map.82 = (f32[1024,4096]{1,0:T(8,128)}, f32[4096,1024]{1,0:T(8,128)}, bf16[1024,4096]{1,0:T(8,128)(2,1)}, bf16[4096,1024]{1,0:T(8,128)(2,1)}) custom-call(bf16[2048,1024]{1,0:T(8,128)(2,1)} %get-tuple-element.197.refs_0_, ...), custom_call_target="tpu_custom_call", output_to_operand_aliasing={{0}: (7, {}), {1}: (8, {}), {2}: (9, {}), {3}: (10, {})} | custom-call | flops 25769803776 | bytes 75497472 | tf_op jit(solution)/shard_map/pallas_call | solution.py:269
  378.1 44.9 %collective-permute-done.30.near_ref = bf16[1024,1024]{1,0:T(8,128)(2,1)} collective-permute-done((bf16[1024,1024]{1,0:T(8,128)(2,1)}, bf16[1024,1024]{1,0:T(8,128)(2,1)}, u32[]{:S(2)}, u32[]{:S(2)}) %collective-permute-start.30) | collective-permute-done | bytes 2097184 | tf_op jit(solution)/shard_map/ppermute | solution.py:377
  423.0 36.5 %shard_map.83 = (bf16[2048,4096]{1,0:T(8,128)(2,1)}, f32[2048,4096]{1,0:T(8,128)}, bf16[1024,2048]{1,0:T(8,128)(2,1)}) custom-call(bf16[1,1,4,2048,1024]{4,3,2,1,0:T(8,128)(2,1)} %h_ref.15, bf16[1024,4096]{1,0:T(8,128)(2,1)} %get-tuple-element.204.w1_ref), custom_call_target="tpu_custom_call" | custom-call | flops 17179869184 | bytes 58720256 | tf_op jit(solution)/shard_map/pallas_call | solution.py:79
  459.5 24.5 shard_map.84.h_ref.refs_7_
  486.0 26.9 %collective-permute-done.16.near_ref = bf16[256,4096]{1,0:T(8,128)(2,1)} collective-permute-done((bf16[256,4096]{1,0:T(8,128)(2,1)}, bf16[256,4096]{1,0:T(8,128)(2,1)}, u32[]{:S(2)}, u32[]{:S(2)}) %collective-permute-start.16) | collective-permute-done | bytes 2097184 | tf_op jit(solution)/shard_map/ppermute | solution.py:377
  512.9 44.9 %collective-permute-done.14.near_ref = bf16[256,4096]{1,0:T(8,128)(2,1)} collective-permute-done((bf16[256,4096]{1,0:T(8,128)(2,1)}, bf16[256,4096]{1,0:T(8,128)(2,1)}, u32[]{:S(2)}, u32[]{:S(2)}) %collective-permute-start.14) | collective-permute-done | bytes 2097184 | tf_op jit(solution)/shard_map/ppermute | solution.py:377
  557.8 44.9 %collective-permute-done.12.near_ref = bf16[256,4096]{1,0:T(8,128)(2,1)} collective-permute-done((bf16[256,4096]{1,0:T(8,128)(2,1)}, bf16[256,4096]{1,0:T(8,128)(2,1)}, u32[]{:S(2)}, u32[]{:S(2)}) %collective-permute-start.12) | collective-permute-done | bytes 2097184 | tf_op jit(solution)/shard_map/ppermute | solution.py:377
  602.8 44.9 %collective-permute-done.10.near_ref = bf16[256,4096]{1,0:T(8,128)(2,1)} collective-permute-done((bf16[256,4096]{1,0:T(8,128)(2,1)}, bf16[256,4096]{1,0:T(8,128)(2,1)}, u32[]{:S(2)}, u32[]{:S(2)}) %collective-permute-start.10) | collective-permute-done | bytes 2097184 | tf_op jit(solution)/shard_map/ppermute | solution.py:377
  649.2 36.9 %shard_map.85 = (bf16[2048,4096]{1,0:T(8,128)(2,1)}, f32[2048,4096]{1,0:T(8,128)}, bf16[1024,2048]{1,0:T(8,128)(2,1)}) custom-call(bf16[2048,1024]{1,0:T(8,128)(2,1)} %shard_map.84.h_ref.refs_7_, bf16[1024,4096]{1,0:T(8,128)(2,1)} %get-tuple-element.207.w1_ref.refs_5_), custom_call_target="tpu_custom_call" | custom-call | flops 17179869184 | bytes 58720256 | tf_op jit(solution)/shard_map/pallas_call | solution.py:79
  686.1 25.5 shard_map.86
  711.6 26.0 collective-permute-done.5.near_ref
  739.1 43.4 %collective-permute-done.3.near_ref = bf16[256,4096]{1,0:T(8,128)(2,1)} collective-permute-done((bf16[256,4096]{1,0:T(8,128)(2,1)}, bf16[256,4096]{1,0:T(8,128)(2,1)}, u32[]{:S(2)}, u32[]{:S(2)}) %collective-permute-start.3) | collective-permute-done | bytes 2097184 | tf_op jit(solution)/shard_map/ppermute | solution.py:377
  784.0 40.9 %collective-permute-done.1.near_ref = bf16[256,4096]{1,0:T(8,128)(2,1)} collective-permute-done((bf16[256,4096]{1,0:T(8,128)(2,1)}, bf16[256,4096]{1,0:T(8,128)(2,1)}, u32[]{:S(2)}, u32[]{:S(2)}) %collective-permute-start.1) | collective-permute-done | bytes 2097184 | tf_op jit(solution)/shard_map/ppermute | solution.py:377
  827.0 48.3 %shard_map.87 = (f32[1024,4096]{1,0:T(8,128)}, f32[4096,1024]{1,0:T(8,128)}, f32[2048,1024]{1,0:T(8,128)}) custom-call(bf16[2048,1024]{1,0:T(8,128)(2,1)} %get-tuple-element.210.refs_0_, bf16[1024,2048]{1,0:T(8,128)(2,1)} %get-tuple-element.211.refs_1_, bf16[2048,4096]{1,0:T(8,128)(2,1)} %get-tuple-element.208.act_ref.refs_2_, ...), custom_call_target="tpu_custom_call" | custom-call | flops 34359738368 | bytes 75497472 | tf_op jit(solution)/shard_map/pallas_call | solution.py:269
  877.3 41.4 %collective-permute-done.35.far_ref = bf16[1024,1024]{1,0:T(8,128)(2,1)} collective-permute-done((bf16[1024,1024]{1,0:T(8,128)(2,1)}, bf16[1024,1024]{1,0:T(8,128)(2,1)}, u32[]{:S(2)}, u32[]{:S(2)}) %collective-permute-start.35) | collective-permute-done | bytes 2097184 | tf_op jit(solution)/shard_map/ppermute | solution.py:378
  920.2 54.4 %shard_map.88 = (f32[1024,4096]{1,0:T(8,128)}, f32[4096,1024]{1,0:T(8,128)}, bf16[2048,1024]{1,0:T(8,128)(2,1)}) custom-call(bf16[2048,1024]{1,0:T(8,128)(2,1)} %get-tuple-element.210.refs_0_, bf16[1024,2048]{1,0:T(8,128)(2,1)} %get-tuple-element.211.refs_1_, ...), custom_call_target="tpu_custom_call", output_to_operand_aliasing={{0}: (12, {}), {1}: (13, {})} | custom-call | flops 34359738368 | bytes 75497472 | tf_op jit(solution)/shard_map/pallas_call | solution.py:269
  974.7 30.9 %collective-permute-done.15.far_ref = bf16[256,4096]{1,0:T(8,128)(2,1)} collective-permute-done((bf16[256,4096]{1,0:T(8,128)(2,1)}, bf16[256,4096]{1,0:T(8,128)(2,1)}, u32[]{:S(2)}, u32[]{:S(2)}) %collective-permute-start.15) | collective-permute-done | bytes 2097184 | tf_op jit(solution)/shard_map/ppermute | solution.py:378
  1007.0 35.0 %shard_map.89 = (f32[1024,4096]{1,0:T(8,128)}, f32[4096,1024]{1,0:T(8,128)}) custom-call(bf16[2048,1024]{1,0:T(8,128)(2,1)} %get-tuple-element.224.refs_0_, bf16[1024,2048]{1,0:T(8,128)(2,1)} %get-tuple-element.225.refs_1_, bf16[2048,4096]{1,0:T(8,128)(2,1)} %get-tuple-element.205.act_ref.refs_2_, f32[2048,4096]{1,0:T(8,128)} %get-tuple-element.226.refs_3_, ...), custom_call_target="tpu_custom_call" | custom-call | flops 25769803776 | bytes 75497472 | tf_op jit(solution)/shard_map/pallas_call | solution.py:269
  1052.8 35.1 %shard_map.90 = (f32[1024,4096]{1,0:T(8,128)}, f32[4096,1024]{1,0:T(8,128)}) custom-call(bf16[2048,1024]{1,0:T(8,128)(2,1)} %get-tuple-element.224.refs_0_, bf16[1024,2048]{1,0:T(8,128)(2,1)} %get-tuple-element.225.refs_1_, bf16[2048,4096]{1,0:T(8,128)(2,1)} %get-tuple-element.205.act_ref.refs_2_, ...), custom_call_target="tpu_custom_call", output_to_operand_aliasing={{0}: (7, {}), {1}: (8, {})} | custom-call | flops 25769803776 | bytes 75497472 | tf_op jit(solution)/shard_map/pallas_call | solution.py:269
  1088.4 10.8 shard_map.91
  1101.6 10.8 shard_map.92
  1112.4 10.8 shard_map.93
  1134.5 36.8 %shard_map.99 = (bf16[2048,4096]{1,0:T(8,128)(2,1)}, f32[2048,4096]{1,0:T(8,128)}, bf16[1024,2048]{1,0:T(8,128)(2,1)}) custom-call(bf16[1,1,4,2048,1024]{4,3,2,1,0:T(8,128)(2,1)} %h_ref.15, bf16[1024,4096]{1,0:T(8,128)(2,1)} %get-tuple-element.250.w1_ref), custom_call_target="tpu_custom_call" | custom-call | flops 17179869184 | bytes 58720256 | tf_op jit(solution)/shard_map/pallas_call | solution.py:79
  1171.3 10.7 shard_map.100
  1228.4 24.5 shard_map.104.h_ref.refs_7_
  1275.0 10.8 shard_map.95
  1298.4 26.5 %collective-permute-done.4.far_ref = bf16[256,4096]{1,0:T(8,128)(2,1)} collective-permute-done((bf16[256,4096]{1,0:T(8,128)(2,1)}, bf16[256,4096]{1,0:T(8,128)(2,1)}, u32[]{:S(2)}, u32[]{:S(2)}) %collective-permute-start.4) | collective-permute-done | bytes 2097184 | tf_op jit(solution)/shard_map/ppermute | solution.py:378
  1325.2 10.8 shard_map.97
  1335.9 33.9 %collective-permute-done.2.far_ref = bf16[256,4096]{1,0:T(8,128)(2,1)} collective-permute-done((bf16[256,4096]{1,0:T(8,128)(2,1)}, bf16[256,4096]{1,0:T(8,128)(2,1)}, u32[]{:S(2)}, u32[]{:S(2)}) %collective-permute-start.2) | collective-permute-done | bytes 2097184 | tf_op jit(solution)/shard_map/ppermute | solution.py:378
  1380.8 36.5 %shard_map.105 = (bf16[2048,4096]{1,0:T(8,128)(2,1)}, f32[2048,4096]{1,0:T(8,128)}, bf16[1024,2048]{1,0:T(8,128)(2,1)}) custom-call(bf16[2048,1024]{1,0:T(8,128)(2,1)} %shard_map.104.h_ref.refs_7_, bf16[1024,4096]{1,0:T(8,128)(2,1)} %get-tuple-element.264.w1_ref.refs_5_), custom_call_target="tpu_custom_call" | custom-call | flops 17179869184 | bytes 58720256 | tf_op jit(solution)/shard_map/pallas_call | solution.py:79
  1419.1 10.7 shard_map.109
  1429.8 25.9 shard_map.110
  1455.7 48.7 %shard_map.111 = (f32[1024,4096]{1,0:T(8,128)}, f32[4096,1024]{1,0:T(8,128)}, bf16[1024,4096]{1,0:T(8,128)(2,1)}, bf16[4096,1024]{1,0:T(8,128)(2,1)}, f32[2048,1024]{1,0:T(8,128)}) custom-call(bf16[2048,1024]{1,0:T(8,128)(2,1)} %get-tuple-element.279.refs_0_, bf16[1024,2048]{1,0:T(8,128)(2,1)} %get-tuple-element.280.refs_1_, ...), custom_call_target="tpu_custom_call" | custom-call | flops 34359738368 | bytes 75497472 | tf_op jit(solution)/shard_map/pallas_call | solution.py:269
  1504.4 55.0 %shard_map.112 = (f32[1024,4096]{1,0:T(8,128)}, f32[4096,1024]{1,0:T(8,128)}, bf16[1024,4096]{1,0:T(8,128)(2,1)}, bf16[4096,1024]{1,0:T(8,128)(2,1)}, bf16[2048,1024]{1,0:T(8,128)(2,1)}) custom-call(bf16[2048,1024]{1,0:T(8,128)(2,1)} %get-tuple-element.279.refs_0_, ...), custom_call_target="tpu_custom_call", output_to_operand_aliasing={{0}: (12, {}), {1}: (13, {}), {2}: (14, {}), {3}: (15, {})} | custom-call | flops 34359738368 | bytes 75497472 | tf_op jit(solution)/shard_map/pallas_call | solution.py:269
  1563.5 35.5 %shard_map.113 = (f32[1024,4096]{1,0:T(8,128)}, f32[4096,1024]{1,0:T(8,128)}, bf16[1024,4096]{1,0:T(8,128)(2,1)}, bf16[4096,1024]{1,0:T(8,128)(2,1)}) custom-call(bf16[2048,1024]{1,0:T(8,128)(2,1)} %get-tuple-element.289.refs_0_, bf16[1024,2048]{1,0:T(8,128)(2,1)} %get-tuple-element.290.refs_1_, bf16[2048,4096]{1,0:T(8,128)(2,1)} %get-tuple-element.251.act_ref.refs_2_, ...), custom_call_target="tpu_custom_call" | custom-call | flops 25769803776 | bytes 75497472 | tf_op jit(solution)/shard_map/pallas_call | solution.py:269
  1608.6 44.6 %collective-permute-done.57.near_ref = bf16[1024,1024]{1,0:T(8,128)(2,1)} collective-permute-done((bf16[1024,1024]{1,0:T(8,128)(2,1)}, bf16[1024,1024]{1,0:T(8,128)(2,1)}, u32[]{:S(2)}, u32[]{:S(2)}) %collective-permute-start.57) | collective-permute-done | bytes 2097184 | tf_op jit(solution)/shard_map/ppermute | solution.py:377
  1653.5 44.6 %collective-permute-done.55.near_ref = bf16[1024,1024]{1,0:T(8,128)(2,1)} collective-permute-done((bf16[1024,1024]{1,0:T(8,128)(2,1)}, bf16[1024,1024]{1,0:T(8,128)(2,1)}, u32[]{:S(2)}, u32[]{:S(2)}) %collective-permute-start.55) | collective-permute-done | bytes 2097184 | tf_op jit(solution)/shard_map/ppermute | solution.py:377
  1698.5 44.6 %collective-permute-done.52.near_ref = bf16[256,4096]{1,0:T(8,128)(2,1)} collective-permute-done((bf16[256,4096]{1,0:T(8,128)(2,1)}, bf16[256,4096]{1,0:T(8,128)(2,1)}, u32[]{:S(2)}, u32[]{:S(2)}) %collective-permute-start.52) | collective-permute-done | bytes 2097184 | tf_op jit(solution)/shard_map/ppermute | solution.py:377
  1743.4 35.5 %shard_map.114 = (f32[1024,4096]{1,0:T(8,128)}, f32[4096,1024]{1,0:T(8,128)}, bf16[1024,4096]{1,0:T(8,128)(2,1)}, bf16[4096,1024]{1,0:T(8,128)(2,1)}) custom-call(bf16[2048,1024]{1,0:T(8,128)(2,1)} %get-tuple-element.289.refs_0_, ...), custom_call_target="tpu_custom_call", output_to_operand_aliasing={{0}: (7, {}), {1}: (8, {}), {2}: (9, {}), {3}: (10, {})} | custom-call | flops 25769803776 | bytes 75497472 | tf_op jit(solution)/shard_map/pallas_call | solution.py:269
  1788.3 44.6 %collective-permute-done.48.near_ref = bf16[256,4096]{1,0:T(8,128)(2,1)} collective-permute-done((bf16[256,4096]{1,0:T(8,128)(2,1)}, bf16[256,4096]{1,0:T(8,128)(2,1)}, u32[]{:S(2)}, u32[]{:S(2)}) %collective-permute-start.48) | collective-permute-done | bytes 2097184 | tf_op jit(solution)/shard_map/ppermute | solution.py:377
  1833.3 44.6 %collective-permute-done.46.near_ref = bf16[256,4096]{1,0:T(8,128)(2,1)} collective-permute-done((bf16[256,4096]{1,0:T(8,128)(2,1)}, bf16[256,4096]{1,0:T(8,128)(2,1)}, u32[]{:S(2)}, u32[]{:S(2)}) %collective-permute-start.46) | collective-permute-done | bytes 2097184 | tf_op jit(solution)/shard_map/ppermute | solution.py:377
  1879.4 43.5 %collective-permute-done.43.near_ref = bf16[256,4096]{1,0:T(8,128)(2,1)} collective-permute-done((bf16[256,4096]{1,0:T(8,128)(2,1)}, bf16[256,4096]{1,0:T(8,128)(2,1)}, u32[]{:S(2)}, u32[]{:S(2)}) %collective-permute-start.43) | collective-permute-done | bytes 2097184 | tf_op jit(solution)/shard_map/ppermute | solution.py:377
  1924.3 43.5 %collective-permute-done.41.near_ref = bf16[256,4096]{1,0:T(8,128)(2,1)} collective-permute-done((bf16[256,4096]{1,0:T(8,128)(2,1)}, bf16[256,4096]{1,0:T(8,128)(2,1)}, u32[]{:S(2)}, u32[]{:S(2)}) %collective-permute-start.41) | collective-permute-done | bytes 2097184 | tf_op jit(solution)/shard_map/ppermute | solution.py:377
  1969.3 36.5 %shard_map.115 = (bf16[2048,4096]{1,0:T(8,128)(2,1)}, f32[2048,4096]{1,0:T(8,128)}, bf16[1024,2048]{1,0:T(8,128)(2,1)}) custom-call(bf16[1,1,4,2048,1024]{4,3,2,1,0:T(8,128)(2,1)} %h_ref.15, bf16[1024,4096]{1,0:T(8,128)(2,1)} %get-tuple-element.296.w1_ref), custom_call_target="tpu_custom_call" | custom-call | flops 17179869184 | bytes 58720256 | tf_op jit(solution)/shard_map/pallas_call | solution.py:79
  2005.7 24.5 shard_map.116.h_ref.refs_7_
  2030.8 15.3 collective-permute-done.37.near_ref
  2050.1 36.7 %shard_map.117 = (bf16[2048,4096]{1,0:T(8,128)(2,1)}, f32[2048,4096]{1,0:T(8,128)}, bf16[1024,2048]{1,0:T(8,128)(2,1)}) custom-call(bf16[2048,1024]{1,0:T(8,128)(2,1)} %shard_map.116.h_ref.refs_7_, bf16[1024,4096]{1,0:T(8,128)(2,1)} %get-tuple-element.299.w1_ref.refs_5_), custom_call_target="tpu_custom_call" | custom-call | flops 17179869184 | bytes 58720256 | tf_op jit(solution)/shard_map/pallas_call | solution.py:79
  2086.8 25.5 shard_map.118
  2120.6 44.9 %collective-permute-done.60.far_ref = bf16[1024,1024]{1,0:T(8,128)(2,1)} collective-permute-done((bf16[1024,1024]{1,0:T(8,128)(2,1)}, bf16[1024,1024]{1,0:T(8,128)(2,1)}, u32[]{:S(2)}, u32[]{:S(2)}) %collective-permute-start.60) | collective-permute-done | bytes 2097184 | tf_op jit(solution)/shard_map/ppermute | solution.py:378
  2165.5 44.9 %collective-permute-done.58.far_ref = bf16[1024,1024]{1,0:T(8,128)(2,1)} collective-permute-done((bf16[1024,1024]{1,0:T(8,128)(2,1)}, bf16[1024,1024]{1,0:T(8,128)(2,1)}, u32[]{:S(2)}, u32[]{:S(2)}) %collective-permute-start.58) | collective-permute-done | bytes 2097184 | tf_op jit(solution)/shard_map/ppermute | solution.py:378
  2210.5 44.9 %collective-permute-done.56.far_ref = bf16[1024,1024]{1,0:T(8,128)(2,1)} collective-permute-done((bf16[1024,1024]{1,0:T(8,128)(2,1)}, bf16[1024,1024]{1,0:T(8,128)(2,1)}, u32[]{:S(2)}, u32[]{:S(2)}) %collective-permute-start.56) | collective-permute-done | bytes 2097184 | tf_op jit(solution)/shard_map/ppermute | solution.py:378
  2255.4 48.2 %shard_map.119 = (f32[1024,4096]{1,0:T(8,128)}, f32[4096,1024]{1,0:T(8,128)}, f32[2048,1024]{1,0:T(8,128)}) custom-call(bf16[2048,1024]{1,0:T(8,128)(2,1)} %get-tuple-element.302.refs_0_, bf16[1024,2048]{1,0:T(8,128)(2,1)} %get-tuple-element.303.refs_1_, bf16[2048,4096]{1,0:T(8,128)(2,1)} %get-tuple-element.300.act_ref.refs_2_, ...), custom_call_target="tpu_custom_call" | custom-call | flops 34359738368 | bytes 75497472 | tf_op jit(solution)/shard_map/pallas_call | solution.py:269
  2303.7 38.6 %collective-permute-done.51.far_ref = bf16[256,4096]{1,0:T(8,128)(2,1)} collective-permute-done((bf16[256,4096]{1,0:T(8,128)(2,1)}, bf16[256,4096]{1,0:T(8,128)(2,1)}, u32[]{:S(2)}, u32[]{:S(2)}) %collective-permute-start.51) | collective-permute-done | bytes 2097184 | tf_op jit(solution)/shard_map/ppermute | solution.py:378
  2342.3 54.5 %shard_map.120 = (f32[1024,4096]{1,0:T(8,128)}, f32[4096,1024]{1,0:T(8,128)}, bf16[2048,1024]{1,0:T(8,128)(2,1)}) custom-call(bf16[2048,1024]{1,0:T(8,128)(2,1)} %get-tuple-element.302.refs_0_, bf16[1024,2048]{1,0:T(8,128)(2,1)} %get-tuple-element.303.refs_1_, ...), custom_call_target="tpu_custom_call", output_to_operand_aliasing={{0}: (12, {}), {1}: (13, {})} | custom-call | flops 34359738368 | bytes 75497472 | tf_op jit(solution)/shard_map/pallas_call | solution.py:269
  2398.8 35.1 %shard_map.121 = (f32[1024,4096]{1,0:T(8,128)}, f32[4096,1024]{1,0:T(8,128)}) custom-call(bf16[2048,1024]{1,0:T(8,128)(2,1)} %get-tuple-element.316.refs_0_, bf16[1024,2048]{1,0:T(8,128)(2,1)} %get-tuple-element.317.refs_1_, bf16[2048,4096]{1,0:T(8,128)(2,1)} %get-tuple-element.297.act_ref.refs_2_, f32[2048,4096]{1,0:T(8,128)} %get-tuple-element.318.refs_3_, ...), custom_call_target="tpu_custom_call" | custom-call | flops 25769803776 | bytes 75497472 | tf_op jit(solution)/shard_map/pallas_call | solution.py:269
  2433.9 11.2 collective-permute-done.47.far_ref
  2449.7 35.2 %shard_map.122 = (f32[1024,4096]{1,0:T(8,128)}, f32[4096,1024]{1,0:T(8,128)}) custom-call(bf16[2048,1024]{1,0:T(8,128)(2,1)} %get-tuple-element.316.refs_0_, bf16[1024,2048]{1,0:T(8,128)(2,1)} %get-tuple-element.317.refs_1_, bf16[2048,4096]{1,0:T(8,128)(2,1)} %get-tuple-element.297.act_ref.refs_2_, ...), custom_call_target="tpu_custom_call", output_to_operand_aliasing={{0}: (7, {}), {1}: (8, {})} | custom-call | flops 25769803776 | bytes 75497472 | tf_op jit(solution)/shard_map/pallas_call | solution.py:269
  (160 shorter events, 411.2 us)
Async XLA Ops:
  4.4 324.8 %collective-permute-start.25 = (bf16[1024,1024]{1,0:T(8,128)(2,1)}, bf16[1024,1024]{1,0:T(8,128)(2,1)}, u32[]{:S(2)}, u32[]{:S(2)}) collective-permute-start(bf16[1024,1024]{1,0:T(8,128)(2,1)} %get-tuple-element.256), channel_id=1, source_target_pairs={{0,2},{2,0},{4,6},{6,4},{1,3},{3,1},{5,7},{7,5}} | collective-permute-start | bytes 6291464 | tf_op jit(solution)/shard_map/ppermute | solution.py:377
  11.4 317.8 %collective-permute-start.23 = (bf16[1024,1024]{1,0:T(8,128)(2,1)}, bf16[1024,1024]{1,0:T(8,128)(2,1)}, u32[]{:S(2)}, u32[]{:S(2)}) collective-permute-start(bf16[1024,1024]{1,0:T(8,128)(2,1)} %get-tuple-element.255), channel_id=1, source_target_pairs={{0,2},{2,0},{4,6},{6,4},{1,3},{3,1},{5,7},{7,5}} | collective-permute-start | bytes 6291464 | tf_op jit(solution)/shard_map/ppermute | solution.py:377
  15.2 351.4 %collective-permute-start.21 = (bf16[1024,1024]{1,0:T(8,128)(2,1)}, bf16[1024,1024]{1,0:T(8,128)(2,1)}, u32[]{:S(2)}, u32[]{:S(2)}) collective-permute-start(bf16[1024,1024]{1,0:T(8,128)(2,1)} %get-tuple-element.254), channel_id=1, source_target_pairs={{0,2},{2,0},{4,6},{6,4},{1,3},{3,1},{5,7},{7,5}} | collective-permute-start | bytes 6291464 | tf_op jit(solution)/shard_map/ppermute | solution.py:377
  20.9 345.7 %collective-permute-start.19 = (bf16[1024,1024]{1,0:T(8,128)(2,1)}, bf16[1024,1024]{1,0:T(8,128)(2,1)}, u32[]{:S(2)}, u32[]{:S(2)}) collective-permute-start(bf16[1024,1024]{1,0:T(8,128)(2,1)} %get-tuple-element.253), channel_id=1, source_target_pairs={{0,2},{2,0},{4,6},{6,4},{1,3},{3,1},{5,7},{7,5}} | collective-permute-start | bytes 6291464 | tf_op jit(solution)/shard_map/ppermute | solution.py:377
  24.6 344.0 %collective-permute-start.34 = (bf16[1024,1024]{1,0:T(8,128)(2,1)}, bf16[1024,1024]{1,0:T(8,128)(2,1)}, u32[]{:S(2)}, u32[]{:S(2)}) collective-permute-start(bf16[1024,1024]{1,0:T(8,128)(2,1)} %get-tuple-element.270), channel_id=1, source_target_pairs={{0,2},{2,0},{4,6},{6,4},{1,3},{3,1},{5,7},{7,5}} | collective-permute-start | bytes 6291464 | tf_op jit(solution)/shard_map/ppermute | solution.py:377
  329.3 93.7 %collective-permute-start.30 = (bf16[1024,1024]{1,0:T(8,128)(2,1)}, bf16[1024,1024]{1,0:T(8,128)(2,1)}, u32[]{:S(2)}, u32[]{:S(2)}) collective-permute-start(bf16[1024,1024]{1,0:T(8,128)(2,1)} %get-tuple-element.268), channel_id=1, source_target_pairs={{0,2},{2,0},{4,6},{6,4},{1,3},{3,1},{5,7},{7,5}} | collective-permute-start | bytes 6291464 | tf_op jit(solution)/shard_map/ppermute | solution.py:377
  366.6 117.4 %collective-permute-start.28 = (bf16[1024,1024]{1,0:T(8,128)(2,1)}, bf16[1024,1024]{1,0:T(8,128)(2,1)}, u32[]{:S(2)}, u32[]{:S(2)}) collective-permute-start(bf16[1024,1024]{1,0:T(8,128)(2,1)} %get-tuple-element.267), channel_id=1, source_target_pairs={{0,2},{2,0},{4,6},{6,4},{1,3},{3,1},{5,7},{7,5}} | collective-permute-start | bytes 6291464 | tf_op jit(solution)/shard_map/ppermute | solution.py:377
  366.6 146.2 %collective-permute-start.16 = (bf16[256,4096]{1,0:T(8,128)(2,1)}, bf16[256,4096]{1,0:T(8,128)(2,1)}, u32[]{:S(2)}, u32[]{:S(2)}) collective-permute-start(bf16[256,4096]{1,0:T(8,128)(2,1)} %get-tuple-element.235), channel_id=1, source_target_pairs={{0,2},{2,0},{4,6},{6,4},{1,3},{3,1},{5,7},{7,5}} | collective-permute-start | bytes 6291464 | tf_op jit(solution)/shard_map/ppermute | solution.py:377
  368.6 189.2 %collective-permute-start.14 = (bf16[256,4096]{1,0:T(8,128)(2,1)}, bf16[256,4096]{1,0:T(8,128)(2,1)}, u32[]{:S(2)}, u32[]{:S(2)}) collective-permute-start(bf16[256,4096]{1,0:T(8,128)(2,1)} %get-tuple-element.234), channel_id=1, source_target_pairs={{0,2},{2,0},{4,6},{6,4},{1,3},{3,1},{5,7},{7,5}} | collective-permute-start | bytes 6291464 | tf_op jit(solution)/shard_map/ppermute | solution.py:377
  378.0 224.7 %collective-permute-start.12 = (bf16[256,4096]{1,0:T(8,128)(2,1)}, bf16[256,4096]{1,0:T(8,128)(2,1)}, u32[]{:S(2)}, u32[]{:S(2)}) collective-permute-start(bf16[256,4096]{1,0:T(8,128)(2,1)} %get-tuple-element.233), channel_id=1, source_target_pairs={{0,2},{2,0},{4,6},{6,4},{1,3},{3,1},{5,7},{7,5}} | collective-permute-start | bytes 6291464 | tf_op jit(solution)/shard_map/ppermute | solution.py:377
  423.0 224.7 %collective-permute-start.10 = (bf16[256,4096]{1,0:T(8,128)(2,1)}, bf16[256,4096]{1,0:T(8,128)(2,1)}, u32[]{:S(2)}, u32[]{:S(2)}) collective-permute-start(bf16[256,4096]{1,0:T(8,128)(2,1)} %get-tuple-element.232), channel_id=1, source_target_pairs={{0,2},{2,0},{4,6},{6,4},{1,3},{3,1},{5,7},{7,5}} | collective-permute-start | bytes 6291464 | tf_op jit(solution)/shard_map/ppermute | solution.py:377
  484.0 227.6 %collective-permute-start.7 = (bf16[256,4096]{1,0:T(8,128)(2,1)}, bf16[256,4096]{1,0:T(8,128)(2,1)}, u32[]{:S(2)}, u32[]{:S(2)}) collective-permute-start(bf16[256,4096]{1,0:T(8,128)(2,1)} %get-tuple-element.223), channel_id=1, source_target_pairs={{0,2},{2,0},{4,6},{6,4},{1,3},{3,1},{5,7},{7,5}} | collective-permute-start | bytes 6291464 | tf_op jit(solution)/shard_map/ppermute | solution.py:377
  512.9 224.7 %collective-permute-start.5 = (bf16[256,4096]{1,0:T(8,128)(2,1)}, bf16[256,4096]{1,0:T(8,128)(2,1)}, u32[]{:S(2)}, u32[]{:S(2)}) collective-permute-start(bf16[256,4096]{1,0:T(8,128)(2,1)} %get-tuple-element.222), channel_id=1, source_target_pairs={{0,2},{2,0},{4,6},{6,4},{1,3},{3,1},{5,7},{7,5}} | collective-permute-start | bytes 6291464 | tf_op jit(solution)/shard_map/ppermute | solution.py:377
  557.8 224.7 %collective-permute-start.3 = (bf16[256,4096]{1,0:T(8,128)(2,1)}, bf16[256,4096]{1,0:T(8,128)(2,1)}, u32[]{:S(2)}, u32[]{:S(2)}) collective-permute-start(bf16[256,4096]{1,0:T(8,128)(2,1)} %get-tuple-element.221), channel_id=1, source_target_pairs={{0,2},{2,0},{4,6},{6,4},{1,3},{3,1},{5,7},{7,5}} | collective-permute-start | bytes 6291464 | tf_op jit(solution)/shard_map/ppermute | solution.py:377
  602.8 222.2 %collective-permute-start.1 = (bf16[256,4096]{1,0:T(8,128)(2,1)}, bf16[256,4096]{1,0:T(8,128)(2,1)}, u32[]{:S(2)}, u32[]{:S(2)}) collective-permute-start(bf16[256,4096]{1,0:T(8,128)(2,1)} %get-tuple-element.220), channel_id=1, source_target_pairs={{0,2},{2,0},{4,6},{6,4},{1,3},{3,1},{5,7},{7,5}} | collective-permute-start | bytes 6291464 | tf_op jit(solution)/shard_map/ppermute | solution.py:377
  647.7 178.7 %collective-permute-start.26 = (bf16[1024,1024]{1,0:T(8,128)(2,1)}, bf16[1024,1024]{1,0:T(8,128)(2,1)}, u32[]{:S(2)}, u32[]{:S(2)}) collective-permute-start(bf16[1024,1024]{1,0:T(8,128)(2,1)} %collective-permute-done.25.near_ref), channel_id=1, source_target_pairs={{0,4},{2,6},{4,0},{6,2},{1,5},{3,7},{5,1},{7,3}} | collective-permute-start | bytes 6291464 | tf_op jit(solution)/shard_map/ppermute | solution.py:378
  711.6 376.3 %collective-permute-start.9 = (bf16[1024,4096]{1,0:T(8,128)(2,1)}, bf16[1024,4096]{1,0:T(8,128)(2,1)}, u32[]{:S(2)}, u32[]{:S(2)}) collective-permute-start(bf16[1024,4096]{1,0:T(8,128)(2,1)} %get-tuple-element.173.w1_ref), channel_id=1, source_target_pairs={{0,1},{1,0},{2,3},{3,2},{4,5},{5,4},{6,7},{7,6}} | collective-permute-start | bytes 25165832 | tf_op jit(solution)/shard_map/ppermute | solution.py:382
  737.6 137.7 %collective-permute-start.24 = (bf16[1024,1024]{1,0:T(8,128)(2,1)}, bf16[1024,1024]{1,0:T(8,128)(2,1)}, u32[]{:S(2)}, u32[]{:S(2)}) collective-permute-start(bf16[1024,1024]{1,0:T(8,128)(2,1)} %collective-permute-done.23.near_ref), channel_id=1, source_target_pairs={{0,4},{2,6},{4,0},{6,2},{1,5},{3,7},{5,1},{7,3}} | collective-permute-start | bytes 6291464 | tf_op jit(solution)/shard_map/ppermute | solution.py:378
  782.5 92.8 %collective-permute-start.22 = (bf16[1024,1024]{1,0:T(8,128)(2,1)}, bf16[1024,1024]{1,0:T(8,128)(2,1)}, u32[]{:S(2)}, u32[]{:S(2)}) collective-permute-start(bf16[1024,1024]{1,0:T(8,128)(2,1)} %collective-permute-done.21.near_ref), channel_id=1, source_target_pairs={{0,4},{2,6},{4,0},{6,2},{1,5},{3,7},{5,1},{7,3}} | collective-permute-start | bytes 6291464 | tf_op jit(solution)/shard_map/ppermute | solution.py:378
  826.4 92.3 %collective-permute-start.35 = (bf16[1024,1024]{1,0:T(8,128)(2,1)}, bf16[1024,1024]{1,0:T(8,128)(2,1)}, u32[]{:S(2)}, u32[]{:S(2)}) collective-permute-start(bf16[1024,1024]{1,0:T(8,128)(2,1)} %collective-permute-done.34.near_ref), channel_id=1, source_target_pairs={{0,4},{2,6},{4,0},{6,2},{1,5},{3,7},{5,1},{7,3}} | collective-permute-start | bytes 6291464 | tf_op jit(solution)/shard_map/ppermute | solution.py:378
  875.3 258.6 %collective-permute-start.18 = (bf16[4096,1024]{1,0:T(8,128)(2,1)}, bf16[4096,1024]{1,0:T(8,128)(2,1)}, u32[]{:S(2)}, u32[]{:S(2)}) collective-permute-start(bf16[4096,1024]{1,0:T(8,128)(2,1)} %get-tuple-element.178.w2_ref.refs_4_), channel_id=1, source_target_pairs={{0,1},{1,0},{2,3},{3,2},{4,5},{5,4},{6,7},{7,6}} | collective-permute-start | bytes 25165832 | tf_op jit(solution)/shard_map/ppermute | solution.py:382
  875.3 340.9 %collective-permute-start.27 = (bf16[4096,1024]{1,0:T(8,128)(2,1)}, bf16[4096,1024]{1,0:T(8,128)(2,1)}, u32[]{:S(2)}, u32[]{:S(2)}) collective-permute-start(bf16[4096,1024]{1,0:T(8,128)(2,1)} %get-tuple-element.187.w2_ref.refs_4_), channel_id=1, source_target_pairs={{0,1},{1,0},{2,3},{3,2},{4,5},{5,4},{6,7},{7,6}} | collective-permute-start | bytes 25165832 | tf_op jit(solution)/shard_map/ppermute | solution.py:382
  875.8 98.8 %collective-permute-start.17 = (bf16[256,4096]{1,0:T(8,128)(2,1)}, bf16[256,4096]{1,0:T(8,128)(2,1)}, u32[]{:S(2)}, u32[]{:S(2)}) collective-permute-start(bf16[256,4096]{1,0:T(8,128)(2,1)} %collective-permute-done.16.near_ref), channel_id=1, source_target_pairs={{0,4},{2,6},{4,0},{6,2},{1,5},{3,7},{5,1},{7,3}} | collective-permute-start | bytes 6291464 | tf_op jit(solution)/shard_map/ppermute | solution.py:378
  918.7 86.9 %collective-permute-start.15 = (bf16[256,4096]{1,0:T(8,128)(2,1)}, bf16[256,4096]{1,0:T(8,128)(2,1)}, u32[]{:S(2)}, u32[]{:S(2)}) collective-permute-start(bf16[256,4096]{1,0:T(8,128)(2,1)} %collective-permute-done.14.near_ref), channel_id=1, source_target_pairs={{0,4},{2,6},{4,0},{6,2},{1,5},{3,7},{5,1},{7,3}} | collective-permute-start | bytes 6291464 | tf_op jit(solution)/shard_map/ppermute | solution.py:378
  974.6 300.2 %collective-permute-start = (bf16[1024,4096]{1,0:T(8,128)(2,1)}, bf16[1024,4096]{1,0:T(8,128)(2,1)}, u32[]{:S(2)}, u32[]{:S(2)}) collective-permute-start(bf16[1024,4096]{1,0:T(8,128)(2,1)} %get-tuple-element.182.w1_ref.refs_5_), channel_id=1, source_target_pairs={{0,1},{1,0},{2,3},{3,2},{4,5},{5,4},{6,7},{7,6}} | collective-permute-start | bytes 25165832 | tf_op jit(solution)/shard_map/ppermute | solution.py:382
  1087.9 104.8 %collective-permute-start.33 = (bf16[1024,1024]{1,0:T(8,128)(2,1)}, bf16[1024,1024]{1,0:T(8,128)(2,1)}, u32[]{:S(2)}, u32[]{:S(2)}) collective-permute-start(bf16[1024,1024]{1,0:T(8,128)(2,1)} %collective-permute-done.32.near_ref), channel_id=1, source_target_pairs={{0,4},{2,6},{4,0},{6,2},{1,5},{3,7},{5,1},{7,3}} | collective-permute-start | bytes 6291464 | tf_op jit(solution)/shard_map/ppermute | solution.py:378
  1100.2 104.7 %collective-permute-start.31 = (bf16[1024,1024]{1,0:T(8,128)(2,1)}, bf16[1024,1024]{1,0:T(8,128)(2,1)}, u32[]{:S(2)}, u32[]{:S(2)}) collective-permute-start(bf16[1024,1024]{1,0:T(8,128)(2,1)} %collective-permute-done.30.near_ref), channel_id=1, source_target_pairs={{0,4},{2,6},{4,0},{6,2},{1,5},{3,7},{5,1},{7,3}} | collective-permute-start | bytes 6291464 | tf_op jit(solution)/shard_map/ppermute | solution.py:378
  1133.9 118.9 %collective-permute-start.8 = (bf16[256,4096]{1,0:T(8,128)(2,1)}, bf16[256,4096]{1,0:T(8,128)(2,1)}, u32[]{:S(2)}, u32[]{:S(2)}) collective-permute-start(bf16[256,4096]{1,0:T(8,128)(2,1)} %collective-permute-done.7.near_ref), channel_id=1, source_target_pairs={{0,4},{2,6},{4,0},{6,2},{1,5},{3,7},{5,1},{7,3}} | collective-permute-start | bytes 6291464 | tf_op jit(solution)/shard_map/ppermute | solution.py:378
  1192.7 93.1 %collective-permute-start.6 = (bf16[256,4096]{1,0:T(8,128)(2,1)}, bf16[256,4096]{1,0:T(8,128)(2,1)}, u32[]{:S(2)}, u32[]{:S(2)}) collective-permute-start(bf16[256,4096]{1,0:T(8,128)(2,1)} %collective-permute-done.5.near_ref), channel_id=1, source_target_pairs={{0,4},{2,6},{4,0},{6,2},{1,5},{3,7},{5,1},{7,3}} | collective-permute-start | bytes 6291464 | tf_op jit(solution)/shard_map/ppermute | solution.py:378
  1204.9 120.0 %collective-permute-start.4 = (bf16[256,4096]{1,0:T(8,128)(2,1)}, bf16[256,4096]{1,0:T(8,128)(2,1)}, u32[]{:S(2)}, u32[]{:S(2)}) collective-permute-start(bf16[256,4096]{1,0:T(8,128)(2,1)} %collective-permute-done.3.near_ref), channel_id=1, source_target_pairs={{0,4},{2,6},{4,0},{6,2},{1,5},{3,7},{5,1},{7,3}} | collective-permute-start | bytes 6291464 | tf_op jit(solution)/shard_map/ppermute | solution.py:378
  1216.2 153.6 %collective-permute-start.2 = (bf16[256,4096]{1,0:T(8,128)(2,1)}, bf16[256,4096]{1,0:T(8,128)(2,1)}, u32[]{:S(2)}, u32[]{:S(2)}) collective-permute-start(bf16[256,4096]{1,0:T(8,128)(2,1)} %collective-permute-done.1.near_ref), channel_id=1, source_target_pairs={{0,4},{2,6},{4,0},{6,2},{1,5},{3,7},{5,1},{7,3}} | collective-permute-start | bytes 6291464 | tf_op jit(solution)/shard_map/ppermute | solution.py:378
  1252.9 164.5 %collective-permute-start.29 = (bf16[1024,1024]{1,0:T(8,128)(2,1)}, bf16[1024,1024]{1,0:T(8,128)(2,1)}, u32[]{:S(2)}, u32[]{:S(2)}) collective-permute-start(bf16[1024,1024]{1,0:T(8,128)(2,1)} %collective-permute-done.28.near_ref), channel_id=1, source_target_pairs={{0,4},{2,6},{4,0},{6,2},{1,5},{3,7},{5,1},{7,3}} | collective-permute-start | bytes 6291464 | tf_op jit(solution)/shard_map/ppermute | solution.py:378
  1274.8 284.6 %collective-permute-start.70 = (bf16[1024,1024]{1,0:T(8,128)(2,1)}, bf16[1024,1024]{1,0:T(8,128)(2,1)}, u32[]{:S(2)}, u32[]{:S(2)}) collective-permute-start(bf16[1024,1024]{1,0:T(8,128)(2,1)} %get-tuple-element.337), channel_id=1, source_target_pairs={{0,2},{2,0},{4,6},{6,4},{1,3},{3,1},{5,7},{7,5}} | collective-permute-start | bytes 6291464 | tf_op jit(solution)/shard_map/ppermute | solution.py:377
  1285.8 273.9 %collective-permute-start.68 = (bf16[1024,1024]{1,0:T(8,128)(2,1)}, bf16[1024,1024]{1,0:T(8,128)(2,1)}, u32[]{:S(2)}, u32[]{:S(2)}) collective-permute-start(bf16[1024,1024]{1,0:T(8,128)(2,1)} %get-tuple-element.336), channel_id=1, source_target_pairs={{0,2},{2,0},{4,6},{6,4},{1,3},{3,1},{5,7},{7,5}} | collective-permute-start | bytes 6291464 | tf_op jit(solution)/shard_map/ppermute | solution.py:377
  1324.9 236.6 %collective-permute-start.66 = (bf16[1024,1024]{1,0:T(8,128)(2,1)}, bf16[1024,1024]{1,0:T(8,128)(2,1)}, u32[]{:S(2)}, u32[]{:S(2)}) collective-permute-start(bf16[1024,1024]{1,0:T(8,128)(2,1)} %get-tuple-element.335), channel_id=1, source_target_pairs={{0,2},{2,0},{4,6},{6,4},{1,3},{3,1},{5,7},{7,5}} | collective-permute-start | bytes 6291464 | tf_op jit(solution)/shard_map/ppermute | solution.py:377
  1369.8 192.0 %collective-permute-start.64 = (bf16[1024,1024]{1,0:T(8,128)(2,1)}, bf16[1024,1024]{1,0:T(8,128)(2,1)}, u32[]{:S(2)}, u32[]{:S(2)}) collective-permute-start(bf16[1024,1024]{1,0:T(8,128)(2,1)} %get-tuple-element.334), channel_id=1, source_target_pairs={{0,2},{2,0},{4,6},{6,4},{1,3},{3,1},{5,7},{7,5}} | collective-permute-start | bytes 6291464 | tf_op jit(solution)/shard_map/ppermute | solution.py:377
  1417.4 181.7 %collective-permute-start.61 = (bf16[1024,1024]{1,0:T(8,128)(2,1)}, bf16[1024,1024]{1,0:T(8,128)(2,1)}, u32[]{:S(2)}, u32[]{:S(2)}) collective-permute-start(bf16[1024,1024]{1,0:T(8,128)(2,1)} %get-tuple-element.332), channel_id=1, source_target_pairs={{0,2},{2,0},{4,6},{6,4},{1,3},{3,1},{5,7},{7,5}} | collective-permute-start | bytes 6291464 | tf_op jit(solution)/shard_map/ppermute | solution.py:377
  1559.8 93.5 %collective-permute-start.57 = (bf16[1024,1024]{1,0:T(8,128)(2,1)}, bf16[1024,1024]{1,0:T(8,128)(2,1)}, u32[]{:S(2)}, u32[]{:S(2)}) collective-permute-start(bf16[1024,1024]{1,0:T(8,128)(2,1)} %get-tuple-element.330), channel_id=1, source_target_pairs={{0,2},{2,0},{4,6},{6,4},{1,3},{3,1},{5,7},{7,5}} | collective-permute-start | bytes 6291464 | tf_op jit(solution)/shard_map/ppermute | solution.py:377
  1561.5 136.7 %collective-permute-start.55 = (bf16[1024,1024]{1,0:T(8,128)(2,1)}, bf16[1024,1024]{1,0:T(8,128)(2,1)}, u32[]{:S(2)}, u32[]{:S(2)}) collective-permute-start(bf16[1024,1024]{1,0:T(8,128)(2,1)} %get-tuple-element.329), channel_id=1, source_target_pairs={{0,2},{2,0},{4,6},{6,4},{1,3},{3,1},{5,7},{7,5}} | collective-permute-start | bytes 6291464 | tf_op jit(solution)/shard_map/ppermute | solution.py:377
  1561.8 181.3 %collective-permute-start.52 = (bf16[256,4096]{1,0:T(8,128)(2,1)}, bf16[256,4096]{1,0:T(8,128)(2,1)}, u32[]{:S(2)}, u32[]{:S(2)}) collective-permute-start(bf16[256,4096]{1,0:T(8,128)(2,1)} %get-tuple-element.327), channel_id=1, source_target_pairs={{0,2},{2,0},{4,6},{6,4},{1,3},{3,1},{5,7},{7,5}} | collective-permute-start | bytes 6291464 | tf_op jit(solution)/shard_map/ppermute | solution.py:377
  1599.0 189.0 %collective-permute-start.50 = (bf16[256,4096]{1,0:T(8,128)(2,1)}, bf16[256,4096]{1,0:T(8,128)(2,1)}, u32[]{:S(2)}, u32[]{:S(2)}) collective-permute-start(bf16[256,4096]{1,0:T(8,128)(2,1)} %get-tuple-element.326), channel_id=1, source_target_pairs={{0,2},{2,0},{4,6},{6,4},{1,3},{3,1},{5,7},{7,5}} | collective-permute-start | bytes 6291464 | tf_op jit(solution)/shard_map/ppermute | solution.py:377
  1608.3 224.7 %collective-permute-start.48 = (bf16[256,4096]{1,0:T(8,128)(2,1)}, bf16[256,4096]{1,0:T(8,128)(2,1)}, u32[]{:S(2)}, u32[]{:S(2)}) collective-permute-start(bf16[256,4096]{1,0:T(8,128)(2,1)} %get-tuple-element.325), channel_id=1, source_target_pairs={{0,2},{2,0},{4,6},{6,4},{1,3},{3,1},{5,7},{7,5}} | collective-permute-start | bytes 6291464 | tf_op jit(solution)/shard_map/ppermute | solution.py:377
  1653.2 224.7 %collective-permute-start.46 = (bf16[256,4096]{1,0:T(8,128)(2,1)}, bf16[256,4096]{1,0:T(8,128)(2,1)}, u32[]{:S(2)}, u32[]{:S(2)}) collective-permute-start(bf16[256,4096]{1,0:T(8,128)(2,1)} %get-tuple-element.324), channel_id=1, source_target_pairs={{0,2},{2,0},{4,6},{6,4},{1,3},{3,1},{5,7},{7,5}} | collective-permute-start | bytes 6291464 | tf_op jit(solution)/shard_map/ppermute | solution.py:377
  1698.2 224.7 %collective-permute-start.43 = (bf16[256,4096]{1,0:T(8,128)(2,1)}, bf16[256,4096]{1,0:T(8,128)(2,1)}, u32[]{:S(2)}, u32[]{:S(2)}) collective-permute-start(bf16[256,4096]{1,0:T(8,128)(2,1)} %get-tuple-element.315), channel_id=1, source_target_pairs={{0,2},{2,0},{4,6},{6,4},{1,3},{3,1},{5,7},{7,5}} | collective-permute-start | bytes 6291464 | tf_op jit(solution)/shard_map/ppermute | solution.py:377
  1743.1 224.7 %collective-permute-start.41 = (bf16[256,4096]{1,0:T(8,128)(2,1)}, bf16[256,4096]{1,0:T(8,128)(2,1)}, u32[]{:S(2)}, u32[]{:S(2)}) collective-permute-start(bf16[256,4096]{1,0:T(8,128)(2,1)} %get-tuple-element.314), channel_id=1, source_target_pairs={{0,2},{2,0},{4,6},{6,4},{1,3},{3,1},{5,7},{7,5}} | collective-permute-start | bytes 6291464 | tf_op jit(solution)/shard_map/ppermute | solution.py:377
  1788.0 242.2 %collective-permute-start.39 = (bf16[256,4096]{1,0:T(8,128)(2,1)}, bf16[256,4096]{1,0:T(8,128)(2,1)}, u32[]{:S(2)}, u32[]{:S(2)}) collective-permute-start(bf16[256,4096]{1,0:T(8,128)(2,1)} %get-tuple-element.313), channel_id=1, source_target_pairs={{0,2},{2,0},{4,6},{6,4},{1,3},{3,1},{5,7},{7,5}} | collective-permute-start | bytes 6291464 | tf_op jit(solution)/shard_map/ppermute | solution.py:377
  1833.0 213.1 %collective-permute-start.37 = (bf16[256,4096]{1,0:T(8,128)(2,1)}, bf16[256,4096]{1,0:T(8,128)(2,1)}, u32[]{:S(2)}, u32[]{:S(2)}) collective-permute-start(bf16[256,4096]{1,0:T(8,128)(2,1)} %get-tuple-element.312), channel_id=1, source_target_pairs={{0,2},{2,0},{4,6},{6,4},{1,3},{3,1},{5,7},{7,5}} | collective-permute-start | bytes 6291464 | tf_op jit(solution)/shard_map/ppermute | solution.py:377
  1877.9 169.6 %collective-permute-start.71 = (bf16[1024,1024]{1,0:T(8,128)(2,1)}, bf16[1024,1024]{1,0:T(8,128)(2,1)}, u32[]{:S(2)}, u32[]{:S(2)}) collective-permute-start(bf16[1024,1024]{1,0:T(8,128)(2,1)} %collective-permute-done.70.near_ref), channel_id=1, source_target_pairs={{0,4},{2,6},{4,0},{6,2},{1,5},{3,7},{5,1},{7,3}} | collective-permute-start | bytes 6291464 | tf_op jit(solution)/shard_map/ppermute | solution.py:378
  1922.9 125.2 %collective-permute-start.69 = (bf16[1024,1024]{1,0:T(8,128)(2,1)}, bf16[1024,1024]{1,0:T(8,128)(2,1)}, u32[]{:S(2)}, u32[]{:S(2)}) collective-permute-start(bf16[1024,1024]{1,0:T(8,128)(2,1)} %collective-permute-done.68.near_ref), channel_id=1, source_target_pairs={{0,4},{2,6},{4,0},{6,2},{1,5},{3,7},{5,1},{7,3}} | collective-permute-start | bytes 6291464 | tf_op jit(solution)/shard_map/ppermute | solution.py:378
  1967.8 81.7 %collective-permute-start.67 = (bf16[1024,1024]{1,0:T(8,128)(2,1)}, bf16[1024,1024]{1,0:T(8,128)(2,1)}, u32[]{:S(2)}, u32[]{:S(2)}) collective-permute-start(bf16[1024,1024]{1,0:T(8,128)(2,1)} %collective-permute-done.66.near_ref), channel_id=1, source_target_pairs={{0,4},{2,6},{4,0},{6,2},{1,5},{3,7},{5,1},{7,3}} | collective-permute-start | bytes 6291464 | tf_op jit(solution)/shard_map/ppermute | solution.py:378
  2030.2 82.1 %collective-permute-start.65 = (bf16[1024,1024]{1,0:T(8,128)(2,1)}, bf16[1024,1024]{1,0:T(8,128)(2,1)}, u32[]{:S(2)}, u32[]{:S(2)}) collective-permute-start(bf16[1024,1024]{1,0:T(8,128)(2,1)} %collective-permute-done.64.near_ref), channel_id=1, source_target_pairs={{0,4},{2,6},{4,0},{6,2},{1,5},{3,7},{5,1},{7,3}} | collective-permute-start | bytes 6291464 | tf_op jit(solution)/shard_map/ppermute | solution.py:378
  2047.5 118.1 %collective-permute-start.60 = (bf16[1024,1024]{1,0:T(8,128)(2,1)}, bf16[1024,1024]{1,0:T(8,128)(2,1)}, u32[]{:S(2)}, u32[]{:S(2)}) collective-permute-start(bf16[1024,1024]{1,0:T(8,128)(2,1)} %collective-permute-done.59.near_ref), channel_id=1, source_target_pairs={{0,4},{2,6},{4,0},{6,2},{1,5},{3,7},{5,1},{7,3}} | collective-permute-start | bytes 6291464 | tf_op jit(solution)/shard_map/ppermute | solution.py:378
  2048.1 162.4 %collective-permute-start.58 = (bf16[1024,1024]{1,0:T(8,128)(2,1)}, bf16[1024,1024]{1,0:T(8,128)(2,1)}, u32[]{:S(2)}, u32[]{:S(2)}) collective-permute-start(bf16[1024,1024]{1,0:T(8,128)(2,1)} %collective-permute-done.57.near_ref), channel_id=1, source_target_pairs={{0,4},{2,6},{4,0},{6,2},{1,5},{3,7},{5,1},{7,3}} | collective-permute-start | bytes 6291464 | tf_op jit(solution)/shard_map/ppermute | solution.py:378
  2049.5 205.9 %collective-permute-start.56 = (bf16[1024,1024]{1,0:T(8,128)(2,1)}, bf16[1024,1024]{1,0:T(8,128)(2,1)}, u32[]{:S(2)}, u32[]{:S(2)}) collective-permute-start(bf16[1024,1024]{1,0:T(8,128)(2,1)} %collective-permute-done.55.near_ref), channel_id=1, source_target_pairs={{0,4},{2,6},{4,0},{6,2},{1,5},{3,7},{5,1},{7,3}} | collective-permute-start | bytes 6291464 | tf_op jit(solution)/shard_map/ppermute | solution.py:378
  2112.3 335.3 %collective-permute-start.63 = (bf16[4096,1024]{1,0:T(8,128)(2,1)}, bf16[4096,1024]{1,0:T(8,128)(2,1)}, u32[]{:S(2)}, u32[]{:S(2)}) collective-permute-start(bf16[4096,1024]{1,0:T(8,128)(2,1)} %get-tuple-element.263.w2_ref.refs_4_), channel_id=1, source_target_pairs={{0,1},{1,0},{2,3},{3,2},{4,5},{5,4},{6,7},{7,6}} | collective-permute-start | bytes 25165832 | tf_op jit(solution)/shard_map/ppermute | solution.py:382
  2120.6 327.1 %collective-permute-start.54 = (bf16[4096,1024]{1,0:T(8,128)(2,1)}, bf16[4096,1024]{1,0:T(8,128)(2,1)}, u32[]{:S(2)}, u32[]{:S(2)}) collective-permute-start(bf16[4096,1024]{1,0:T(8,128)(2,1)} %get-tuple-element.278.w2_ref.refs_4_), channel_id=1, source_target_pairs={{0,1},{1,0},{2,3},{3,2},{4,5},{5,4},{6,7},{7,6}} | collective-permute-start | bytes 25165832 | tf_op jit(solution)/shard_map/ppermute | solution.py:382
  2165.5 284.2 %collective-permute-start.45 = (bf16[1024,4096]{1,0:T(8,128)(2,1)}, bf16[1024,4096]{1,0:T(8,128)(2,1)}, u32[]{:S(2)}, u32[]{:S(2)}) collective-permute-start(bf16[1024,4096]{1,0:T(8,128)(2,1)} %get-tuple-element.250.w1_ref), channel_id=1, source_target_pairs={{0,1},{1,0},{2,3},{3,2},{4,5},{5,4},{6,7},{7,6}} | collective-permute-start | bytes 25165832 | tf_op jit(solution)/shard_map/ppermute | solution.py:382
  2210.5 93.1 %collective-permute-start.53 = (bf16[256,4096]{1,0:T(8,128)(2,1)}, bf16[256,4096]{1,0:T(8,128)(2,1)}, u32[]{:S(2)}, u32[]{:S(2)}) collective-permute-start(bf16[256,4096]{1,0:T(8,128)(2,1)} %collective-permute-done.52.near_ref), channel_id=1, source_target_pairs={{0,4},{2,6},{4,0},{6,2},{1,5},{3,7},{5,1},{7,3}} | collective-permute-start | bytes 6291464 | tf_op jit(solution)/shard_map/ppermute | solution.py:378
  2255.4 86.9 %collective-permute-start.51 = (bf16[256,4096]{1,0:T(8,128)(2,1)}, bf16[256,4096]{1,0:T(8,128)(2,1)}, u32[]{:S(2)}, u32[]{:S(2)}) collective-permute-start(bf16[256,4096]{1,0:T(8,128)(2,1)} %collective-permute-done.50.near_ref), channel_id=1, source_target_pairs={{0,4},{2,6},{4,0},{6,2},{1,5},{3,7},{5,1},{7,3}} | collective-permute-start | bytes 6291464 | tf_op jit(solution)/shard_map/ppermute | solution.py:378
  2303.6 293.5 %collective-permute-start.36 = (bf16[1024,4096]{1,0:T(8,128)(2,1)}, bf16[1024,4096]{1,0:T(8,128)(2,1)}, u32[]{:S(2)}, u32[]{:S(2)}) collective-permute-start(bf16[1024,4096]{1,0:T(8,128)(2,1)} %get-tuple-element.264.w1_ref.refs_5_), channel_id=1, source_target_pairs={{0,1},{1,0},{2,3},{3,2},{4,5},{5,4},{6,7},{7,6}} | collective-permute-start | bytes 25165832 | tf_op jit(solution)/shard_map/ppermute | solution.py:382
  2445.2 151.9 %collective-permute-start.44 = (bf16[256,4096]{1,0:T(8,128)(2,1)}, bf16[256,4096]{1,0:T(8,128)(2,1)}, u32[]{:S(2)}, u32[]{:S(2)}) collective-permute-start(bf16[256,4096]{1,0:T(8,128)(2,1)} %collective-permute-done.43.near_ref), channel_id=1, source_target_pairs={{0,4},{2,6},{4,0},{6,2},{1,5},{3,7},{5,1},{7,3}} | collective-permute-start | bytes 6291464 | tf_op jit(solution)/shard_map/ppermute | solution.py:378
  2447.7 158.8 %collective-permute-start.42 = (bf16[256,4096]{1,0:T(8,128)(2,1)}, bf16[256,4096]{1,0:T(8,128)(2,1)}, u32[]{:S(2)}, u32[]{:S(2)}) collective-permute-start(bf16[256,4096]{1,0:T(8,128)(2,1)} %collective-permute-done.41.near_ref), channel_id=1, source_target_pairs={{0,4},{2,6},{4,0},{6,2},{1,5},{3,7},{5,1},{7,3}} | collective-permute-start | bytes 6291464 | tf_op jit(solution)/shard_map/ppermute | solution.py:378
  2447.7 168.1 %collective-permute-start.40 = (bf16[256,4096]{1,0:T(8,128)(2,1)}, bf16[256,4096]{1,0:T(8,128)(2,1)}, u32[]{:S(2)}, u32[]{:S(2)}) collective-permute-start(bf16[256,4096]{1,0:T(8,128)(2,1)} %collective-permute-done.39.near_ref), channel_id=1, source_target_pairs={{0,4},{2,6},{4,0},{6,2},{1,5},{3,7},{5,1},{7,3}} | collective-permute-start | bytes 6291464 | tf_op jit(solution)/shard_map/ppermute | solution.py:378
  2449.7 175.4 %collective-permute-start.38 = (bf16[256,4096]{1,0:T(8,128)(2,1)}, bf16[256,4096]{1,0:T(8,128)(2,1)}, u32[]{:S(2)}, u32[]{:S(2)}) collective-permute-start(bf16[256,4096]{1,0:T(8,128)(2,1)} %collective-permute-done.37.near_ref), channel_id=1, source_target_pairs={{0,4},{2,6},{4,0},{6,2},{1,5},{3,7},{5,1},{7,3}} | collective-permute-start | bytes 6291464 | tf_op jit(solution)/shard_map/ppermute | solution.py:378
  (8 other events, 420.6 us)

commit v3 on v2

--- a/solution.py
+++ b/solution.py
@@ -18,11 +18,12 @@
 CONTRACT_LAST = (((1,), (1,)), ((), ()))
 VMEM_LIMIT = 63 * 1024 * 1024
 TILE = 512
+ACT_TILE = 128
 SLAB = 256
 FWD_BLOCK = 512
 BWD_BLOCK = 256
 HID_TILE = 256
-PARTS = 2
+PARTS = (1, 2)
 CHUNKS = 4
 ANY = pl.BlockSpec(memory_space=pl.ANY)
 
@@ -39,7 +40,7 @@
     lax.fori_loop(0, count, lambda i, c: (body(pl.ds(pl.multiple_of(i * SLAB, SLAB), SLAB)), c)[1], 0)
 
 
-def act_kernel(h_ref, w1_ref, act_ref, slope_ref, ut_hbm, u_s, ut_s, sem):
+def act_kernel(h_ref, w1_ref, act_ref, slope_ref, ut_hbm, u_s, ut_s, z_s, sem):
     step = pl.program_id(0)
     rows_total = h_ref.shape[0]
     ut_copy = pltpu.make_async_copy(ut_s, ut_hbm, sem)
@@ -55,12 +56,13 @@
         slabs(rows_total // SLAB, normalize)
         ut_copy.start()
 
-    for i in range(rows_total // TILE):
-        rows = pl.ds(i * TILE, TILE)
-        z = jnp.dot(u_s[rows, :], w1_ref[...], preferred_element_type=F32)
+    for i in range(rows_total // ACT_TILE):
+        rows = pl.ds(i * ACT_TILE, ACT_TILE)
+        z = z_s[rows, :]
         half = 0.5 * (1.0 + lax.erf(z * INV_SQRT2))
         act_ref[rows, :] = (z * half).astype(BF16)
         slope_ref[rows, :] = half + z * jnp.exp(-0.5 * z * z) * INV_SQRT_2PI
+        z_s[rows, :] = jnp.dot(u_s[rows, :], w1_ref[...], preferred_element_type=F32)
 
     @pl.when(step == pl.num_programs(0) - 1)
     def _():
@@ -76,14 +78,17 @@
         h_spec = pl.BlockSpec((rows, depth), lambda j: (0, 0), pipeline_mode=once)
     else:
         h_spec = pl.BlockSpec((None, None, None, rows, depth), lambda j: (0, 0, t, 0, 0), pipeline_mode=once)
+    blocks = ff // block
+    done_block = pl.BlockSpec((rows, block), lambda j: (0, jnp.maximum(j - 1, 0)))
     return pl.pallas_call(
         act_kernel,
-        grid=(ff // block,),
-        in_specs=[h_spec, pl.BlockSpec((depth, block), lambda j: (0, j))],
-        out_specs=[pl.BlockSpec((rows, block), lambda j: (0, j)), pl.BlockSpec((rows, block), lambda j: (0, j)), ANY],
+        grid=(blocks + 1,),
+        in_specs=[h_spec, pl.BlockSpec((depth, block), lambda j: (0, jnp.minimum(j, blocks - 1)))],
+        out_specs=[done_block, done_block, ANY],
         out_shape=[jax.ShapeDtypeStruct((rows, ff), BF16), jax.ShapeDtypeStruct((rows, ff), F32),
                    jax.ShapeDtypeStruct((depth, rows), BF16)],
-        scratch_shapes=[pltpu.VMEM((rows, depth), BF16), pltpu.VMEM((depth, rows), BF16), pltpu.SemaphoreType.DMA],
+        scratch_shapes=[pltpu.VMEM((rows, depth), BF16), pltpu.VMEM((depth, rows), BF16), pltpu.VMEM((rows, block), F32),
+                        pltpu.SemaphoreType.DMA],
         compiler_params=params_of(),
         cost_estimate=pl.CostEstimate(flops=2 * rows * depth * ff, bytes_accessed=rows * ff * 6 + depth * ff * 2,
                                       transcendentals=2 * rows * ff),
@@ -132,7 +137,7 @@
         return taken
 
     g_ref, ut_ref, act_ref, slope_ref, w2_ref = take(5)
-    closing = deep and part == PARTS - 1
+    closing = deep and part == PARTS[1] - 1
     if deep:
         w1_ref, = take(1)
     if deep and part:
@@ -219,9 +224,10 @@
     rows, ff = act.shape
     depth = g.shape[1]
     is_deep = deep is not None
-    closing = is_deep and part == PARTS - 1
+    parts = PARTS[layer]
+    closing = is_deep and part == parts - 1
     block = BWD_BLOCK
-    steps = ff // block // PARTS
+    steps = ff // block // parts
     first = part * steps
     in_cols = pl.BlockSpec((depth, block), lambda j: (0, first + j))
     out_rows = pl.BlockSpec((block, depth), lambda j: (first + j, 0))
@@ -272,72 +278,101 @@
         in_specs=in_specs, out_specs=out_specs, out_shape=out_shape, scratch_shapes=scratch,
         input_output_aliases=aliases,
         compiler_params=params_of(),
-        cost_estimate=pl.CostEstimate(flops=(8 if is_deep else 6) * rows * depth * ff // PARTS,
-                                      bytes_accessed=(rows * ff * 6 + depth * ff * 24) // PARTS, transcendentals=0),
+        cost_estimate=pl.CostEstimate(flops=(8 if is_deep else 6) * rows * depth * ff // parts,
+                                      bytes_accessed=(rows * ff * 6 + depth * ff * 24) // parts, transcendentals=0),
     )(*args)
 
 
-def chunk_specs(shape, layer, part, steps):
+def chunk_specs(shape, layer, part, count, steps):
     rows, cols = shape
     band = rows // CHUNKS // steps
     first = part * steps
+
+    def alone(m):
+        return pl.BlockSpec((band, cols), lambda j: (jnp.clip(j - m * steps, 0, steps - 1), 0))
+
     return (pl.BlockSpec((None, None, None, band, cols), lambda j: (0, 0, layer, first + j, 0)),
             pl.BlockSpec((band, cols), lambda j: (first + j, 0)),
-            pl.BlockSpec((band, cols), lambda j: (j, 0)))
-
-
-def cast_kernel(has_prev, p_ref, *refs):
-    whole_ref, wire_ref = refs[1:] if has_prev else refs
+            [alone(m) for m in range(count)])
+
+
+def in_turn(count, steps, body):
+    if count == 1:
+        return body(0)
+    turn = pl.program_id(0) // steps
+    for m in range(count):
+        pl.when(turn == m)(functools.partial(body, m))
+
+
+def cast_kernel(count, steps, n_prev, p_ref, *refs):
+    whole_ref, *wire_refs = refs[n_prev:]
     value = p_ref[...].astype(BF16)
     whole_ref[...] = value
-    wire_ref[...] = value
-
-
-def cast_chunk(p, layer, part, prev):
+
+    def put(m):
+        wire_refs[m][...] = value
+
+    in_turn(count, steps, put)
+
+
+def cast_chunks(p, layer, part, count, prev):
     shape = p.shape[-2:]
     steps = 2
-    param_spec, layer_spec, wire_spec = chunk_specs(shape, layer, part, steps)
+    param_spec, layer_spec, wire_specs = chunk_specs(shape, layer, part, count, steps)
+    args, in_specs = [p], [param_spec]
+    if prev is not None:
+        args.append(prev)
+        in_specs.append(ANY)
+    wire = jax.ShapeDtypeStruct((shape[0] // CHUNKS, shape[1]), BF16)
     return pl.pallas_call(
-        functools.partial(cast_kernel, prev is not None),
-        grid=(steps,),
-        in_specs=[param_spec] + ([ANY] if prev is not None else []),
-        out_specs=[layer_spec, wire_spec],
-        out_shape=[jax.ShapeDtypeStruct(shape, BF16), jax.ShapeDtypeStruct((shape[0] // CHUNKS, shape[1]), BF16)],
+        functools.partial(cast_kernel, count, steps, len(args) - 1),
+        grid=(count * steps,),
+        in_specs=in_specs,
+        out_specs=[layer_spec, *wire_specs],
+        out_shape=[jax.ShapeDtypeStruct(shape, BF16)] + [wire] * count,
         input_output_aliases={1: 0} if prev is not None else {},
         compiler_params=params_of(),
-        cost_estimate=pl.CostEstimate(flops=10 ** 9, bytes_accessed=8 * shape[0] * shape[1] // CHUNKS, transcendentals=0),
-    )(*([p] + ([prev] if prev is not None else [])))
-
-
-def mix_kernel(rate, n_prev, final, par_ref, p_ref, grad_ref, col_ref, near_ref, far_ref, *refs):
-    refs = refs[n_prev:]
-    near = near_ref[...].astype(F32)
-    far = far_ref[...].astype(F32)
+        cost_estimate=pl.CostEstimate(flops=10 ** 9, bytes_accessed=8 * count * shape[0] * shape[1] // CHUNKS,
+                                      transcendentals=0),
+    )(*args)
+
+
+def mix_kernel(rate, count, steps, n_prev, final, par_ref, p_ref, grad_ref, col_ref, *refs):
+    near_refs, far_refs = refs[:count], refs[count:2 * count]
+    outs = refs[2 * count + n_prev:]
     even = par_ref[0] == 0
-    col = col_ref[...].astype(F32)
-    mix = p_ref[...] + col + col
-    mix = mix + jnp.where(even, far, near)
-    mix = mix + jnp.where(even, near, far)
-    new = mix / 5.0 - rate * grad_ref[...]
-    refs[0][...] = new
-    if not final:
-        value = new.astype(BF16)
-        refs[1][...] = value
-        refs[2][...] = value
-
-
-def mix_chunk(par, p, grad, col, near, far, layer, part, rate, prev_param, prev_layer, final):
+
+    def mix_one(m):
+        near = near_refs[m][...].astype(F32)
+        far = far_refs[m][...].astype(F32)
+        col = col_ref[...].astype(F32)
+        mix = p_ref[...] + col + col
+        mix = mix + jnp.where(even, far, near)
+        mix = mix + jnp.where(even, near, far)
+        new = mix / 5.0 - rate * grad_ref[...]
+        outs[0][...] = new
+        if not final:
+            value = new.astype(BF16)
+            outs[1][...] = value
+            outs[2 + m][...] = value
+
+    in_turn(count, steps, mix_one)
+
+
+def mix_chunks(par, p, grad, col, nears, fars, layer, part, rate, prev_param, prev_layer, final):
     shape = p.shape[-2:]
-    steps = 8
-    param_spec, layer_spec, wire_spec = chunk_specs(shape, layer, part, steps)
-    args = [par, p, grad, col, near, far]
-    in_specs = [pl.BlockSpec(memory_space=pltpu.SMEM), param_spec, layer_spec, layer_spec, wire_spec, wire_spec]
+    steps = 4
+    count = len(nears)
+    param_spec, layer_spec, wire_specs = chunk_specs(shape, layer, part, count, steps)
+    args = [par, p, grad, col, *nears, *fars]
+    in_specs = [pl.BlockSpec(memory_space=pltpu.SMEM), param_spec, layer_spec, layer_spec, *wire_specs, *wire_specs]
     aliases = {}
     out_shape = [jax.ShapeDtypeStruct(p.shape, F32)]
     out_specs = [param_spec]
     if not final:
-        out_shape += [jax.ShapeDtypeStruct(shape, BF16), jax.ShapeDtypeStruct((shape[0] // CHUNKS, shape[1]), BF16)]
-        out_specs += [layer_spec, wire_spec]
+        out_shape += [jax.ShapeDtypeStruct(shape, BF16)]
+        out_shape += [jax.ShapeDtypeStruct((shape[0] // CHUNKS, shape[1]), BF16)] * count
+        out_specs += [layer_spec, *wire_specs]
     n_prev = 0
     for prev, out_idx in ((prev_param, 0), (None if final else prev_layer, 1)):
         if prev is not None:
@@ -346,13 +381,27 @@
             in_specs.append(ANY)
             n_prev += 1
     return pl.pallas_call(
-        functools.partial(mix_kernel, rate, n_prev, final),
-        grid=(steps,),
+        functools.partial(mix_kernel, rate, count, steps, n_prev, final),
+        grid=(count * steps,),
         in_specs=in_specs, out_specs=out_specs, out_shape=out_shape,
         input_output_aliases=aliases,
         compiler_params=params_of(),
-        cost_estimate=pl.CostEstimate(flops=10 ** 9, bytes_accessed=20 * shape[0] * shape[1] // CHUNKS, transcendentals=0),
+        cost_estimate=pl.CostEstimate(flops=10 ** 9, bytes_accessed=20 * count * shape[0] * shape[1] // CHUNKS,
+                                      transcendentals=0),
     )(*args)
+
+
+CAST_GROUPS = (1, 3, 4, 4, 4)
+MIX_GROUPS = (2,) * 8
+LAST_GROUPS = (2,) * 6 + (1,) * 4
+
+
+def grouped(groups):
+    first, out = 0, []
+    for count in groups:
+        out.append((first, count))
+        first += count
+    return out
 
 
 def solution(mesh):
@@ -362,7 +411,6 @@
     near_pairs = [(i, i ^ 1) for i in range(row_size)]
     far_pairs = [(i, i ^ 2) for i in range(row_size)]
     col_pairs = [(i, (i + 1) % col_size) for i in range(col_size)]
-    total = 2 * layers * CHUNKS
 
     def locate(i):
         return i // (2 * CHUNKS), (i // CHUNKS) % 2, i % CHUNKS
@@ -403,7 +451,7 @@
                 act, slope, ut = outs[layer][:3]
                 deep = (outs[layer - 1][3], outs[layer][3], targets) if layer else None
                 res = None
-                for part in range(PARTS):
+                for part in range(PARTS[layer]):
                     res = backward(part, g, ut, act, slope,
                                  *weights[layer], *olds[layer], res, step == 1, rate, layer, deep, scale, t)
                 if layer:
@@ -414,10 +462,11 @@
         params = [w_in, w_out]
         weights = [[None, None] for _ in range(layers)]
         moved = []
-        for i in range(total):
-            layer, kind, part = locate(i)
-            weights[layer][kind], wire = cast_chunk(params[kind], layer, part, weights[layer][kind])
-            moved.append(send(i, wire, weights))
+        for first, count in grouped(CAST_GROUPS):
+            layer, kind, part = locate(first)
+            weights[layer][kind], *wires = cast_chunks(params[kind], layer, part, count,
+                                                  weights[layer][kind])
+            moved += [send(first + m, wire, weights) for m, wire in enumerate(wires)]
         head = run_forward(weights, 0)
         for window in range(windows):
             final = window == windows - 1
@@ -429,17 +478,18 @@
             new_params = [None, None]
             new_weights = [[None, None] for _ in range(layers)]
             new_moved, head = [], []
-            for i in range(total):
+            for i, count in grouped(LAST_GROUPS if final else MIX_GROUPS):
                 layer, kind, part = locate(i)
-                near, far, _ = moved[i]
+                members = moved[i:i + count]
                 cols = moved[i - i % CHUNKS + CHUNKS - 1][2]
-                res = mix_chunk(par, params[kind], second[layer][kind], cols, near, far,
+                res = mix_chunks(par, params[kind], second[layer][kind], cols,
+                             [m[0] for m in members], [m[1] for m in members],
                              layer, part, rate, new_params[kind], new_weights[layer][kind], final)
                 new_params[kind] = res[0]
                 if not final:
                     new_weights[layer][kind] = res[1]
-                    new_moved.append(send(i, res[2], new_weights))
-                    if i % (2 * CHUNKS) == 2 * CHUNKS - 1:
+                    new_moved += [send(i + m, wire, new_weights) for m, wire in enumerate(res[2:])]
+                    if (i + count) % (2 * CHUNKS) == 0:
                         h = inputs if layer == 0 else head[-1][3]
                         head.append(fwd(layer, h, new_weights, step_a + 2))
             params, weights, moved = new_params, new_weights, new_moved

time: 2650 us -> 2590 us (0.977)
  Pallas kernels: 1570 us -> 1450 us
  waiting for transfers between devices: 1010 us -> 1060 us
    pallas_call x56 -> x31, Pallas kernels: 674 us -> 583 us  [the longest x8 272 us: activate(): pl.pallas_call(act_kernel, grid=(blocks + 1,), in_specs=[h_spec, pl.Block...]
    ppermute x32, waiting for transfers between devices: 670 us -> 744 us  [send(): near = lax.ppermute(wire, 'row', near_pairs)]
    pallas_call x16 -> x12, Pallas kernels: 695 us -> 666 us  [backward(): pl.pallas_call(functools.partial(bwd_kernel, is_deep, second, part, scale...]
  transfers between devices with their start and end apart: 72 -> 72, of which waited for: 31 -> 29; matrix products, arithmetic and copies ran while one was open for 0% -> 0% of each run, Pallas kernels for 59% -> 55%
where the time goes in v3:
time: 2590 us; the launch traced here: 2580 us
  Pallas kernels  1450 us (56%)
  waiting for transfers between devices  1060 us (41%)
  starting transfers between devices  78.8 us (3%)
    ppermute x32, waiting for transfers between devices, send(): near = lax.ppermute(wire, 'row', near_pairs)  744 us
    pallas_call x12, Pallas kernels, backward(): pl.pallas_call(functools.partial(bwd_kernel, is_deep, second, part, scale...  666 us
    ppermute x32, waiting for transfers between devices, send(): far = lax.ppermute(near, 'row', far_pairs)  311 us
    pallas_call x8, Pallas kernels, activate(): pl.pallas_call(act_kernel, grid=(blocks + 1,), in_specs=[h_spec, pl.Block...  272 us
    pallas_call x18, Pallas kernels, mix_chunks(): pl.pallas_call(functools.partial(mix_kernel, rate, count, steps, n_prev,...  255 us
    pallas_call x8, Pallas kernels, hidden(): pl.pallas_call(functools.partial(hidden_kernel, last, scale), grid=(rows...  200 us
    pallas_call x5, Pallas kernels, cast_chunks(): pl.pallas_call(functools.partial(cast_kernel, count, steps, len(args) - 1...  56.1 us
  transfers between devices with their start and end apart: 72, of which 29 were waited for; matrix products, arithmetic and copies ran while one was open for 0% of the time, Pallas kernels for 55%

profile of v3, /device:TPU:0, one launch (start us, length us, event | category | flops | bytes accessed | tf_op | source)
XLA Modules:
  0.0 2583.9 jit_solution(5701583021205603723)
XLA Ops:
  64.1 33.9 %shard_map.61 = (bf16[2048,4096]{1,0:T(8,128)(2,1)}, f32[2048,4096]{1,0:T(8,128)}, bf16[1024,2048]{1,0:T(8,128)(2,1)}) custom-call(bf16[1,1,4,2048,1024]{4,3,2,1,0:T(8,128)(2,1)} %h_ref.15, bf16[1024,4096]{1,0:T(8,128)(2,1)} %get-tuple-element.132.w1_ref), custom_call_target="tpu_custom_call" | custom-call | flops 17179869184 | bytes 58720256 | tf_op jit(solution)/shard_map/pallas_call | solution.py:83
  98.0 23.9 shard_map.63.h_ref.refs_7_
  121.9 33.8 %shard_map.65 = (bf16[2048,4096]{1,0:T(8,128)(2,1)}, f32[2048,4096]{1,0:T(8,128)}, bf16[1024,2048]{1,0:T(8,128)(2,1)}) custom-call(bf16[2048,1024]{1,0:T(8,128)(2,1)} %shard_map.63.h_ref.refs_7_, bf16[1024,4096]{1,0:T(8,128)(2,1)} %get-tuple-element.135.w1_ref.refs_5_), custom_call_target="tpu_custom_call" | custom-call | flops 17179869184 | bytes 58720256 | tf_op jit(solution)/shard_map/pallas_call | solution.py:83
  155.7 25.5 shard_map.67
  181.2 49.1 %shard_map.68 = (f32[1024,4096]{1,0:T(8,128)}, f32[4096,1024]{1,0:T(8,128)}, bf16[1024,4096]{1,0:T(8,128)(2,1)}, bf16[4096,1024]{1,0:T(8,128)(2,1)}, f32[2048,1024]{1,0:T(8,128)}) custom-call(bf16[2048,1024]{1,0:T(8,128)(2,1)} %get-tuple-element.138.refs_0_, bf16[1024,2048]{1,0:T(8,128)(2,1)} %get-tuple-element.139.refs_1_, ...), custom_call_target="tpu_custom_call" | custom-call | flops 34359738368 | bytes 75497472 | tf_op jit(solution)/shard_map/pallas_call | solution.py:275
  232.5 54.8 %shard_map.69 = (f32[1024,4096]{1,0:T(8,128)}, f32[4096,1024]{1,0:T(8,128)}, bf16[1024,4096]{1,0:T(8,128)(2,1)}, bf16[4096,1024]{1,0:T(8,128)(2,1)}, bf16[2048,1024]{1,0:T(8,128)(2,1)}) custom-call(bf16[2048,1024]{1,0:T(8,128)(2,1)} %get-tuple-element.138.refs_0_, ...), custom_call_target="tpu_custom_call", output_to_operand_aliasing={{0}: (12, {}), {1}: (13, {}), {2}: (14, {}), {3}: (15, {})} | custom-call | flops 34359738368 | bytes 75497472 | tf_op jit(solution)/shard_map/pallas_call | solution.py:275
  291.5 42.9 %collective-permute-done.28.refs_0_ = bf16[1024,1024]{1,0:T(8,128)(2,1)} collective-permute-done((bf16[1024,1024]{1,0:T(8,128)(2,1)}, bf16[1024,1024]{1,0:T(8,128)(2,1)}, u32[]{:S(2)}, u32[]{:S(2)}) %collective-permute-start.28) | collective-permute-done | bytes 2097184 | tf_op jit(solution)/shard_map/ppermute | solution.py:425
  336.4 63.4 %shard_map.70 = (f32[1024,4096]{1,0:T(8,128)}, f32[4096,1024]{1,0:T(8,128)}, bf16[1024,4096]{1,0:T(8,128)(2,1)}, bf16[4096,1024]{1,0:T(8,128)(2,1)}) custom-call(bf16[2048,1024]{1,0:T(8,128)(2,1)} %get-tuple-element.147.refs_0_, bf16[1024,2048]{1,0:T(8,128)(2,1)} %get-tuple-element.148.refs_1_, bf16[2048,4096]{1,0:T(8,128)(2,1)} %get-tuple-element.133.act_ref.refs_2_, ...), custom_call_target="tpu_custom_call" | custom-call | flops 51539607552 | bytes 150994944 | tf_op jit(solution)/shard_map/pallas_call | solution.py:275
  399.8 24.5 collective-permute-done.15.refs_1_
  426.3 42.9 %collective-permute-done.14.refs_0_ = bf16[256,4096]{1,0:T(8,128)(2,1)} collective-permute-done((bf16[256,4096]{1,0:T(8,128)(2,1)}, bf16[256,4096]{1,0:T(8,128)(2,1)}, u32[]{:S(2)}, u32[]{:S(2)}) %collective-permute-start.14) | collective-permute-done | bytes 2097184 | tf_op jit(solution)/shard_map/ppermute | solution.py:425
  471.2 42.9 %collective-permute-done.10.refs_0_ = bf16[256,4096]{1,0:T(8,128)(2,1)} collective-permute-done((bf16[256,4096]{1,0:T(8,128)(2,1)}, bf16[256,4096]{1,0:T(8,128)(2,1)}, u32[]{:S(2)}, u32[]{:S(2)}) %collective-permute-start.10) | collective-permute-done | bytes 2097184 | tf_op jit(solution)/shard_map/ppermute | solution.py:425
  516.2 42.9 %collective-permute-done.11.refs_1_ = bf16[256,4096]{1,0:T(8,128)(2,1)} collective-permute-done((bf16[256,4096]{1,0:T(8,128)(2,1)}, bf16[256,4096]{1,0:T(8,128)(2,1)}, u32[]{:S(2)}, u32[]{:S(2)}) %collective-permute-start.11) | collective-permute-done | bytes 2097184 | tf_op jit(solution)/shard_map/ppermute | solution.py:425
  561.1 34.2 %shard_map.71 = (bf16[2048,4096]{1,0:T(8,128)(2,1)}, f32[2048,4096]{1,0:T(8,128)}, bf16[1024,2048]{1,0:T(8,128)(2,1)}) custom-call(bf16[1,1,4,2048,1024]{4,3,2,1,0:T(8,128)(2,1)} %h_ref.15, bf16[1024,4096]{1,0:T(8,128)(2,1)} %get-tuple-element.150.w1_ref), custom_call_target="tpu_custom_call" | custom-call | flops 17179869184 | bytes 58720256 | tf_op jit(solution)/shard_map/pallas_call | solution.py:83
  595.4 24.5 shard_map.72.h_ref.refs_7_
  619.8 29.1 %collective-permute-done.6.refs_1_ = bf16[256,4096]{1,0:T(8,128)(2,1)} collective-permute-done((bf16[256,4096]{1,0:T(8,128)(2,1)}, bf16[256,4096]{1,0:T(8,128)(2,1)}, u32[]{:S(2)}, u32[]{:S(2)}) %collective-permute-start.6) | collective-permute-done | bytes 2097184 | tf_op jit(solution)/shard_map/ppermute | solution.py:425
  651.0 42.9 %collective-permute-done.1.refs_0_ = bf16[256,4096]{1,0:T(8,128)(2,1)} collective-permute-done((bf16[256,4096]{1,0:T(8,128)(2,1)}, bf16[256,4096]{1,0:T(8,128)(2,1)}, u32[]{:S(2)}, u32[]{:S(2)}) %collective-permute-start.1) | collective-permute-done | bytes 2097184 | tf_op jit(solution)/shard_map/ppermute | solution.py:425
  696.0 42.0 %collective-permute-done.2.refs_1_ = bf16[256,4096]{1,0:T(8,128)(2,1)} collective-permute-done((bf16[256,4096]{1,0:T(8,128)(2,1)}, bf16[256,4096]{1,0:T(8,128)(2,1)}, u32[]{:S(2)}, u32[]{:S(2)}) %collective-permute-start.2) | collective-permute-done | bytes 2097184 | tf_op jit(solution)/shard_map/ppermute | solution.py:425
  740.0 33.9 %shard_map.73 = (bf16[2048,4096]{1,0:T(8,128)(2,1)}, f32[2048,4096]{1,0:T(8,128)}, bf16[1024,2048]{1,0:T(8,128)(2,1)}) custom-call(bf16[2048,1024]{1,0:T(8,128)(2,1)} %shard_map.72.h_ref.refs_7_, bf16[1024,4096]{1,0:T(8,128)(2,1)} %get-tuple-element.153.w1_ref.refs_5_), custom_call_target="tpu_custom_call" | custom-call | flops 17179869184 | bytes 58720256 | tf_op jit(solution)/shard_map/pallas_call | solution.py:83
  773.9 25.5 shard_map.74
  801.5 30.3 %collective-permute-done.17.refs_3_ = bf16[256,4096]{1,0:T(8,128)(2,1)} collective-permute-done((bf16[256,4096]{1,0:T(8,128)(2,1)}, bf16[256,4096]{1,0:T(8,128)(2,1)}, u32[]{:S(2)}, u32[]{:S(2)}) %collective-permute-start.17) | collective-permute-done | bytes 2097184 | tf_op jit(solution)/shard_map/ppermute | solution.py:426
  833.5 48.5 %shard_map.75 = (f32[1024,4096]{1,0:T(8,128)}, f32[4096,1024]{1,0:T(8,128)}, f32[2048,1024]{1,0:T(8,128)}) custom-call(bf16[2048,1024]{1,0:T(8,128)(2,1)} %get-tuple-element.156.refs_0_, bf16[1024,2048]{1,0:T(8,128)(2,1)} %get-tuple-element.157.refs_1_, bf16[2048,4096]{1,0:T(8,128)(2,1)} %get-tuple-element.154.act_ref.refs_2_, ...), custom_call_target="tpu_custom_call" | custom-call | flops 34359738368 | bytes 75497472 | tf_op jit(solution)/shard_map/pallas_call | solution.py:275
  882.1 39.5 %collective-permute-done.12.refs_2_ = bf16[256,4096]{1,0:T(8,128)(2,1)} collective-permute-done((bf16[256,4096]{1,0:T(8,128)(2,1)}, bf16[256,4096]{1,0:T(8,128)(2,1)}, u32[]{:S(2)}, u32[]{:S(2)}) %collective-permute-start.12) | collective-permute-done | bytes 2097184 | tf_op jit(solution)/shard_map/ppermute | solution.py:426
  923.4 43.2 %collective-permute-done.13.refs_3_ = bf16[256,4096]{1,0:T(8,128)(2,1)} collective-permute-done((bf16[256,4096]{1,0:T(8,128)(2,1)}, bf16[256,4096]{1,0:T(8,128)(2,1)}, u32[]{:S(2)}, u32[]{:S(2)}) %collective-permute-start.13) | collective-permute-done | bytes 2097184 | tf_op jit(solution)/shard_map/ppermute | solution.py:426
  968.4 54.3 %shard_map.76 = (f32[1024,4096]{1,0:T(8,128)}, f32[4096,1024]{1,0:T(8,128)}, bf16[2048,1024]{1,0:T(8,128)(2,1)}) custom-call(bf16[2048,1024]{1,0:T(8,128)(2,1)} %get-tuple-element.156.refs_0_, bf16[1024,2048]{1,0:T(8,128)(2,1)} %get-tuple-element.157.refs_1_, ...), custom_call_target="tpu_custom_call", output_to_operand_aliasing={{0}: (12, {}), {1}: (13, {})} | custom-call | flops 34359738368 | bytes 75497472 | tf_op jit(solution)/shard_map/pallas_call | solution.py:275
  1022.7 32.1 %collective-permute-done.8.refs_3_ = bf16[256,4096]{1,0:T(8,128)(2,1)} collective-permute-done((bf16[256,4096]{1,0:T(8,128)(2,1)}, bf16[256,4096]{1,0:T(8,128)(2,1)}, u32[]{:S(2)}, u32[]{:S(2)}) %collective-permute-start.8) | collective-permute-done | bytes 2097184 | tf_op jit(solution)/shard_map/ppermute | solution.py:426
  1056.8 63.0 %shard_map.77 = (f32[1024,4096]{1,0:T(8,128)}, f32[4096,1024]{1,0:T(8,128)}) custom-call(bf16[2048,1024]{1,0:T(8,128)(2,1)} %get-tuple-element.170.refs_0_, bf16[1024,2048]{1,0:T(8,128)(2,1)} %get-tuple-element.171.refs_1_, bf16[2048,4096]{1,0:T(8,128)(2,1)} %get-tuple-element.151.act_ref.refs_2_, f32[2048,4096]{1,0:T(8,128)} %get-tuple-element.172.refs_3_, ...), custom_call_target="tpu_custom_call" | custom-call | flops 51539607552 | bytes 150994944 | tf_op jit(solution)/shard_map/pallas_call | solution.py:275
  1119.8 17.6 shard_map.78
  1137.5 17.2 shard_map.79
  1156.7 34.0 %shard_map.82 = (bf16[2048,4096]{1,0:T(8,128)(2,1)}, f32[2048,4096]{1,0:T(8,128)}, bf16[1024,2048]{1,0:T(8,128)(2,1)}) custom-call(bf16[1,1,4,2048,1024]{4,3,2,1,0:T(8,128)(2,1)} %h_ref.15, bf16[1024,4096]{1,0:T(8,128)(2,1)} %get-tuple-element.186.w1_ref), custom_call_target="tpu_custom_call" | custom-call | flops 17179869184 | bytes 58720256 | tf_op jit(solution)/shard_map/pallas_call | solution.py:83
  1190.7 17.2 shard_map.83
  1207.9 17.2 shard_map.84
  1227.2 24.5 shard_map.85.h_ref.refs_7_
  1251.6 17.1 shard_map.80
  1268.8 17.2 shard_map.81
  1289.5 33.9 %shard_map.86 = (bf16[2048,4096]{1,0:T(8,128)(2,1)}, f32[2048,4096]{1,0:T(8,128)}, bf16[1024,2048]{1,0:T(8,128)(2,1)}) custom-call(bf16[2048,1024]{1,0:T(8,128)(2,1)} %shard_map.85.h_ref.refs_7_, bf16[1024,4096]{1,0:T(8,128)(2,1)} %get-tuple-element.196.w1_ref.refs_5_), custom_call_target="tpu_custom_call" | custom-call | flops 17179869184 | bytes 58720256 | tf_op jit(solution)/shard_map/pallas_call | solution.py:83
  1323.4 17.2 shard_map.87
  1342.6 17.1 shard_map.88
  1359.7 25.4 shard_map.89
  1387.2 37.4 %collective-permute-done.64.refs_0_ = bf16[1024,1024]{1,0:T(8,128)(2,1)} collective-permute-done((bf16[1024,1024]{1,0:T(8,128)(2,1)}, bf16[1024,1024]{1,0:T(8,128)(2,1)}, u32[]{:S(2)}, u32[]{:S(2)}) %collective-permute-start.64) | collective-permute-done | bytes 2097184 | tf_op jit(solution)/shard_map/ppermute | solution.py:425
  1426.1 48.8 %shard_map.90 = (f32[1024,4096]{1,0:T(8,128)}, f32[4096,1024]{1,0:T(8,128)}, bf16[1024,4096]{1,0:T(8,128)(2,1)}, bf16[4096,1024]{1,0:T(8,128)(2,1)}, f32[2048,1024]{1,0:T(8,128)}) custom-call(bf16[2048,1024]{1,0:T(8,128)(2,1)} %get-tuple-element.207.refs_0_, bf16[1024,2048]{1,0:T(8,128)(2,1)} %get-tuple-element.208.refs_1_, ...), custom_call_target="tpu_custom_call" | custom-call | flops 34359738368 | bytes 75497472 | tf_op jit(solution)/shard_map/pallas_call | solution.py:275
  1475.5 39.0 %collective-permute-done.61.refs_0_ = bf16[1024,1024]{1,0:T(8,128)(2,1)} collective-permute-done((bf16[1024,1024]{1,0:T(8,128)(2,1)}, bf16[1024,1024]{1,0:T(8,128)(2,1)}, u32[]{:S(2)}, u32[]{:S(2)}) %collective-permute-start.61) | collective-permute-done | bytes 2097184 | tf_op jit(solution)/shard_map/ppermute | solution.py:425
  1516.0 43.5 %collective-permute-done.59.refs_0_ = bf16[1024,1024]{1,0:T(8,128)(2,1)} collective-permute-done((bf16[1024,1024]{1,0:T(8,128)(2,1)}, bf16[1024,1024]{1,0:T(8,128)(2,1)}, u32[]{:S(2)}, u32[]{:S(2)}) %collective-permute-start.59) | collective-permute-done | bytes 2097184 | tf_op jit(solution)/shard_map/ppermute | solution.py:425
  1561.0 43.5 %collective-permute-done.57.refs_0_ = bf16[1024,1024]{1,0:T(8,128)(2,1)} collective-permute-done((bf16[1024,1024]{1,0:T(8,128)(2,1)}, bf16[1024,1024]{1,0:T(8,128)(2,1)}, u32[]{:S(2)}, u32[]{:S(2)}) %collective-permute-start.57) | collective-permute-done | bytes 2097184 | tf_op jit(solution)/shard_map/ppermute | solution.py:425
  1605.9 43.5 %collective-permute-done.55.refs_0_ = bf16[1024,1024]{1,0:T(8,128)(2,1)} collective-permute-done((bf16[1024,1024]{1,0:T(8,128)(2,1)}, bf16[1024,1024]{1,0:T(8,128)(2,1)}, u32[]{:S(2)}, u32[]{:S(2)}) %collective-permute-start.55) | collective-permute-done | bytes 2097184 | tf_op jit(solution)/shard_map/ppermute | solution.py:425
  1650.9 55.2 %shard_map.91 = (f32[1024,4096]{1,0:T(8,128)}, f32[4096,1024]{1,0:T(8,128)}, bf16[1024,4096]{1,0:T(8,128)(2,1)}, bf16[4096,1024]{1,0:T(8,128)(2,1)}, bf16[2048,1024]{1,0:T(8,128)(2,1)}) custom-call(bf16[2048,1024]{1,0:T(8,128)(2,1)} %get-tuple-element.207.refs_0_, ...), custom_call_target="tpu_custom_call", output_to_operand_aliasing={{0}: (12, {}), {1}: (13, {}), {2}: (14, {}), {3}: (15, {})} | custom-call | flops 34359738368 | bytes 75497472 | tf_op jit(solution)/shard_map/pallas_call | solution.py:275
  1706.6 32.7 %collective-permute-done.51.refs_1_ = bf16[256,4096]{1,0:T(8,128)(2,1)} collective-permute-done((bf16[256,4096]{1,0:T(8,128)(2,1)}, bf16[256,4096]{1,0:T(8,128)(2,1)}, u32[]{:S(2)}, u32[]{:S(2)}) %collective-permute-start.51) | collective-permute-done | bytes 2097184 | tf_op jit(solution)/shard_map/ppermute | solution.py:425
  1740.7 43.5 %collective-permute-done.46.refs_0_ = bf16[256,4096]{1,0:T(8,128)(2,1)} collective-permute-done((bf16[256,4096]{1,0:T(8,128)(2,1)}, bf16[256,4096]{1,0:T(8,128)(2,1)}, u32[]{:S(2)}, u32[]{:S(2)}) %collective-permute-start.46) | collective-permute-done | bytes 2097184 | tf_op jit(solution)/shard_map/ppermute | solution.py:425
  1785.7 43.5 %collective-permute-done.47.refs_1_ = bf16[256,4096]{1,0:T(8,128)(2,1)} collective-permute-done((bf16[256,4096]{1,0:T(8,128)(2,1)}, bf16[256,4096]{1,0:T(8,128)(2,1)}, u32[]{:S(2)}, u32[]{:S(2)}) %collective-permute-start.47) | collective-permute-done | bytes 2097184 | tf_op jit(solution)/shard_map/ppermute | solution.py:425
  1830.6 43.4 %collective-permute-done.41.refs_0_ = bf16[256,4096]{1,0:T(8,128)(2,1)} collective-permute-done((bf16[256,4096]{1,0:T(8,128)(2,1)}, bf16[256,4096]{1,0:T(8,128)(2,1)}, u32[]{:S(2)}, u32[]{:S(2)}) %collective-permute-start.41) | collective-permute-done | bytes 2097184 | tf_op jit(solution)/shard_map/ppermute | solution.py:425
  1875.6 63.4 %shard_map.92 = (f32[1024,4096]{1,0:T(8,128)}, f32[4096,1024]{1,0:T(8,128)}, bf16[1024,4096]{1,0:T(8,128)(2,1)}, bf16[4096,1024]{1,0:T(8,128)(2,1)}) custom-call(bf16[2048,1024]{1,0:T(8,128)(2,1)} %get-tuple-element.217.refs_0_, bf16[1024,2048]{1,0:T(8,128)(2,1)} %get-tuple-element.218.refs_1_, bf16[2048,4096]{1,0:T(8,128)(2,1)} %get-tuple-element.187.act_ref.refs_2_, ...), custom_call_target="tpu_custom_call" | custom-call | flops 51539607552 | bytes 150994944 | tf_op jit(solution)/shard_map/pallas_call | solution.py:275
  1939.6 24.4 collective-permute-done.37.refs_0_
  1965.5 39.2 %collective-permute-done.38.refs_1_ = bf16[256,4096]{1,0:T(8,128)(2,1)} collective-permute-done((bf16[256,4096]{1,0:T(8,128)(2,1)}, bf16[256,4096]{1,0:T(8,128)(2,1)}, u32[]{:S(2)}, u32[]{:S(2)}) %collective-permute-start.38) | collective-permute-done | bytes 2097184 | tf_op jit(solution)/shard_map/ppermute | solution.py:425
  2007.9 34.0 %shard_map.93 = (bf16[2048,4096]{1,0:T(8,128)(2,1)}, f32[2048,4096]{1,0:T(8,128)}, bf16[1024,2048]{1,0:T(8,128)(2,1)}) custom-call(bf16[1,1,4,2048,1024]{4,3,2,1,0:T(8,128)(2,1)} %h_ref.15, bf16[1024,4096]{1,0:T(8,128)(2,1)} %get-tuple-element.220.w1_ref), custom_call_target="tpu_custom_call" | custom-call | flops 17179869184 | bytes 58720256 | tf_op jit(solution)/shard_map/pallas_call | solution.py:83
  2042.0 24.9 shard_map.94.h_ref.refs_7_
  2077.7 44.9 %collective-permute-done.60.refs_1_ = bf16[1024,1024]{1,0:T(8,128)(2,1)} collective-permute-done((bf16[1024,1024]{1,0:T(8,128)(2,1)}, bf16[1024,1024]{1,0:T(8,128)(2,1)}, u32[]{:S(2)}, u32[]{:S(2)}) %collective-permute-start.60) | collective-permute-done | bytes 2097184 | tf_op jit(solution)/shard_map/ppermute | solution.py:426
  2123.2 44.4 %collective-permute-done.58.refs_1_ = bf16[1024,1024]{1,0:T(8,128)(2,1)} collective-permute-done((bf16[1024,1024]{1,0:T(8,128)(2,1)}, bf16[1024,1024]{1,0:T(8,128)(2,1)}, u32[]{:S(2)}, u32[]{:S(2)}) %collective-permute-start.58) | collective-permute-done | bytes 2097184 | tf_op jit(solution)/shard_map/ppermute | solution.py:426
  2168.1 33.8 %shard_map.95 = (bf16[2048,4096]{1,0:T(8,128)(2,1)}, f32[2048,4096]{1,0:T(8,128)}, bf16[1024,2048]{1,0:T(8,128)(2,1)}) custom-call(bf16[2048,1024]{1,0:T(8,128)(2,1)} %shard_map.94.h_ref.refs_7_, bf16[1024,4096]{1,0:T(8,128)(2,1)} %get-tuple-element.223.w1_ref.refs_5_), custom_call_target="tpu_custom_call" | custom-call | flops 17179869184 | bytes 58720256 | tf_op jit(solution)/shard_map/pallas_call | solution.py:83
  2201.9 25.5 shard_map.96
  2229.0 28.5 %collective-permute-done.52.refs_2_ = bf16[256,4096]{1,0:T(8,128)(2,1)} collective-permute-done((bf16[256,4096]{1,0:T(8,128)(2,1)}, bf16[256,4096]{1,0:T(8,128)(2,1)}, u32[]{:S(2)}, u32[]{:S(2)}) %collective-permute-start.52) | collective-permute-done | bytes 2097184 | tf_op jit(solution)/shard_map/ppermute | solution.py:426
  2258.0 48.3 %shard_map.97 = (f32[1024,4096]{1,0:T(8,128)}, f32[4096,1024]{1,0:T(8,128)}, f32[2048,1024]{1,0:T(8,128)}) custom-call(bf16[2048,1024]{1,0:T(8,128)(2,1)} %get-tuple-element.226.refs_0_, bf16[1024,2048]{1,0:T(8,128)(2,1)} %get-tuple-element.227.refs_1_, bf16[2048,4096]{1,0:T(8,128)(2,1)} %get-tuple-element.224.act_ref.refs_2_, ...), custom_call_target="tpu_custom_call" | custom-call | flops 34359738368 | bytes 75497472 | tf_op jit(solution)/shard_map/pallas_call | solution.py:275
  2306.4 38.0 %collective-permute-done.48.refs_2_ = bf16[256,4096]{1,0:T(8,128)(2,1)} collective-permute-done((bf16[256,4096]{1,0:T(8,128)(2,1)}, bf16[256,4096]{1,0:T(8,128)(2,1)}, u32[]{:S(2)}, u32[]{:S(2)}) %collective-permute-start.48) | collective-permute-done | bytes 2097184 | tf_op jit(solution)/shard_map/ppermute | solution.py:426
  2344.9 54.4 %shard_map.98 = (f32[1024,4096]{1,0:T(8,128)}, f32[4096,1024]{1,0:T(8,128)}, bf16[2048,1024]{1,0:T(8,128)(2,1)}) custom-call(bf16[2048,1024]{1,0:T(8,128)(2,1)} %get-tuple-element.226.refs_0_, bf16[1024,2048]{1,0:T(8,128)(2,1)} %get-tuple-element.227.refs_1_, ...), custom_call_target="tpu_custom_call", output_to_operand_aliasing={{0}: (12, {}), {1}: (13, {})} | custom-call | flops 34359738368 | bytes 75497472 | tf_op jit(solution)/shard_map/pallas_call | solution.py:275
  2403.4 63.1 %shard_map.99 = (f32[1024,4096]{1,0:T(8,128)}, f32[4096,1024]{1,0:T(8,128)}) custom-call(bf16[2048,1024]{1,0:T(8,128)(2,1)} %get-tuple-element.240.refs_0_, bf16[1024,2048]{1,0:T(8,128)(2,1)} %get-tuple-element.241.refs_1_, bf16[2048,4096]{1,0:T(8,128)(2,1)} %get-tuple-element.221.act_ref.refs_2_, f32[2048,4096]{1,0:T(8,128)} %get-tuple-element.242.refs_3_, ...), custom_call_target="tpu_custom_call" | custom-call | flops 51539607552 | bytes 150994944 | tf_op jit(solution)/shard_map/pallas_call | solution.py:275
  2526.1 14.5 shard_map.100.refs_4_
  (131 shorter events, 248.1 us)
Async XLA Ops:
  14.6 215.8 %collective-permute-start.23 = (bf16[1024,1024]{1,0:T(8,128)(2,1)}, bf16[1024,1024]{1,0:T(8,128)(2,1)}, u32[]{:S(2)}, u32[]{:S(2)}) collective-permute-start(bf16[1024,1024]{1,0:T(8,128)(2,1)} %get-tuple-element.191), channel_id=1, source_target_pairs={{0,2},{2,0},{4,6},{6,4},{1,3},{3,1},{5,7},{7,5}} | collective-permute-start | bytes 6291464 | tf_op jit(solution)/shard_map/ppermute | solution.py:425
  17.9 212.5 %collective-permute-start.24 = (bf16[1024,1024]{1,0:T(8,128)(2,1)}, bf16[1024,1024]{1,0:T(8,128)(2,1)}, u32[]{:S(2)}, u32[]{:S(2)}) collective-permute-start(bf16[1024,1024]{1,0:T(8,128)(2,1)} %get-tuple-element.192), channel_id=1, source_target_pairs={{0,2},{2,0},{4,6},{6,4},{1,3},{3,1},{5,7},{7,5}} | collective-permute-start | bytes 6291464 | tf_op jit(solution)/shard_map/ppermute | solution.py:425
  18.0 269.3 %collective-permute-start.19 = (bf16[1024,1024]{1,0:T(8,128)(2,1)}, bf16[1024,1024]{1,0:T(8,128)(2,1)}, u32[]{:S(2)}, u32[]{:S(2)}) collective-permute-start(bf16[1024,1024]{1,0:T(8,128)(2,1)} %get-tuple-element.189), channel_id=1, source_target_pairs={{0,2},{2,0},{4,6},{6,4},{1,3},{3,1},{5,7},{7,5}} | collective-permute-start | bytes 6291464 | tf_op jit(solution)/shard_map/ppermute | solution.py:425
  20.0 267.3 %collective-permute-start.20 = (bf16[1024,1024]{1,0:T(8,128)(2,1)}, bf16[1024,1024]{1,0:T(8,128)(2,1)}, u32[]{:S(2)}, u32[]{:S(2)}) collective-permute-start(bf16[1024,1024]{1,0:T(8,128)(2,1)} %get-tuple-element.190), channel_id=1, source_target_pairs={{0,2},{2,0},{4,6},{6,4},{1,3},{3,1},{5,7},{7,5}} | collective-permute-start | bytes 6291464 | tf_op jit(solution)/shard_map/ppermute | solution.py:425
  34.0 255.3 %collective-permute-start.32 = (bf16[1024,1024]{1,0:T(8,128)(2,1)}, bf16[1024,1024]{1,0:T(8,128)(2,1)}, u32[]{:S(2)}, u32[]{:S(2)}) collective-permute-start(bf16[1024,1024]{1,0:T(8,128)(2,1)} %get-tuple-element.201), channel_id=1, source_target_pairs={{0,2},{2,0},{4,6},{6,4},{1,3},{3,1},{5,7},{7,5}} | collective-permute-start | bytes 6291464 | tf_op jit(solution)/shard_map/ppermute | solution.py:425
  230.4 103.9 %collective-permute-start.28 = (bf16[1024,1024]{1,0:T(8,128)(2,1)}, bf16[1024,1024]{1,0:T(8,128)(2,1)}, u32[]{:S(2)}, u32[]{:S(2)}) collective-permute-start(bf16[1024,1024]{1,0:T(8,128)(2,1)} %get-tuple-element.199), channel_id=1, source_target_pairs={{0,2},{2,0},{4,6},{6,4},{1,3},{3,1},{5,7},{7,5}} | collective-permute-start | bytes 6291464 | tf_op jit(solution)/shard_map/ppermute | solution.py:425
  287.2 112.5 %collective-permute-start.29 = (bf16[1024,1024]{1,0:T(8,128)(2,1)}, bf16[1024,1024]{1,0:T(8,128)(2,1)}, u32[]{:S(2)}, u32[]{:S(2)}) collective-permute-start(bf16[1024,1024]{1,0:T(8,128)(2,1)} %get-tuple-element.200), channel_id=1, source_target_pairs={{0,2},{2,0},{4,6},{6,4},{1,3},{3,1},{5,7},{7,5}} | collective-permute-start | bytes 6291464 | tf_op jit(solution)/shard_map/ppermute | solution.py:425
  287.3 137.0 %collective-permute-start.15 = (bf16[256,4096]{1,0:T(8,128)(2,1)}, bf16[256,4096]{1,0:T(8,128)(2,1)}, u32[]{:S(2)}, u32[]{:S(2)}) collective-permute-start(bf16[256,4096]{1,0:T(8,128)(2,1)} %get-tuple-element.179), channel_id=1, source_target_pairs={{0,2},{2,0},{4,6},{6,4},{1,3},{3,1},{5,7},{7,5}} | collective-permute-start | bytes 6291464 | tf_op jit(solution)/shard_map/ppermute | solution.py:425
  289.3 179.9 %collective-permute-start.14 = (bf16[256,4096]{1,0:T(8,128)(2,1)}, bf16[256,4096]{1,0:T(8,128)(2,1)}, u32[]{:S(2)}, u32[]{:S(2)}) collective-permute-start(bf16[256,4096]{1,0:T(8,128)(2,1)} %get-tuple-element.178), channel_id=1, source_target_pairs={{0,2},{2,0},{4,6},{6,4},{1,3},{3,1},{5,7},{7,5}} | collective-permute-start | bytes 6291464 | tf_op jit(solution)/shard_map/ppermute | solution.py:425
  289.4 224.7 %collective-permute-start.10 = (bf16[256,4096]{1,0:T(8,128)(2,1)}, bf16[256,4096]{1,0:T(8,128)(2,1)}, u32[]{:S(2)}, u32[]{:S(2)}) collective-permute-start(bf16[256,4096]{1,0:T(8,128)(2,1)} %get-tuple-element.176), channel_id=1, source_target_pairs={{0,2},{2,0},{4,6},{6,4},{1,3},{3,1},{5,7},{7,5}} | collective-permute-start | bytes 6291464 | tf_op jit(solution)/shard_map/ppermute | solution.py:425
  334.4 224.7 %collective-permute-start.11 = (bf16[256,4096]{1,0:T(8,128)(2,1)}, bf16[256,4096]{1,0:T(8,128)(2,1)}, u32[]{:S(2)}, u32[]{:S(2)}) collective-permute-start(bf16[256,4096]{1,0:T(8,128)(2,1)} %get-tuple-element.177), channel_id=1, source_target_pairs={{0,2},{2,0},{4,6},{6,4},{1,3},{3,1},{5,7},{7,5}} | collective-permute-start | bytes 6291464 | tf_op jit(solution)/shard_map/ppermute | solution.py:425
  399.8 220.1 %collective-permute-start.5 = (bf16[256,4096]{1,0:T(8,128)(2,1)}, bf16[256,4096]{1,0:T(8,128)(2,1)}, u32[]{:S(2)}, u32[]{:S(2)}) collective-permute-start(bf16[256,4096]{1,0:T(8,128)(2,1)} %get-tuple-element.168), channel_id=1, source_target_pairs={{0,2},{2,0},{4,6},{6,4},{1,3},{3,1},{5,7},{7,5}} | collective-permute-start | bytes 6291464 | tf_op jit(solution)/shard_map/ppermute | solution.py:425
  424.3 224.7 %collective-permute-start.6 = (bf16[256,4096]{1,0:T(8,128)(2,1)}, bf16[256,4096]{1,0:T(8,128)(2,1)}, u32[]{:S(2)}, u32[]{:S(2)}) collective-permute-start(bf16[256,4096]{1,0:T(8,128)(2,1)} %get-tuple-element.169), channel_id=1, source_target_pairs={{0,2},{2,0},{4,6},{6,4},{1,3},{3,1},{5,7},{7,5}} | collective-permute-start | bytes 6291464 | tf_op jit(solution)/shard_map/ppermute | solution.py:425
  469.2 224.7 %collective-permute-start.1 = (bf16[256,4096]{1,0:T(8,128)(2,1)}, bf16[256,4096]{1,0:T(8,128)(2,1)}, u32[]{:S(2)}, u32[]{:S(2)}) collective-permute-start(bf16[256,4096]{1,0:T(8,128)(2,1)} %get-tuple-element.166), channel_id=1, source_target_pairs={{0,2},{2,0},{4,6},{6,4},{1,3},{3,1},{5,7},{7,5}} | collective-permute-start | bytes 6291464 | tf_op jit(solution)/shard_map/ppermute | solution.py:425
  514.1 223.9 %collective-permute-start.2 = (bf16[256,4096]{1,0:T(8,128)(2,1)}, bf16[256,4096]{1,0:T(8,128)(2,1)}, u32[]{:S(2)}, u32[]{:S(2)}) collective-permute-start(bf16[256,4096]{1,0:T(8,128)(2,1)} %get-tuple-element.167), channel_id=1, source_target_pairs={{0,2},{2,0},{4,6},{6,4},{1,3},{3,1},{5,7},{7,5}} | collective-permute-start | bytes 6291464 | tf_op jit(solution)/shard_map/ppermute | solution.py:425
  559.1 180.7 %collective-permute-start.25 = (bf16[1024,1024]{1,0:T(8,128)(2,1)}, bf16[1024,1024]{1,0:T(8,128)(2,1)}, u32[]{:S(2)}, u32[]{:S(2)}) collective-permute-start(bf16[1024,1024]{1,0:T(8,128)(2,1)} %collective-permute-done.23.refs_0_), channel_id=1, source_target_pairs={{0,4},{2,6},{4,0},{6,2},{1,5},{3,7},{5,1},{7,3}} | collective-permute-start | bytes 6291464 | tf_op jit(solution)/shard_map/ppermute | solution.py:426
  619.8 436.4 %collective-permute-start.9 = (bf16[1024,4096]{1,0:T(8,128)(2,1)}, bf16[1024,4096]{1,0:T(8,128)(2,1)}, u32[]{:S(2)}, u32[]{:S(2)}) collective-permute-start(bf16[1024,4096]{1,0:T(8,128)(2,1)} %get-tuple-element.132.w1_ref), channel_id=1, source_target_pairs={{0,1},{1,0},{2,3},{3,2},{4,5},{5,4},{6,7},{7,6}} | collective-permute-start | bytes 25165832 | tf_op jit(solution)/shard_map/ppermute | solution.py:430
  649.0 150.5 %collective-permute-start.26 = (bf16[1024,1024]{1,0:T(8,128)(2,1)}, bf16[1024,1024]{1,0:T(8,128)(2,1)}, u32[]{:S(2)}, u32[]{:S(2)}) collective-permute-start(bf16[1024,1024]{1,0:T(8,128)(2,1)} %collective-permute-done.24.refs_1_), channel_id=1, source_target_pairs={{0,4},{2,6},{4,0},{6,2},{1,5},{3,7},{5,1},{7,3}} | collective-permute-start | bytes 6291464 | tf_op jit(solution)/shard_map/ppermute | solution.py:426
  693.9 105.5 %collective-permute-start.21 = (bf16[1024,1024]{1,0:T(8,128)(2,1)}, bf16[1024,1024]{1,0:T(8,128)(2,1)}, u32[]{:S(2)}, u32[]{:S(2)}) collective-permute-start(bf16[1024,1024]{1,0:T(8,128)(2,1)} %collective-permute-done.19.refs_0_), channel_id=1, source_target_pairs={{0,4},{2,6},{4,0},{6,2},{1,5},{3,7},{5,1},{7,3}} | collective-permute-start | bytes 6291464 | tf_op jit(solution)/shard_map/ppermute | solution.py:426
  739.8 92.0 %collective-permute-start.17 = (bf16[256,4096]{1,0:T(8,128)(2,1)}, bf16[256,4096]{1,0:T(8,128)(2,1)}, u32[]{:S(2)}, u32[]{:S(2)}) collective-permute-start(bf16[256,4096]{1,0:T(8,128)(2,1)} %collective-permute-done.15.refs_1_), channel_id=1, source_target_pairs={{0,4},{2,6},{4,0},{6,2},{1,5},{3,7},{5,1},{7,3}} | collective-permute-start | bytes 6291464 | tf_op jit(solution)/shard_map/ppermute | solution.py:426
  799.4 356.7 %collective-permute-start.18 = (bf16[4096,1024]{1,0:T(8,128)(2,1)}, bf16[4096,1024]{1,0:T(8,128)(2,1)}, u32[]{:S(2)}, u32[]{:S(2)}) collective-permute-start(bf16[4096,1024]{1,0:T(8,128)(2,1)} %get-tuple-element.134.w2_ref.refs_4_), channel_id=1, source_target_pairs={{0,1},{1,0},{2,3},{3,2},{4,5},{5,4},{6,7},{7,6}} | collective-permute-start | bytes 25165832 | tf_op jit(solution)/shard_map/ppermute | solution.py:430
  801.2 120.5 %collective-permute-start.12 = (bf16[256,4096]{1,0:T(8,128)(2,1)}, bf16[256,4096]{1,0:T(8,128)(2,1)}, u32[]{:S(2)}, u32[]{:S(2)}) collective-permute-start(bf16[256,4096]{1,0:T(8,128)(2,1)} %collective-permute-done.10.refs_0_), channel_id=1, source_target_pairs={{0,4},{2,6},{4,0},{6,2},{1,5},{3,7},{5,1},{7,3}} | collective-permute-start | bytes 6291464 | tf_op jit(solution)/shard_map/ppermute | solution.py:426
  831.8 134.8 %collective-permute-start.13 = (bf16[256,4096]{1,0:T(8,128)(2,1)}, bf16[256,4096]{1,0:T(8,128)(2,1)}, u32[]{:S(2)}, u32[]{:S(2)}) collective-permute-start(bf16[256,4096]{1,0:T(8,128)(2,1)} %collective-permute-done.11.refs_1_), channel_id=1, source_target_pairs={{0,4},{2,6},{4,0},{6,2},{1,5},{3,7},{5,1},{7,3}} | collective-permute-start | bytes 6291464 | tf_op jit(solution)/shard_map/ppermute | solution.py:426
  882.1 344.5 %collective-permute-start = (bf16[1024,4096]{1,0:T(8,128)(2,1)}, bf16[1024,4096]{1,0:T(8,128)(2,1)}, u32[]{:S(2)}, u32[]{:S(2)}) collective-permute-start(bf16[1024,4096]{1,0:T(8,128)(2,1)} %get-tuple-element.135.w1_ref.refs_5_), channel_id=1, source_target_pairs={{0,1},{1,0},{2,3},{3,2},{4,5},{5,4},{6,7},{7,6}} | collective-permute-start | bytes 25165832 | tf_op jit(solution)/shard_map/ppermute | solution.py:430
  921.6 101.0 %collective-permute-start.7 = (bf16[256,4096]{1,0:T(8,128)(2,1)}, bf16[256,4096]{1,0:T(8,128)(2,1)}, u32[]{:S(2)}, u32[]{:S(2)}) collective-permute-start(bf16[256,4096]{1,0:T(8,128)(2,1)} %collective-permute-done.5.refs_0_), channel_id=1, source_target_pairs={{0,4},{2,6},{4,0},{6,2},{1,5},{3,7},{5,1},{7,3}} | collective-permute-start | bytes 6291464 | tf_op jit(solution)/shard_map/ppermute | solution.py:426
  1022.7 265.4 %collective-permute-start.27 = (bf16[4096,1024]{1,0:T(8,128)(2,1)}, bf16[4096,1024]{1,0:T(8,128)(2,1)}, u32[]{:S(2)}, u32[]{:S(2)}) collective-permute-start(bf16[4096,1024]{1,0:T(8,128)(2,1)} %get-tuple-element.137.w2_ref.refs_4_), channel_id=1, source_target_pairs={{0,1},{1,0},{2,3},{3,2},{4,5},{5,4},{6,7},{7,6}} | collective-permute-start | bytes 25165832 | tf_op jit(solution)/shard_map/ppermute | solution.py:430
  1054.8 99.8 %collective-permute-start.3 = (bf16[256,4096]{1,0:T(8,128)(2,1)}, bf16[256,4096]{1,0:T(8,128)(2,1)}, u32[]{:S(2)}, u32[]{:S(2)}) collective-permute-start(bf16[256,4096]{1,0:T(8,128)(2,1)} %collective-permute-done.1.refs_0_), channel_id=1, source_target_pairs={{0,4},{2,6},{4,0},{6,2},{1,5},{3,7},{5,1},{7,3}} | collective-permute-start | bytes 6291464 | tf_op jit(solution)/shard_map/ppermute | solution.py:426
  1056.3 168.9 %collective-permute-start.4 = (bf16[256,4096]{1,0:T(8,128)(2,1)}, bf16[256,4096]{1,0:T(8,128)(2,1)}, u32[]{:S(2)}, u32[]{:S(2)}) collective-permute-start(bf16[256,4096]{1,0:T(8,128)(2,1)} %collective-permute-done.2.refs_1_), channel_id=1, source_target_pairs={{0,4},{2,6},{4,0},{6,2},{1,5},{3,7},{5,1},{7,3}} | collective-permute-start | bytes 6291464 | tf_op jit(solution)/shard_map/ppermute | solution.py:426
  1154.6 131.3 %collective-permute-start.34 = (bf16[1024,1024]{1,0:T(8,128)(2,1)}, bf16[1024,1024]{1,0:T(8,128)(2,1)}, u32[]{:S(2)}, u32[]{:S(2)}) collective-permute-start(bf16[1024,1024]{1,0:T(8,128)(2,1)} %collective-permute-done.32.refs_0_), channel_id=1, source_target_pairs={{0,4},{2,6},{4,0},{6,2},{1,5},{3,7},{5,1},{7,3}} | collective-permute-start | bytes 6291464 | tf_op jit(solution)/shard_map/ppermute | solution.py:426
  1156.1 131.3 %collective-permute-start.35 = (bf16[1024,1024]{1,0:T(8,128)(2,1)}, bf16[1024,1024]{1,0:T(8,128)(2,1)}, u32[]{:S(2)}, u32[]{:S(2)}) collective-permute-start(bf16[1024,1024]{1,0:T(8,128)(2,1)} %collective-permute-done.33.refs_1_), channel_id=1, source_target_pairs={{0,4},{2,6},{4,0},{6,2},{1,5},{3,7},{5,1},{7,3}} | collective-permute-start | bytes 6291464 | tf_op jit(solution)/shard_map/ppermute | solution.py:426
  1225.1 115.4 %collective-permute-start.30 = (bf16[1024,1024]{1,0:T(8,128)(2,1)}, bf16[1024,1024]{1,0:T(8,128)(2,1)}, u32[]{:S(2)}, u32[]{:S(2)}) collective-permute-start(bf16[1024,1024]{1,0:T(8,128)(2,1)} %collective-permute-done.28.refs_0_), channel_id=1, source_target_pairs={{0,4},{2,6},{4,0},{6,2},{1,5},{3,7},{5,1},{7,3}} | collective-permute-start | bytes 6291464 | tf_op jit(solution)/shard_map/ppermute | solution.py:426
  1226.6 114.6 %collective-permute-start.31 = (bf16[1024,1024]{1,0:T(8,128)(2,1)}, bf16[1024,1024]{1,0:T(8,128)(2,1)}, u32[]{:S(2)}, u32[]{:S(2)}) collective-permute-start(bf16[1024,1024]{1,0:T(8,128)(2,1)} %collective-permute-done.29.refs_1_), channel_id=1, source_target_pairs={{0,4},{2,6},{4,0},{6,2},{1,5},{3,7},{5,1},{7,3}} | collective-permute-start | bytes 6291464 | tf_op jit(solution)/shard_map/ppermute | solution.py:426
  1286.0 99.2 %collective-permute-start.68 = (bf16[1024,1024]{1,0:T(8,128)(2,1)}, bf16[1024,1024]{1,0:T(8,128)(2,1)}, u32[]{:S(2)}, u32[]{:S(2)}) collective-permute-start(bf16[1024,1024]{1,0:T(8,128)(2,1)} %get-tuple-element.258), channel_id=1, source_target_pairs={{0,2},{2,0},{4,6},{6,4},{1,3},{3,1},{5,7},{7,5}} | collective-permute-start | bytes 6291464 | tf_op jit(solution)/shard_map/ppermute | solution.py:425
  1287.4 98.4 %collective-permute-start.69 = (bf16[1024,1024]{1,0:T(8,128)(2,1)}, bf16[1024,1024]{1,0:T(8,128)(2,1)}, u32[]{:S(2)}, u32[]{:S(2)}) collective-permute-start(bf16[1024,1024]{1,0:T(8,128)(2,1)} %get-tuple-element.259), channel_id=1, source_target_pairs={{0,2},{2,0},{4,6},{6,4},{1,3},{3,1},{5,7},{7,5}} | collective-permute-start | bytes 6291464 | tf_op jit(solution)/shard_map/ppermute | solution.py:425
  1288.0 136.7 %collective-permute-start.64 = (bf16[1024,1024]{1,0:T(8,128)(2,1)}, bf16[1024,1024]{1,0:T(8,128)(2,1)}, u32[]{:S(2)}, u32[]{:S(2)}) collective-permute-start(bf16[1024,1024]{1,0:T(8,128)(2,1)} %get-tuple-element.256), channel_id=1, source_target_pairs={{0,2},{2,0},{4,6},{6,4},{1,3},{3,1},{5,7},{7,5}} | collective-permute-start | bytes 6291464 | tf_op jit(solution)/shard_map/ppermute | solution.py:425
  1340.6 134.4 %collective-permute-start.65 = (bf16[1024,1024]{1,0:T(8,128)(2,1)}, bf16[1024,1024]{1,0:T(8,128)(2,1)}, u32[]{:S(2)}, u32[]{:S(2)}) collective-permute-start(bf16[1024,1024]{1,0:T(8,128)(2,1)} %get-tuple-element.257), channel_id=1, source_target_pairs={{0,2},{2,0},{4,6},{6,4},{1,3},{3,1},{5,7},{7,5}} | collective-permute-start | bytes 6291464 | tf_op jit(solution)/shard_map/ppermute | solution.py:425
  1341.2 173.4 %collective-permute-start.61 = (bf16[1024,1024]{1,0:T(8,128)(2,1)}, bf16[1024,1024]{1,0:T(8,128)(2,1)}, u32[]{:S(2)}, u32[]{:S(2)}) collective-permute-start(bf16[1024,1024]{1,0:T(8,128)(2,1)} %get-tuple-element.254), channel_id=1, source_target_pairs={{0,2},{2,0},{4,6},{6,4},{1,3},{3,1},{5,7},{7,5}} | collective-permute-start | bytes 6291464 | tf_op jit(solution)/shard_map/ppermute | solution.py:425
  1385.2 174.3 %collective-permute-start.59 = (bf16[1024,1024]{1,0:T(8,128)(2,1)}, bf16[1024,1024]{1,0:T(8,128)(2,1)}, u32[]{:S(2)}, u32[]{:S(2)}) collective-permute-start(bf16[1024,1024]{1,0:T(8,128)(2,1)} %get-tuple-element.253), channel_id=1, source_target_pairs={{0,2},{2,0},{4,6},{6,4},{1,3},{3,1},{5,7},{7,5}} | collective-permute-start | bytes 6291464 | tf_op jit(solution)/shard_map/ppermute | solution.py:425
  1385.8 218.6 %collective-permute-start.57 = (bf16[1024,1024]{1,0:T(8,128)(2,1)}, bf16[1024,1024]{1,0:T(8,128)(2,1)}, u32[]{:S(2)}, u32[]{:S(2)}) collective-permute-start(bf16[1024,1024]{1,0:T(8,128)(2,1)} %get-tuple-element.252), channel_id=1, source_target_pairs={{0,2},{2,0},{4,6},{6,4},{1,3},{3,1},{5,7},{7,5}} | collective-permute-start | bytes 6291464 | tf_op jit(solution)/shard_map/ppermute | solution.py:425
  1424.7 224.7 %collective-permute-start.55 = (bf16[1024,1024]{1,0:T(8,128)(2,1)}, bf16[1024,1024]{1,0:T(8,128)(2,1)}, u32[]{:S(2)}, u32[]{:S(2)}) collective-permute-start(bf16[1024,1024]{1,0:T(8,128)(2,1)} %get-tuple-element.251), channel_id=1, source_target_pairs={{0,2},{2,0},{4,6},{6,4},{1,3},{3,1},{5,7},{7,5}} | collective-permute-start | bytes 6291464 | tf_op jit(solution)/shard_map/ppermute | solution.py:425
  1475.0 231.1 %collective-permute-start.50 = (bf16[256,4096]{1,0:T(8,128)(2,1)}, bf16[256,4096]{1,0:T(8,128)(2,1)}, u32[]{:S(2)}, u32[]{:S(2)}) collective-permute-start(bf16[256,4096]{1,0:T(8,128)(2,1)} %get-tuple-element.248), channel_id=1, source_target_pairs={{0,2},{2,0},{4,6},{6,4},{1,3},{3,1},{5,7},{7,5}} | collective-permute-start | bytes 6291464 | tf_op jit(solution)/shard_map/ppermute | solution.py:425
  1514.6 224.7 %collective-permute-start.51 = (bf16[256,4096]{1,0:T(8,128)(2,1)}, bf16[256,4096]{1,0:T(8,128)(2,1)}, u32[]{:S(2)}, u32[]{:S(2)}) collective-permute-start(bf16[256,4096]{1,0:T(8,128)(2,1)} %get-tuple-element.249), channel_id=1, source_target_pairs={{0,2},{2,0},{4,6},{6,4},{1,3},{3,1},{5,7},{7,5}} | collective-permute-start | bytes 6291464 | tf_op jit(solution)/shard_map/ppermute | solution.py:425
  1559.5 224.7 %collective-permute-start.46 = (bf16[256,4096]{1,0:T(8,128)(2,1)}, bf16[256,4096]{1,0:T(8,128)(2,1)}, u32[]{:S(2)}, u32[]{:S(2)}) collective-permute-start(bf16[256,4096]{1,0:T(8,128)(2,1)} %get-tuple-element.246), channel_id=1, source_target_pairs={{0,2},{2,0},{4,6},{6,4},{1,3},{3,1},{5,7},{7,5}} | collective-permute-start | bytes 6291464 | tf_op jit(solution)/shard_map/ppermute | solution.py:425
  1604.4 224.7 %collective-permute-start.47 = (bf16[256,4096]{1,0:T(8,128)(2,1)}, bf16[256,4096]{1,0:T(8,128)(2,1)}, u32[]{:S(2)}, u32[]{:S(2)}) collective-permute-start(bf16[256,4096]{1,0:T(8,128)(2,1)} %get-tuple-element.247), channel_id=1, source_target_pairs={{0,2},{2,0},{4,6},{6,4},{1,3},{3,1},{5,7},{7,5}} | collective-permute-start | bytes 6291464 | tf_op jit(solution)/shard_map/ppermute | solution.py:425
  1649.4 224.7 %collective-permute-start.41 = (bf16[256,4096]{1,0:T(8,128)(2,1)}, bf16[256,4096]{1,0:T(8,128)(2,1)}, u32[]{:S(2)}, u32[]{:S(2)}) collective-permute-start(bf16[256,4096]{1,0:T(8,128)(2,1)} %get-tuple-element.238), channel_id=1, source_target_pairs={{0,2},{2,0},{4,6},{6,4},{1,3},{3,1},{5,7},{7,5}} | collective-permute-start | bytes 6291464 | tf_op jit(solution)/shard_map/ppermute | solution.py:425
  1706.0 233.0 %collective-permute-start.42 = (bf16[256,4096]{1,0:T(8,128)(2,1)}, bf16[256,4096]{1,0:T(8,128)(2,1)}, u32[]{:S(2)}, u32[]{:S(2)}) collective-permute-start(bf16[256,4096]{1,0:T(8,128)(2,1)} %get-tuple-element.239), channel_id=1, source_target_pairs={{0,2},{2,0},{4,6},{6,4},{1,3},{3,1},{5,7},{7,5}} | collective-permute-start | bytes 6291464 | tf_op jit(solution)/shard_map/ppermute | solution.py:425
  1739.3 224.7 %collective-permute-start.37 = (bf16[256,4096]{1,0:T(8,128)(2,1)}, bf16[256,4096]{1,0:T(8,128)(2,1)}, u32[]{:S(2)}, u32[]{:S(2)}) collective-permute-start(bf16[256,4096]{1,0:T(8,128)(2,1)} %get-tuple-element.236), channel_id=1, source_target_pairs={{0,2},{2,0},{4,6},{6,4},{1,3},{3,1},{5,7},{7,5}} | collective-permute-start | bytes 6291464 | tf_op jit(solution)/shard_map/ppermute | solution.py:425
  1784.2 220.5 %collective-permute-start.38 = (bf16[256,4096]{1,0:T(8,128)(2,1)}, bf16[256,4096]{1,0:T(8,128)(2,1)}, u32[]{:S(2)}, u32[]{:S(2)}) collective-permute-start(bf16[256,4096]{1,0:T(8,128)(2,1)} %get-tuple-element.237), channel_id=1, source_target_pairs={{0,2},{2,0},{4,6},{6,4},{1,3},{3,1},{5,7},{7,5}} | collective-permute-start | bytes 6291464 | tf_op jit(solution)/shard_map/ppermute | solution.py:425
  1829.2 176.7 %collective-permute-start.70 = (bf16[1024,1024]{1,0:T(8,128)(2,1)}, bf16[1024,1024]{1,0:T(8,128)(2,1)}, u32[]{:S(2)}, u32[]{:S(2)}) collective-permute-start(bf16[1024,1024]{1,0:T(8,128)(2,1)} %collective-permute-done.68.refs_0_), channel_id=1, source_target_pairs={{0,4},{2,6},{4,0},{6,2},{1,5},{3,7},{5,1},{7,3}} | collective-permute-start | bytes 6291464 | tf_op jit(solution)/shard_map/ppermute | solution.py:426
  1874.1 132.6 %collective-permute-start.71 = (bf16[1024,1024]{1,0:T(8,128)(2,1)}, bf16[1024,1024]{1,0:T(8,128)(2,1)}, u32[]{:S(2)}, u32[]{:S(2)}) collective-permute-start(bf16[1024,1024]{1,0:T(8,128)(2,1)} %collective-permute-done.69.refs_1_), channel_id=1, source_target_pairs={{0,4},{2,6},{4,0},{6,2},{1,5},{3,7},{5,1},{7,3}} | collective-permute-start | bytes 6291464 | tf_op jit(solution)/shard_map/ppermute | solution.py:426
  1939.0 127.8 %collective-permute-start.66 = (bf16[1024,1024]{1,0:T(8,128)(2,1)}, bf16[1024,1024]{1,0:T(8,128)(2,1)}, u32[]{:S(2)}, u32[]{:S(2)}) collective-permute-start(bf16[1024,1024]{1,0:T(8,128)(2,1)} %collective-permute-done.64.refs_0_), channel_id=1, source_target_pairs={{0,4},{2,6},{4,0},{6,2},{1,5},{3,7},{5,1},{7,3}} | collective-permute-start | bytes 6291464 | tf_op jit(solution)/shard_map/ppermute | solution.py:426
  1964.0 102.9 %collective-permute-start.67 = (bf16[1024,1024]{1,0:T(8,128)(2,1)}, bf16[1024,1024]{1,0:T(8,128)(2,1)}, u32[]{:S(2)}, u32[]{:S(2)}) collective-permute-start(bf16[1024,1024]{1,0:T(8,128)(2,1)} %collective-permute-done.65.refs_1_), channel_id=1, source_target_pairs={{0,4},{2,6},{4,0},{6,2},{1,5},{3,7},{5,1},{7,3}} | collective-permute-start | bytes 6291464 | tf_op jit(solution)/shard_map/ppermute | solution.py:426
  2005.9 116.8 %collective-permute-start.60 = (bf16[1024,1024]{1,0:T(8,128)(2,1)}, bf16[1024,1024]{1,0:T(8,128)(2,1)}, u32[]{:S(2)}, u32[]{:S(2)}) collective-permute-start(bf16[1024,1024]{1,0:T(8,128)(2,1)} %collective-permute-done.59.refs_0_), channel_id=1, source_target_pairs={{0,4},{2,6},{4,0},{6,2},{1,5},{3,7},{5,1},{7,3}} | collective-permute-start | bytes 6291464 | tf_op jit(solution)/shard_map/ppermute | solution.py:426
  2006.7 160.9 %collective-permute-start.58 = (bf16[1024,1024]{1,0:T(8,128)(2,1)}, bf16[1024,1024]{1,0:T(8,128)(2,1)}, u32[]{:S(2)}, u32[]{:S(2)}) collective-permute-start(bf16[1024,1024]{1,0:T(8,128)(2,1)} %collective-permute-done.57.refs_0_), channel_id=1, source_target_pairs={{0,4},{2,6},{4,0},{6,2},{1,5},{3,7},{5,1},{7,3}} | collective-permute-start | bytes 6291464 | tf_op jit(solution)/shard_map/ppermute | solution.py:426
  2066.9 334.0 %collective-permute-start.63 = (bf16[4096,1024]{1,0:T(8,128)(2,1)}, bf16[4096,1024]{1,0:T(8,128)(2,1)}, u32[]{:S(2)}, u32[]{:S(2)}) collective-permute-start(bf16[4096,1024]{1,0:T(8,128)(2,1)} %get-tuple-element.195.w2_ref.refs_4_), channel_id=1, source_target_pairs={{0,1},{1,0},{2,3},{3,2},{4,5},{5,4},{6,7},{7,6}} | collective-permute-start | bytes 25165832 | tf_op jit(solution)/shard_map/ppermute | solution.py:430
  2066.9 334.5 %collective-permute-start.54 = (bf16[4096,1024]{1,0:T(8,128)(2,1)}, bf16[4096,1024]{1,0:T(8,128)(2,1)}, u32[]{:S(2)}, u32[]{:S(2)}) collective-permute-start(bf16[4096,1024]{1,0:T(8,128)(2,1)} %get-tuple-element.206.w2_ref.refs_4_), channel_id=1, source_target_pairs={{0,1},{1,0},{2,3},{3,2},{4,5},{5,4},{6,7},{7,6}} | collective-permute-start | bytes 25165832 | tf_op jit(solution)/shard_map/ppermute | solution.py:430
  2077.7 325.2 %collective-permute-start.45 = (bf16[1024,4096]{1,0:T(8,128)(2,1)}, bf16[1024,4096]{1,0:T(8,128)(2,1)}, u32[]{:S(2)}, u32[]{:S(2)}) collective-permute-start(bf16[1024,4096]{1,0:T(8,128)(2,1)} %get-tuple-element.186.w1_ref), channel_id=1, source_target_pairs={{0,1},{1,0},{2,3},{3,2},{4,5},{5,4},{6,7},{7,6}} | collective-permute-start | bytes 25165832 | tf_op jit(solution)/shard_map/ppermute | solution.py:430
  2122.7 104.8 %collective-permute-start.56 = (bf16[1024,1024]{1,0:T(8,128)(2,1)}, bf16[1024,1024]{1,0:T(8,128)(2,1)}, u32[]{:S(2)}, u32[]{:S(2)}) collective-permute-start(bf16[1024,1024]{1,0:T(8,128)(2,1)} %collective-permute-done.55.refs_0_), channel_id=1, source_target_pairs={{0,4},{2,6},{4,0},{6,2},{1,5},{3,7},{5,1},{7,3}} | collective-permute-start | bytes 6291464 | tf_op jit(solution)/shard_map/ppermute | solution.py:426
  2167.6 89.9 %collective-permute-start.52 = (bf16[256,4096]{1,0:T(8,128)(2,1)}, bf16[256,4096]{1,0:T(8,128)(2,1)}, u32[]{:S(2)}, u32[]{:S(2)}) collective-permute-start(bf16[256,4096]{1,0:T(8,128)(2,1)} %collective-permute-done.50.refs_0_), channel_id=1, source_target_pairs={{0,4},{2,6},{4,0},{6,2},{1,5},{3,7},{5,1},{7,3}} | collective-permute-start | bytes 6291464 | tf_op jit(solution)/shard_map/ppermute | solution.py:426
  2306.4 248.6 %collective-permute-start.36 = (bf16[1024,4096]{1,0:T(8,128)(2,1)}, bf16[1024,4096]{1,0:T(8,128)(2,1)}, u32[]{:S(2)}, u32[]{:S(2)}) collective-permute-start(bf16[1024,4096]{1,0:T(8,128)(2,1)} %get-tuple-element.196.w1_ref.refs_5_), channel_id=1, source_target_pairs={{0,1},{1,0},{2,3},{3,2},{4,5},{5,4},{6,7},{7,6}} | collective-permute-start | bytes 25165832 | tf_op jit(solution)/shard_map/ppermute | solution.py:430
  2399.3 155.6 %collective-permute-start.43 = (bf16[256,4096]{1,0:T(8,128)(2,1)}, bf16[256,4096]{1,0:T(8,128)(2,1)}, u32[]{:S(2)}, u32[]{:S(2)}) collective-permute-start(bf16[256,4096]{1,0:T(8,128)(2,1)} %collective-permute-done.41.refs_0_), channel_id=1, source_target_pairs={{0,4},{2,6},{4,0},{6,2},{1,5},{3,7},{5,1},{7,3}} | collective-permute-start | bytes 6291464 | tf_op jit(solution)/shard_map/ppermute | solution.py:426
  2400.9 154.1 %collective-permute-start.44 = (bf16[256,4096]{1,0:T(8,128)(2,1)}, bf16[256,4096]{1,0:T(8,128)(2,1)}, u32[]{:S(2)}, u32[]{:S(2)}) collective-permute-start(bf16[256,4096]{1,0:T(8,128)(2,1)} %collective-permute-done.42.refs_1_), channel_id=1, source_target_pairs={{0,4},{2,6},{4,0},{6,2},{1,5},{3,7},{5,1},{7,3}} | collective-permute-start | bytes 6291464 | tf_op jit(solution)/shard_map/ppermute | solution.py:426
  2401.4 167.9 %collective-permute-start.39 = (bf16[256,4096]{1,0:T(8,128)(2,1)}, bf16[256,4096]{1,0:T(8,128)(2,1)}, u32[]{:S(2)}, u32[]{:S(2)}) collective-permute-start(bf16[256,4096]{1,0:T(8,128)(2,1)} %collective-permute-done.37.refs_0_), channel_id=1, source_target_pairs={{0,4},{2,6},{4,0},{6,2},{1,5},{3,7},{5,1},{7,3}} | collective-permute-start | bytes 6291464 | tf_op jit(solution)/shard_map/ppermute | solution.py:426
  2402.9 166.4 %collective-permute-start.40 = (bf16[256,4096]{1,0:T(8,128)(2,1)}, bf16[256,4096]{1,0:T(8,128)(2,1)}, u32[]{:S(2)}, u32[]{:S(2)}) collective-permute-start(bf16[256,4096]{1,0:T(8,128)(2,1)} %collective-permute-done.38.refs_1_), channel_id=1, source_target_pairs={{0,4},{2,6},{4,0},{6,2},{1,5},{3,7},{5,1},{7,3}} | collective-permute-start | bytes 6291464 | tf_op jit(solution)/shard_map/ppermute | solution.py:426
  (8 other events, 586.8 us)

commit v4 on v3

--- a/solution.py
+++ b/solution.py
@@ -12,6 +12,7 @@
 EPS = 1e-6
 INV_SQRT2 = 0.7071067811865476
 INV_SQRT_2PI = 0.3989422804014327
+HALF_LOG2E = -0.7213475204444817
 F32 = jnp.float32
 BF16 = jnp.bfloat16
 CONTRACT_ROWS = (((0,), (0,)), ((), ()))
@@ -23,7 +24,7 @@
 FWD_BLOCK = 512
 BWD_BLOCK = 256
 HID_TILE = 256
-PARTS = (1, 2)
+SPLIT = ((0, 0), (0, 1), (1, 1))
 CHUNKS = 4
 ANY = pl.BlockSpec(memory_space=pl.ANY)
 
@@ -40,20 +41,31 @@
     lax.fori_loop(0, count, lambda i, c: (body(pl.ds(pl.multiple_of(i * SLAB, SLAB), SLAB)), c)[1], 0)
 
 
-def act_kernel(h_ref, w1_ref, act_ref, slope_ref, ut_hbm, u_s, ut_s, z_s, sem):
+def act_kernel(t, h_hbm, w1_ref, act_ref, slope_ref, ut_hbm, h_s, u_s, ut_s, z_s, sem, h_sems):
     step = pl.program_id(0)
-    rows_total = h_ref.shape[0]
+    rows_total = h_s.shape[0]
     ut_copy = pltpu.make_async_copy(ut_s, ut_hbm, sem)
+    h_rows = h_hbm if t is None else h_hbm.at[0, 0, t]
+
+    def load(i):
+        rows = pl.ds(pl.multiple_of(i * SLAB, SLAB), SLAB)
+        return pltpu.make_async_copy(h_rows.at[rows], h_s.at[rows], h_sems.at[i])
 
     @pl.when(step == 0)
     def _():
-        def normalize(rows):
-            h = h_ref[rows, :].astype(F32)
+        for i in range(rows_total // SLAB):
+            load(i).start()
+
+        def normalize(i, carry):
+            rows = pl.ds(pl.multiple_of(i * SLAB, SLAB), SLAB)
+            load(i).wait()
+            h = h_s[rows, :].astype(F32)
             u = h * inv_rms_of(h)
             u_s[rows, :] = u.astype(BF16)
             ut_s[:, rows] = u.T.astype(BF16)
-
-        slabs(rows_total // SLAB, normalize)
+            return carry
+
+        lax.fori_loop(0, rows_total // SLAB, normalize, 0)
         ut_copy.start()
 
     for i in range(rows_total // ACT_TILE):
@@ -61,7 +73,7 @@
         z = z_s[rows, :]
         half = 0.5 * (1.0 + lax.erf(z * INV_SQRT2))
         act_ref[rows, :] = (z * half).astype(BF16)
-        slope_ref[rows, :] = half + z * jnp.exp(-0.5 * z * z) * INV_SQRT_2PI
+        slope_ref[rows, :] = half + (z * INV_SQRT_2PI) * jnp.exp2(z * z * HALF_LOG2E)
         z_s[rows, :] = jnp.dot(u_s[rows, :], w1_ref[...], preferred_element_type=F32)
 
     @pl.when(step == pl.num_programs(0) - 1)
@@ -73,31 +85,45 @@
     depth, ff = w1.shape
     rows = h.shape[-2]
     block = FWD_BLOCK
-    once = pl.Buffered(1)
-    if t is None:
-        h_spec = pl.BlockSpec((rows, depth), lambda j: (0, 0), pipeline_mode=once)
-    else:
-        h_spec = pl.BlockSpec((None, None, None, rows, depth), lambda j: (0, 0, t, 0, 0), pipeline_mode=once)
     blocks = ff // block
     done_block = pl.BlockSpec((rows, block), lambda j: (0, jnp.maximum(j - 1, 0)))
     return pl.pallas_call(
-        act_kernel,
+        functools.partial(act_kernel, t),
         grid=(blocks + 1,),
-        in_specs=[h_spec, pl.BlockSpec((depth, block), lambda j: (0, jnp.minimum(j, blocks - 1)))],
+        in_specs=[ANY, pl.BlockSpec((depth, block), lambda j: (0, jnp.minimum(j, blocks - 1)))],
         out_specs=[done_block, done_block, ANY],
         out_shape=[jax.ShapeDtypeStruct((rows, ff), BF16), jax.ShapeDtypeStruct((rows, ff), F32),
                    jax.ShapeDtypeStruct((depth, rows), BF16)],
-        scratch_shapes=[pltpu.VMEM((rows, depth), BF16), pltpu.VMEM((depth, rows), BF16), pltpu.VMEM((rows, block), F32),
-                        pltpu.SemaphoreType.DMA],
+        scratch_shapes=[pltpu.VMEM((rows, depth), BF16), pltpu.VMEM((rows, depth), BF16), pltpu.VMEM((depth, rows), BF16),
+                        pltpu.VMEM((rows, block), F32), pltpu.SemaphoreType.DMA, pltpu.SemaphoreType.DMA((rows // SLAB,))],
         compiler_params=params_of(),
         cost_estimate=pl.CostEstimate(flops=2 * rows * depth * ff, bytes_accessed=rows * ff * 6 + depth * ff * 2,
                                       transcendentals=2 * rows * ff),
     )(h, w1)
 
 
-def hidden_kernel(last, scale, act_ref, w2_ref, h_ref, *refs):
-    add = jnp.dot(act_ref[...], w2_ref[...], preferred_element_type=F32)
-    h = (h_ref[...].astype(F32) + add).astype(BF16)
+def hidden_kernel(last, scale, act_ref, w2_hbm, h_ref, *refs):
+    *refs, w2_s, add_s, sems = refs
+    step = pl.program_id(0)
+    bands = 4
+    band = w2_s.shape[0] // bands
+
+    @pl.when(step == 0)
+    def _():
+        pieces = [pl.ds(i * band, band) for i in range(bands)]
+        loads = [pltpu.make_async_copy(w2_hbm.at[piece], w2_s.at[piece], sems.at[i]) for i, piece in enumerate(pieces)]
+        for load in loads:
+            load.start()
+        for i, (piece, load) in enumerate(zip(pieces, loads)):
+            load.wait()
+            add = jnp.dot(act_ref[:, piece], w2_s[piece, :], preferred_element_type=F32)
+            add_s[...] = add_s[...] + add if i else add
+
+    @pl.when(step > 0)
+    def _():
+        add_s[...] = jnp.dot(act_ref[...], w2_s[...], preferred_element_type=F32)
+
+    h = (h_ref[...].astype(F32) + add_s[...]).astype(BF16)
     if last:
         tgt_ref, hout_ref, g_ref = refs
         g_ref[...] = ((h.astype(F32) - tgt_ref[...].astype(F32)) * scale).astype(BF16)
@@ -118,17 +144,22 @@
         functools.partial(hidden_kernel, last, scale),
         grid=(rows // tile,),
         in_specs=[pl.BlockSpec((tile, ff), lambda i: (i, 0)),
-                  pl.BlockSpec((ff, depth), lambda i: (0, 0), pipeline_mode=pl.Buffered(1)),
+                  ANY,
                   plain if t is None else of_step(t)] + ([of_step(target_t)] if last else []),
         out_specs=[plain] * n_out,
         out_shape=[jax.ShapeDtypeStruct((rows, depth), BF16)] * n_out,
+        scratch_shapes=[pltpu.VMEM((ff, depth), BF16), pltpu.VMEM((tile, depth), F32), pltpu.SemaphoreType.DMA((4,))],
         compiler_params=params_of(),
         cost_estimate=pl.CostEstimate(flops=2 * rows * depth * ff, bytes_accessed=rows * ff * 2 + depth * ff * 2,
                                       transcendentals=0),
     )(act, w2, h, *([target] if last else []))
 
 
-def bwd_kernel(deep, second, part, scale, rate, t, n_prev, *refs):
+def parts_of(window, step, layer):
+    return 2 if layer or (window, step) in SPLIT else 1
+
+
+def bwd_kernel(deep, second, part, parts, scale, rate, t, n_prev, *refs):
     refs = list(refs)
 
     def take(count):
@@ -137,7 +168,7 @@
         return taken
 
     g_ref, ut_ref, act_ref, slope_ref, w2_ref = take(5)
-    closing = deep and part == PARTS[1] - 1
+    closing = deep and part == parts - 1
     if deep:
         w1_ref, = take(1)
     if deep and part:
@@ -174,10 +205,8 @@
         loads = [pltpu.make_async_copy(src, dst, sems.at[i + 1])
                  for i, (src, dst) in enumerate(((h_hbm, h_s), (hl_hbm, hl_s), (tgt_hbm.at[0, 0, t], tgt_s)))]
 
-        @pl.when(step == 0)
-        def _():
-            for load in loads:
-                load.start()
+        for i, load in enumerate(loads):
+            pl.when(step == i + 2)(load.start)
 
     for i in range(rows_total // TILE):
         rows = pl.ds(i * TILE, TILE)
@@ -220,11 +249,10 @@
             out_copy.wait()
 
 
-def backward(part, g, ut, act, slope, w1, w2, old1, old2, prev, second, rate, layer, deep, scale, t):
+def backward(part, parts, g, ut, act, slope, w1, w2, old1, old2, prev, second, rate, layer, deep, scale, t):
     rows, ff = act.shape
     depth = g.shape[1]
     is_deep = deep is not None
-    parts = PARTS[layer]
     closing = is_deep and part == parts - 1
     block = BWD_BLOCK
     steps = ff // block // parts
@@ -273,7 +301,7 @@
     if closing:
         scratch += [pltpu.VMEM((rows, depth), BF16)] * 4
     return pl.pallas_call(
-        functools.partial(bwd_kernel, is_deep, second, part, scale, rate, t, n_prev),
+        functools.partial(bwd_kernel, is_deep, second, part, parts, scale, rate, t, n_prev),
         grid=(steps,),
         in_specs=in_specs, out_specs=out_specs, out_shape=out_shape, scratch_shapes=scratch,
         input_output_aliases=aliases,
@@ -391,9 +419,9 @@
     )(*args)
 
 
-CAST_GROUPS = (1, 3, 4, 4, 4)
-MIX_GROUPS = (2,) * 8
-LAST_GROUPS = (2,) * 6 + (1,) * 4
+CAST_GROUPS = (1, 3, 4, 4, 1, 3)
+MIX_GROUPS = (4, 4, 4, 2, 2)
+LAST_GROUPS = (4, 4, 4, 1, 1, 1, 1)
 
 
 def grouped(groups):
@@ -444,15 +472,16 @@
                 h = outs[-1][3]
             return outs
 
-        def grads(step, outs, weights, t, olds):
+        def grads(window, step, outs, weights, t, olds):
             g = outs[-1][4]
             found = [None] * layers
             for layer in reversed(range(layers)):
                 act, slope, ut = outs[layer][:3]
                 deep = (outs[layer - 1][3], outs[layer][3], targets) if layer else None
                 res = None
-                for part in range(PARTS[layer]):
-                    res = backward(part, g, ut, act, slope,
+                parts = parts_of(window, step, layer)
+                for part in range(parts):
+                    res = backward(part, parts, g, ut, act, slope,
                                  *weights[layer], *olds[layer], res, step == 1, rate, layer, deep, scale, t)
                 if layer:
                     g = res[-1]
@@ -471,10 +500,10 @@
         for window in range(windows):
             final = window == windows - 1
             step_a = 2 * window
-            first = grads(0, head, weights, step_a, [params] * layers)
+            first = grads(window, 0, head, weights, step_a, [params] * layers)
             moved_on = [r[2:4] for r in first]
             middle = run_forward(moved_on, step_a + 1)
-            second = grads(1, middle, moved_on, step_a + 1, [r[:2] for r in first])
+            second = grads(window, 1, middle, moved_on, step_a + 1, [r[:2] for r in first])
             new_params = [None, None]
             new_weights = [[None, None] for _ in range(layers)]
             new_moved, head = [], []

time: 2590 us -> 2580 us (level)
    ppermute x32, waiting for transfers between devices: 744 us -> 704 us  [send(): near = lax.ppermute(wire, 'row', near_pairs)]
    pallas_call x20 -> x23, Pallas kernels: 938 us -> 958 us  [the longest x15 688 us: backward(): pl.pallas_call(functools.partial(bwd_kernel, is_deep, second, part, parts...]
    pallas_call x18 -> x12, Pallas kernels: 255 us -> 249 us  [mix_chunks(): pl.pallas_call(functools.partial(mix_kernel, rate, count, steps, n_prev,...]
    pallas_call x5 -> x6, Pallas kernels: 56.1 us -> 56.5 us  [cast_chunks(): pl.pallas_call(functools.partial(cast_kernel, count, steps, len(args) - 1...]
  transfers between devices with their start and end apart: 72 -> 72, of which waited for: 29 -> 31; matrix products, arithmetic and copies ran while one was open for 0% -> 0% of each run, Pallas kernels for 55% -> 55%
where the time goes in v4:
time: 2580 us; the launch traced here: 2570 us
  Pallas kernels  1460 us (57%)
  waiting for transfers between devices  1040 us (40%)
  starting transfers between devices  61.4 us (2%)
    ppermute x32, waiting for transfers between devices, send(): near = lax.ppermute(wire, 'row', near_pairs)  704 us
    pallas_call x15, Pallas kernels, backward(): pl.pallas_call(functools.partial(bwd_kernel, is_deep, second, part, parts...  688 us
    ppermute x32, waiting for transfers between devices, send(): far = lax.ppermute(near, 'row', far_pairs)  336 us
    pallas_call x8, Pallas kernels, activate(): pl.pallas_call(functools.partial(act_kernel, t), grid=(blocks + 1,), in_s...  270 us
    pallas_call x12, Pallas kernels, mix_chunks(): pl.pallas_call(functools.partial(mix_kernel, rate, count, steps, n_prev,...  249 us
    pallas_call x8, Pallas kernels, hidden(): pl.pallas_call(functools.partial(hidden_kernel, last, scale), grid=(rows...  201 us
    pallas_call x6, Pallas kernels, cast_chunks(): pl.pallas_call(functools.partial(cast_kernel, count, steps, len(args) - 1...  56.5 us
  transfers between devices with their start and end apart: 72, of which 31 were waited for; matrix products, arithmetic and copies ran while one was open for 0% of the time, Pallas kernels for 55%

profile of v4, /device:TPU:0, one launch (start us, length us, event | category | flops | bytes accessed | tf_op | source)
XLA Modules:
  0.0 2568.0 jit_solution(8690780398505079190)
XLA Ops:
  64.5 33.7 %shard_map.61 = (bf16[2048,4096]{1,0:T(8,128)(2,1)}, f32[2048,4096]{1,0:T(8,128)}, bf16[1024,2048]{1,0:T(8,128)(2,1)}) custom-call(bf16[1,1,4,2048,1024]{4,3,2,1,0:T(8,128)(2,1)} %h_ref.7, bf16[1024,4096]{1,0:T(8,128)(2,1)} %get-tuple-element.135.w1_ref), custom_call_target="tpu_custom_call" | custom-call | flops 17179869184 | bytes 58720256 | tf_op jit(solution)/shard_map/pallas_call | solution.py:90
  98.2 24.0 shard_map.63.h_hbm.h_ref.refs_7_
  122.3 33.7 %shard_map.65 = (bf16[2048,4096]{1,0:T(8,128)(2,1)}, f32[2048,4096]{1,0:T(8,128)}, bf16[1024,2048]{1,0:T(8,128)(2,1)}) custom-call(bf16[2048,1024]{1,0:T(8,128)(2,1)} %shard_map.63.h_hbm.h_ref.refs_7_, bf16[1024,4096]{1,0:T(8,128)(2,1)} %get-tuple-element.138.w1_ref.refs_5_), custom_call_target="tpu_custom_call" | custom-call | flops 17179869184 | bytes 58720256 | tf_op jit(solution)/shard_map/pallas_call | solution.py:90
  156.0 26.3 %shard_map.68 = (bf16[2048,1024]{1,0:T(8,128)(2,1)}, bf16[2048,1024]{1,0:T(8,128)(2,1)}) custom-call(bf16[2048,4096]{1,0:T(8,128)(2,1)} %get-tuple-element.139.act_ref.refs_2_, bf16[4096,1024]{1,0:T(8,128)(2,1)} %get-tuple-element.141.w2_hbm.refs_4_, bf16[2048,1024]{1,0:T(8,128)(2,1)} %shard_map.63.h_hbm.h_ref.refs_7_, bf16[1,1,4,2048,1024]{4,3,2,1,0:T(8,128)(2,1)} %refs_9_.7), custom_call_target="tpu_custom_call" | custom-call | flops 17179869184 | bytes 25165824 | tf_op jit(solution)/shard_map/pallas_call | solution.py:143
  182.3 48.6 %shard_map.69 = (f32[1024,4096]{1,0:T(8,128)}, f32[4096,1024]{1,0:T(8,128)}, bf16[1024,4096]{1,0:T(8,128)(2,1)}, bf16[4096,1024]{1,0:T(8,128)(2,1)}, f32[2048,1024]{1,0:T(8,128)}) custom-call(bf16[2048,1024]{1,0:T(8,128)(2,1)} %get-tuple-element.142.refs_0_, bf16[1024,2048]{1,0:T(8,128)(2,1)} %get-tuple-element.143.refs_1_, ...), custom_call_target="tpu_custom_call" | custom-call | flops 34359738368 | bytes 75497472 | tf_op jit(solution)/shard_map/pallas_call | solution.py:303
  231.0 55.2 %shard_map.70 = (f32[1024,4096]{1,0:T(8,128)}, f32[4096,1024]{1,0:T(8,128)}, bf16[1024,4096]{1,0:T(8,128)(2,1)}, bf16[4096,1024]{1,0:T(8,128)(2,1)}, bf16[2048,1024]{1,0:T(8,128)(2,1)}) custom-call(bf16[2048,1024]{1,0:T(8,128)(2,1)} %get-tuple-element.142.refs_0_, ...), custom_call_target="tpu_custom_call", output_to_operand_aliasing={{0}: (12, {}), {1}: (13, {}), {2}: (14, {}), {3}: (15, {})} | custom-call | flops 34359738368 | bytes 75497472 | tf_op jit(solution)/shard_map/pallas_call | solution.py:303
  286.2 35.3 %shard_map.71 = (f32[1024,4096]{1,0:T(8,128)}, f32[4096,1024]{1,0:T(8,128)}, bf16[1024,4096]{1,0:T(8,128)(2,1)}, bf16[4096,1024]{1,0:T(8,128)(2,1)}) custom-call(bf16[2048,1024]{1,0:T(8,128)(2,1)} %get-tuple-element.151.refs_0_, bf16[1024,2048]{1,0:T(8,128)(2,1)} %get-tuple-element.152.refs_1_, bf16[2048,4096]{1,0:T(8,128)(2,1)} %get-tuple-element.136.act_ref.refs_2_, ...), custom_call_target="tpu_custom_call" | custom-call | flops 25769803776 | bytes 75497472 | tf_op jit(solution)/shard_map/pallas_call | solution.py:303
  335.0 35.3 %shard_map.72 = (f32[1024,4096]{1,0:T(8,128)}, f32[4096,1024]{1,0:T(8,128)}, bf16[1024,4096]{1,0:T(8,128)(2,1)}, bf16[4096,1024]{1,0:T(8,128)(2,1)}) custom-call(bf16[2048,1024]{1,0:T(8,128)(2,1)} %get-tuple-element.151.refs_0_, ...), custom_call_target="tpu_custom_call", output_to_operand_aliasing={{0}: (7, {}), {1}: (8, {}), {2}: (9, {}), {3}: (10, {})} | custom-call | flops 25769803776 | bytes 75497472 | tf_op jit(solution)/shard_map/pallas_call | solution.py:303
  379.9 44.9 %collective-permute-done.29.refs_1_ = bf16[1024,1024]{1,0:T(8,128)(2,1)} collective-permute-done((bf16[1024,1024]{1,0:T(8,128)(2,1)}, bf16[1024,1024]{1,0:T(8,128)(2,1)}, u32[]{:S(2)}, u32[]{:S(2)}) %collective-permute-start.29) | collective-permute-done | bytes 2097184 | tf_op jit(solution)/shard_map/ppermute | solution.py:453
  424.9 44.9 %collective-permute-done.11.refs_1_ = bf16[256,4096]{1,0:T(8,128)(2,1)} collective-permute-done((bf16[256,4096]{1,0:T(8,128)(2,1)}, bf16[256,4096]{1,0:T(8,128)(2,1)}, u32[]{:S(2)}, u32[]{:S(2)}) %collective-permute-start.11) | collective-permute-done | bytes 2097184 | tf_op jit(solution)/shard_map/ppermute | solution.py:453
  469.8 44.9 %collective-permute-done.12.refs_2_ = bf16[256,4096]{1,0:T(8,128)(2,1)} collective-permute-done((bf16[256,4096]{1,0:T(8,128)(2,1)}, bf16[256,4096]{1,0:T(8,128)(2,1)}, u32[]{:S(2)}, u32[]{:S(2)}) %collective-permute-start.12) | collective-permute-done | bytes 2097184 | tf_op jit(solution)/shard_map/ppermute | solution.py:453
  514.8 44.9 %collective-permute-done.13.refs_3_ = bf16[256,4096]{1,0:T(8,128)(2,1)} collective-permute-done((bf16[256,4096]{1,0:T(8,128)(2,1)}, bf16[256,4096]{1,0:T(8,128)(2,1)}, u32[]{:S(2)}, u32[]{:S(2)}) %collective-permute-start.13) | collective-permute-done | bytes 2097184 | tf_op jit(solution)/shard_map/ppermute | solution.py:453
  559.7 33.9 %shard_map.73 = (bf16[2048,4096]{1,0:T(8,128)(2,1)}, f32[2048,4096]{1,0:T(8,128)}, bf16[1024,2048]{1,0:T(8,128)(2,1)}) custom-call(bf16[1,1,4,2048,1024]{4,3,2,1,0:T(8,128)(2,1)} %h_ref.7, bf16[1024,4096]{1,0:T(8,128)(2,1)} %get-tuple-element.158.w1_ref), custom_call_target="tpu_custom_call" | custom-call | flops 17179869184 | bytes 58720256 | tf_op jit(solution)/shard_map/pallas_call | solution.py:90
  593.6 24.0 shard_map.74.h_hbm.h_ref.refs_7_
  619.7 29.9 %collective-permute-done.1.refs_0_ = bf16[256,4096]{1,0:T(8,128)(2,1)} collective-permute-done((bf16[256,4096]{1,0:T(8,128)(2,1)}, bf16[256,4096]{1,0:T(8,128)(2,1)}, u32[]{:S(2)}, u32[]{:S(2)}) %collective-permute-start.1) | collective-permute-done | bytes 2097184 | tf_op jit(solution)/shard_map/ppermute | solution.py:453
  651.1 43.4 %collective-permute-done.2.refs_1_ = bf16[256,4096]{1,0:T(8,128)(2,1)} collective-permute-done((bf16[256,4096]{1,0:T(8,128)(2,1)}, bf16[256,4096]{1,0:T(8,128)(2,1)}, u32[]{:S(2)}, u32[]{:S(2)}) %collective-permute-start.2) | collective-permute-done | bytes 2097184 | tf_op jit(solution)/shard_map/ppermute | solution.py:453
  696.0 43.4 %collective-permute-done.3.refs_2_ = bf16[256,4096]{1,0:T(8,128)(2,1)} collective-permute-done((bf16[256,4096]{1,0:T(8,128)(2,1)}, bf16[256,4096]{1,0:T(8,128)(2,1)}, u32[]{:S(2)}, u32[]{:S(2)}) %collective-permute-start.3) | collective-permute-done | bytes 2097184 | tf_op jit(solution)/shard_map/ppermute | solution.py:453
  741.0 40.9 %collective-permute-done.4.refs_3_ = bf16[256,4096]{1,0:T(8,128)(2,1)} collective-permute-done((bf16[256,4096]{1,0:T(8,128)(2,1)}, bf16[256,4096]{1,0:T(8,128)(2,1)}, u32[]{:S(2)}, u32[]{:S(2)}) %collective-permute-start.4) | collective-permute-done | bytes 2097184 | tf_op jit(solution)/shard_map/ppermute | solution.py:453
  783.4 33.7 %shard_map.75 = (bf16[2048,4096]{1,0:T(8,128)(2,1)}, f32[2048,4096]{1,0:T(8,128)}, bf16[1024,2048]{1,0:T(8,128)(2,1)}) custom-call(bf16[2048,1024]{1,0:T(8,128)(2,1)} %shard_map.74.h_hbm.h_ref.refs_7_, bf16[1024,4096]{1,0:T(8,128)(2,1)} %get-tuple-element.161.w1_ref.refs_5_), custom_call_target="tpu_custom_call" | custom-call | flops 17179869184 | bytes 58720256 | tf_op jit(solution)/shard_map/pallas_call | solution.py:90
  817.1 26.3 %shard_map.76 = (bf16[2048,1024]{1,0:T(8,128)(2,1)}, bf16[2048,1024]{1,0:T(8,128)(2,1)}) custom-call(bf16[2048,4096]{1,0:T(8,128)(2,1)} %get-tuple-element.162.act_ref.refs_2_, bf16[4096,1024]{1,0:T(8,128)(2,1)} %get-tuple-element.163.w2_hbm.refs_4_, bf16[2048,1024]{1,0:T(8,128)(2,1)} %shard_map.74.h_hbm.h_ref.refs_7_, bf16[1,1,4,2048,1024]{4,3,2,1,0:T(8,128)(2,1)} %refs_9_.7), custom_call_target="tpu_custom_call" | custom-call | flops 17179869184 | bytes 25165824 | tf_op jit(solution)/shard_map/pallas_call | solution.py:143
  846.5 48.3 %shard_map.77 = (f32[1024,4096]{1,0:T(8,128)}, f32[4096,1024]{1,0:T(8,128)}, f32[2048,1024]{1,0:T(8,128)}) custom-call(bf16[2048,1024]{1,0:T(8,128)(2,1)} %get-tuple-element.164.refs_0_, bf16[1024,2048]{1,0:T(8,128)(2,1)} %get-tuple-element.165.refs_1_, bf16[2048,4096]{1,0:T(8,128)(2,1)} %get-tuple-element.162.act_ref.refs_2_, ...), custom_call_target="tpu_custom_call" | custom-call | flops 34359738368 | bytes 75497472 | tf_op jit(solution)/shard_map/pallas_call | solution.py:303
  894.8 42.9 %collective-permute-done.15.refs_5_ = bf16[256,4096]{1,0:T(8,128)(2,1)} collective-permute-done((bf16[256,4096]{1,0:T(8,128)(2,1)}, bf16[256,4096]{1,0:T(8,128)(2,1)}, u32[]{:S(2)}, u32[]{:S(2)}) %collective-permute-start.15) | collective-permute-done | bytes 2097184 | tf_op jit(solution)/shard_map/ppermute | solution.py:454
  937.7 44.0 %collective-permute-done.16.refs_6_ = bf16[256,4096]{1,0:T(8,128)(2,1)} collective-permute-done((bf16[256,4096]{1,0:T(8,128)(2,1)}, bf16[256,4096]{1,0:T(8,128)(2,1)}, u32[]{:S(2)}, u32[]{:S(2)}) %collective-permute-start.16) | collective-permute-done | bytes 2097184 | tf_op jit(solution)/shard_map/ppermute | solution.py:454
  982.2 54.7 %shard_map.78 = (f32[1024,4096]{1,0:T(8,128)}, f32[4096,1024]{1,0:T(8,128)}, bf16[2048,1024]{1,0:T(8,128)(2,1)}) custom-call(bf16[2048,1024]{1,0:T(8,128)(2,1)} %get-tuple-element.164.refs_0_, bf16[1024,2048]{1,0:T(8,128)(2,1)} %get-tuple-element.165.refs_1_, ...), custom_call_target="tpu_custom_call", output_to_operand_aliasing={{0}: (12, {}), {1}: (13, {})} | custom-call | flops 34359738368 | bytes 75497472 | tf_op jit(solution)/shard_map/pallas_call | solution.py:303
  1038.5 35.0 %shard_map.79 = (f32[1024,4096]{1,0:T(8,128)}, f32[4096,1024]{1,0:T(8,128)}) custom-call(bf16[2048,1024]{1,0:T(8,128)(2,1)} %get-tuple-element.178.refs_0_, bf16[1024,2048]{1,0:T(8,128)(2,1)} %get-tuple-element.179.refs_1_, bf16[2048,4096]{1,0:T(8,128)(2,1)} %get-tuple-element.159.act_ref.refs_2_, f32[2048,4096]{1,0:T(8,128)} %get-tuple-element.180.refs_3_, ...), custom_call_target="tpu_custom_call" | custom-call | flops 25769803776 | bytes 75497472 | tf_op jit(solution)/shard_map/pallas_call | solution.py:303
  1085.8 35.1 %shard_map.80 = (f32[1024,4096]{1,0:T(8,128)}, f32[4096,1024]{1,0:T(8,128)}) custom-call(bf16[2048,1024]{1,0:T(8,128)(2,1)} %get-tuple-element.178.refs_0_, bf16[1024,2048]{1,0:T(8,128)(2,1)} %get-tuple-element.179.refs_1_, bf16[2048,4096]{1,0:T(8,128)(2,1)} %get-tuple-element.159.act_ref.refs_2_, ...), custom_call_target="tpu_custom_call", output_to_operand_aliasing={{0}: (7, {}), {1}: (8, {})} | custom-call | flops 25769803776 | bytes 75497472 | tf_op jit(solution)/shard_map/pallas_call | solution.py:303
  1120.8 33.7 %shard_map.81 = (f32[1,1,2,1024,4096]{4,3,2,1,0:T(8,128)}, bf16[1024,4096]{1,0:T(8,128)(2,1)}, bf16[256,4096]{1,0:T(8,128)(2,1)}, bf16[256,4096]{1,0:T(8,128)(2,...) custom-call(s32[1]{0:T(128)} %bitcast.par_ref, f32[1,1,2,1024,4096]{4,3,2,1,0:T(8,128)} %p_ref.18, ...), custom_call_target="tpu_custom_call" | custom-call | flops 1000000000 | bytes 83886080 | tf_op jit(solution)/shard_map/pallas_call | solution.py:411
  1156.6 33.7 %shard_map.83 = (bf16[2048,4096]{1,0:T(8,128)(2,1)}, f32[2048,4096]{1,0:T(8,128)}, bf16[1024,2048]{1,0:T(8,128)(2,1)}) custom-call(bf16[1,1,4,2048,1024]{4,3,2,1,0:T(8,128)(2,1)} %h_ref.7, bf16[1024,4096]{1,0:T(8,128)(2,1)} %get-tuple-element.192.w1_ref), custom_call_target="tpu_custom_call" | custom-call | flops 17179869184 | bytes 58720256 | tf_op jit(solution)/shard_map/pallas_call | solution.py:90
  1190.3 33.6 %shard_map.84 = (f32[1,1,2,4096,1024]{4,3,2,1,0:T(8,128)}, bf16[4096,1024]{1,0:T(8,128)(2,1)}, bf16[1024,1024]{1,0:T(8,128)(2,1)}, bf16[1024,1024]{1,0:T(8,128)(...) custom-call(s32[1]{0:T(128)} %bitcast.par_ref, f32[1,1,2,4096,1024]{4,3,2,1,0:T(8,128)} %p_ref.21, ...), custom_call_target="tpu_custom_call" | custom-call | flops 1000000000 | bytes 83886080 | tf_op jit(solution)/shard_map/pallas_call | solution.py:411
  1226.0 24.0 shard_map.85.h_hbm.h_ref.refs_7_
  1250.0 17.2 shard_map.87
  1269.6 33.8 %shard_map.82 = (f32[1,1,2,1024,4096]{4,3,2,1,0:T(8,128)}, bf16[1024,4096]{1,0:T(8,128)(2,1)}, bf16[256,4096]{1,0:T(8,128)(2,1)}, bf16[256,4096]{1,0:T(8,128)(2,...) custom-call(s32[1]{0:T(128)} %bitcast.par_ref, ...), custom_call_target="tpu_custom_call", output_to_operand_aliasing={{0}: (12, {})} | custom-call | flops 1000000000 | bytes 83886080 | tf_op jit(solution)/shard_map/pallas_call | solution.py:411
  1303.4 33.7 %shard_map.86 = (bf16[2048,4096]{1,0:T(8,128)(2,1)}, f32[2048,4096]{1,0:T(8,128)}, bf16[1024,2048]{1,0:T(8,128)(2,1)}) custom-call(bf16[2048,1024]{1,0:T(8,128)(2,1)} %shard_map.85.h_hbm.h_ref.refs_7_, bf16[1024,4096]{1,0:T(8,128)(2,1)} %get-tuple-element.200.w1_ref.refs_5_), custom_call_target="tpu_custom_call" | custom-call | flops 17179869184 | bytes 58720256 | tf_op jit(solution)/shard_map/pallas_call | solution.py:90
  1338.8 15.5 collective-permute-done.31.refs_3_
  1354.8 17.2 shard_map.88
  1371.9 26.1 %shard_map.89 = (bf16[2048,1024]{1,0:T(8,128)(2,1)}, bf16[2048,1024]{1,0:T(8,128)(2,1)}) custom-call(bf16[2048,4096]{1,0:T(8,128)(2,1)} %get-tuple-element.201.act_ref.refs_2_, bf16[4096,1024]{1,0:T(8,128)(2,1)} %get-tuple-element.210.w2_hbm.refs_4_, bf16[2048,1024]{1,0:T(8,128)(2,1)} %shard_map.85.h_hbm.h_ref.refs_7_, bf16[1,1,4,2048,1024]{4,3,2,1,0:T(8,128)(2,1)} %refs_9_.7), custom_call_target="tpu_custom_call" | custom-call | flops 17179869184 | bytes 25165824 | tf_op jit(solution)/shard_map/pallas_call | solution.py:143
  1398.0 49.2 %shard_map.90 = (f32[1024,4096]{1,0:T(8,128)}, f32[4096,1024]{1,0:T(8,128)}, bf16[1024,4096]{1,0:T(8,128)(2,1)}, bf16[4096,1024]{1,0:T(8,128)(2,1)}, f32[2048,1024]{1,0:T(8,128)}) custom-call(bf16[2048,1024]{1,0:T(8,128)(2,1)} %get-tuple-element.211.refs_0_, bf16[1024,2048]{1,0:T(8,128)(2,1)} %get-tuple-element.212.refs_1_, ...), custom_call_target="tpu_custom_call" | custom-call | flops 34359738368 | bytes 75497472 | tf_op jit(solution)/shard_map/pallas_call | solution.py:303
  1451.3 54.8 %shard_map.91 = (f32[1024,4096]{1,0:T(8,128)}, f32[4096,1024]{1,0:T(8,128)}, bf16[1024,4096]{1,0:T(8,128)(2,1)}, bf16[4096,1024]{1,0:T(8,128)(2,1)}, bf16[2048,1024]{1,0:T(8,128)(2,1)}) custom-call(bf16[2048,1024]{1,0:T(8,128)(2,1)} %get-tuple-element.211.refs_0_, ...), custom_call_target="tpu_custom_call", output_to_operand_aliasing={{0}: (12, {}), {1}: (13, {}), {2}: (14, {}), {3}: (15, {})} | custom-call | flops 34359738368 | bytes 75497472 | tf_op jit(solution)/shard_map/pallas_call | solution.py:303
  1507.8 33.0 %collective-permute-done.59.refs_0_ = bf16[1024,1024]{1,0:T(8,128)(2,1)} collective-permute-done((bf16[1024,1024]{1,0:T(8,128)(2,1)}, bf16[1024,1024]{1,0:T(8,128)(2,1)}, u32[]{:S(2)}, u32[]{:S(2)}) %collective-permute-start.59) | collective-permute-done | bytes 2097184 | tf_op jit(solution)/shard_map/ppermute | solution.py:453
  1541.1 44.6 %collective-permute-done.57.refs_0_ = bf16[1024,1024]{1,0:T(8,128)(2,1)} collective-permute-done((bf16[1024,1024]{1,0:T(8,128)(2,1)}, bf16[1024,1024]{1,0:T(8,128)(2,1)}, u32[]{:S(2)}, u32[]{:S(2)}) %collective-permute-start.57) | collective-permute-done | bytes 2097184 | tf_op jit(solution)/shard_map/ppermute | solution.py:453
  1586.0 44.6 %collective-permute-done.55.refs_0_ = bf16[1024,1024]{1,0:T(8,128)(2,1)} collective-permute-done((bf16[1024,1024]{1,0:T(8,128)(2,1)}, bf16[1024,1024]{1,0:T(8,128)(2,1)}, u32[]{:S(2)}, u32[]{:S(2)}) %collective-permute-start.55) | collective-permute-done | bytes 2097184 | tf_op jit(solution)/shard_map/ppermute | solution.py:453
  1631.0 44.6 %collective-permute-done.46.refs_0_ = bf16[256,4096]{1,0:T(8,128)(2,1)} collective-permute-done((bf16[256,4096]{1,0:T(8,128)(2,1)}, bf16[256,4096]{1,0:T(8,128)(2,1)}, u32[]{:S(2)}, u32[]{:S(2)}) %collective-permute-start.46) | collective-permute-done | bytes 2097184 | tf_op jit(solution)/shard_map/ppermute | solution.py:453
  1675.9 63.4 %shard_map.92 = (f32[1024,4096]{1,0:T(8,128)}, f32[4096,1024]{1,0:T(8,128)}, bf16[1024,4096]{1,0:T(8,128)(2,1)}, bf16[4096,1024]{1,0:T(8,128)(2,1)}) custom-call(bf16[2048,1024]{1,0:T(8,128)(2,1)} %get-tuple-element.221.refs_0_, bf16[1024,2048]{1,0:T(8,128)(2,1)} %get-tuple-element.222.refs_1_, bf16[2048,4096]{1,0:T(8,128)(2,1)} %get-tuple-element.193.act_ref.refs_2_, ...), custom_call_target="tpu_custom_call" | custom-call | flops 51539607552 | bytes 150994944 | tf_op jit(solution)/shard_map/pallas_call | solution.py:303
  1741.1 24.4 collective-permute-done.48.refs_2_
  1765.8 44.6 %collective-permute-done.49.refs_3_ = bf16[256,4096]{1,0:T(8,128)(2,1)} collective-permute-done((bf16[256,4096]{1,0:T(8,128)(2,1)}, bf16[256,4096]{1,0:T(8,128)(2,1)}, u32[]{:S(2)}, u32[]{:S(2)}) %collective-permute-start.49) | collective-permute-done | bytes 2097184 | tf_op jit(solution)/shard_map/ppermute | solution.py:453
  1811.9 43.4 %collective-permute-done.37.refs_0_ = bf16[256,4096]{1,0:T(8,128)(2,1)} collective-permute-done((bf16[256,4096]{1,0:T(8,128)(2,1)}, bf16[256,4096]{1,0:T(8,128)(2,1)}, u32[]{:S(2)}, u32[]{:S(2)}) %collective-permute-start.37) | collective-permute-done | bytes 2097184 | tf_op jit(solution)/shard_map/ppermute | solution.py:453
  1856.8 43.4 %collective-permute-done.38.refs_1_ = bf16[256,4096]{1,0:T(8,128)(2,1)} collective-permute-done((bf16[256,4096]{1,0:T(8,128)(2,1)}, bf16[256,4096]{1,0:T(8,128)(2,1)}, u32[]{:S(2)}, u32[]{:S(2)}) %collective-permute-start.38) | collective-permute-done | bytes 2097184 | tf_op jit(solution)/shard_map/ppermute | solution.py:453
  1901.8 33.9 %shard_map.93 = (bf16[2048,4096]{1,0:T(8,128)(2,1)}, f32[2048,4096]{1,0:T(8,128)}, bf16[1024,2048]{1,0:T(8,128)(2,1)}) custom-call(bf16[1,1,4,2048,1024]{4,3,2,1,0:T(8,128)(2,1)} %h_ref.7, bf16[1024,4096]{1,0:T(8,128)(2,1)} %get-tuple-element.224.w1_ref), custom_call_target="tpu_custom_call" | custom-call | flops 17179869184 | bytes 58720256 | tf_op jit(solution)/shard_map/pallas_call | solution.py:90
  1935.7 24.0 shard_map.94.h_hbm.h_ref.refs_7_
  1960.3 25.3 collective-permute-done.40.refs_3_
  1989.6 33.6 %shard_map.95 = (bf16[2048,4096]{1,0:T(8,128)(2,1)}, f32[2048,4096]{1,0:T(8,128)}, bf16[1024,2048]{1,0:T(8,128)(2,1)}) custom-call(bf16[2048,1024]{1,0:T(8,128)(2,1)} %shard_map.94.h_hbm.h_ref.refs_7_, bf16[1024,4096]{1,0:T(8,128)(2,1)} %get-tuple-element.227.w1_ref.refs_5_), custom_call_target="tpu_custom_call" | custom-call | flops 17179869184 | bytes 58720256 | tf_op jit(solution)/shard_map/pallas_call | solution.py:90
  2023.2 26.3 %shard_map.96 = (bf16[2048,1024]{1,0:T(8,128)(2,1)}, bf16[2048,1024]{1,0:T(8,128)(2,1)}) custom-call(bf16[2048,4096]{1,0:T(8,128)(2,1)} %get-tuple-element.228.act_ref.refs_2_, bf16[4096,1024]{1,0:T(8,128)(2,1)} %get-tuple-element.229.w2_hbm.refs_4_, bf16[2048,1024]{1,0:T(8,128)(2,1)} %shard_map.94.h_hbm.h_ref.refs_7_, bf16[1,1,4,2048,1024]{4,3,2,1,0:T(8,128)(2,1)} %refs_9_.7), custom_call_target="tpu_custom_call" | custom-call | flops 17179869184 | bytes 25165824 | tf_op jit(solution)/shard_map/pallas_call | solution.py:143
  2053.5 44.9 %collective-permute-done.60.refs_1_ = bf16[1024,1024]{1,0:T(8,128)(2,1)} collective-permute-done((bf16[1024,1024]{1,0:T(8,128)(2,1)}, bf16[1024,1024]{1,0:T(8,128)(2,1)}, u32[]{:S(2)}, u32[]{:S(2)}) %collective-permute-start.60) | collective-permute-done | bytes 2097184 | tf_op jit(solution)/shard_map/ppermute | solution.py:454
  2098.4 44.9 %collective-permute-done.58.refs_1_ = bf16[1024,1024]{1,0:T(8,128)(2,1)} collective-permute-done((bf16[1024,1024]{1,0:T(8,128)(2,1)}, bf16[1024,1024]{1,0:T(8,128)(2,1)}, u32[]{:S(2)}, u32[]{:S(2)}) %collective-permute-start.58) | collective-permute-done | bytes 2097184 | tf_op jit(solution)/shard_map/ppermute | solution.py:454
  2143.9 44.4 %collective-permute-done.56.refs_1_ = bf16[1024,1024]{1,0:T(8,128)(2,1)} collective-permute-done((bf16[1024,1024]{1,0:T(8,128)(2,1)}, bf16[1024,1024]{1,0:T(8,128)(2,1)}, u32[]{:S(2)}, u32[]{:S(2)}) %collective-permute-start.56) | collective-permute-done | bytes 2097184 | tf_op jit(solution)/shard_map/ppermute | solution.py:454
  2188.8 48.3 %shard_map.97 = (f32[1024,4096]{1,0:T(8,128)}, f32[4096,1024]{1,0:T(8,128)}, f32[2048,1024]{1,0:T(8,128)}) custom-call(bf16[2048,1024]{1,0:T(8,128)(2,1)} %get-tuple-element.230.refs_0_, bf16[1024,2048]{1,0:T(8,128)(2,1)} %get-tuple-element.231.refs_1_, bf16[2048,4096]{1,0:T(8,128)(2,1)} %get-tuple-element.228.act_ref.refs_2_, ...), custom_call_target="tpu_custom_call" | custom-call | flops 34359738368 | bytes 75497472 | tf_op jit(solution)/shard_map/pallas_call | solution.py:303
  2237.2 38.0 %collective-permute-done.51.refs_5_ = bf16[256,4096]{1,0:T(8,128)(2,1)} collective-permute-done((bf16[256,4096]{1,0:T(8,128)(2,1)}, bf16[256,4096]{1,0:T(8,128)(2,1)}, u32[]{:S(2)}, u32[]{:S(2)}) %collective-permute-start.51) | collective-permute-done | bytes 2097184 | tf_op jit(solution)/shard_map/ppermute | solution.py:454
  2275.7 54.5 %shard_map.98 = (f32[1024,4096]{1,0:T(8,128)}, f32[4096,1024]{1,0:T(8,128)}, bf16[2048,1024]{1,0:T(8,128)(2,1)}) custom-call(bf16[2048,1024]{1,0:T(8,128)(2,1)} %get-tuple-element.230.refs_0_, bf16[1024,2048]{1,0:T(8,128)(2,1)} %get-tuple-element.231.refs_1_, ...), custom_call_target="tpu_custom_call", output_to_operand_aliasing={{0}: (12, {}), {1}: (13, {})} | custom-call | flops 34359738368 | bytes 75497472 | tf_op jit(solution)/shard_map/pallas_call | solution.py:303
  2331.7 35.1 %shard_map.99 = (f32[1024,4096]{1,0:T(8,128)}, f32[4096,1024]{1,0:T(8,128)}) custom-call(bf16[2048,1024]{1,0:T(8,128)(2,1)} %get-tuple-element.244.refs_0_, bf16[1024,2048]{1,0:T(8,128)(2,1)} %get-tuple-element.245.refs_1_, bf16[2048,4096]{1,0:T(8,128)(2,1)} %get-tuple-element.225.act_ref.refs_2_, f32[2048,4096]{1,0:T(8,128)} %get-tuple-element.246.refs_3_, ...), custom_call_target="tpu_custom_call" | custom-call | flops 25769803776 | bytes 75497472 | tf_op jit(solution)/shard_map/pallas_call | solution.py:303
  2373.4 35.1 %shard_map.100 = (f32[1024,4096]{1,0:T(8,128)}, f32[4096,1024]{1,0:T(8,128)}) custom-call(bf16[2048,1024]{1,0:T(8,128)(2,1)} %get-tuple-element.244.refs_0_, bf16[1024,2048]{1,0:T(8,128)(2,1)} %get-tuple-element.245.refs_1_, bf16[2048,4096]{1,0:T(8,128)(2,1)} %get-tuple-element.225.act_ref.refs_2_, ...), custom_call_target="tpu_custom_call", output_to_operand_aliasing={{0}: (7, {}), {1}: (8, {})} | custom-call | flops 25769803776 | bytes 75497472 | tf_op jit(solution)/shard_map/pallas_call | solution.py:303
  2408.5 27.5 %shard_map.103.refs_2_ = f32[1,1,2,4096,1024]{4,3,2,1,0:T(8,128)} custom-call(s32[1]{0:T(128)} %bitcast.par_ref, f32[1,1,2,4096,1024]{4,3,2,1,0:T(8,128)} %get-tuple-element.214.refs_7_.refs_11_.refs_6_.p_ref, f32[4096,1024]{1,0:T(8,128)} %get-tuple-element.261.grad_ref, bf16[4096,1024]{1,0:T(8,128)(2,1)} %collective-permute-done.63.col_ref, ...), custom_call_target="tpu_custom_call" | custom-call | flops 1000000000 | bytes 83886080 | tf_op jit(solution)/shard_map/pallas_call | solution.py:411
  2467.2 27.5 %shard_map.101.refs_8_ = f32[1,1,2,1024,4096]{4,3,2,1,0:T(8,128)} custom-call(s32[1]{0:T(128)} %bitcast.par_ref, f32[1,1,2,1024,4096]{4,3,2,1,0:T(8,128)} %get-tuple-element.191.refs_6_.refs_10_.refs_5_.p_ref, f32[1024,4096]{1,0:T(8,128)} %get-tuple-element.251.grad_ref, bf16[1024,4096]{1,0:T(8,128)(2,1)} %collective-permute-done.45.col_ref, ...), custom_call_target="tpu_custom_call" | custom-call | flops 1000000000 | bytes 83886080 | tf_op jit(solution)/shard_map/pallas_call | solution.py:411
  2508.0 32.0 %collective-permute-done.44.refs_7_ = bf16[256,4096]{1,0:T(8,128)(2,1)} collective-permute-done((bf16[256,4096]{1,0:T(8,128)(2,1)}, bf16[256,4096]{1,0:T(8,128)(2,1)}, u32[]{:S(2)}, u32[]{:S(2)}) %collective-permute-start.44) | collective-permute-done | bytes 2097184 | tf_op jit(solution)/shard_map/ppermute | solution.py:454
  2540.0 27.5 %shard_map.102 = f32[1,1,2,1024,4096]{4,3,2,1,0:T(8,128)} custom-call(s32[1]{0:T(128)} %bitcast.par_ref, f32[1,1,2,1024,4096]{4,3,2,1,0:T(8,128)} %get-tuple-element.191.refs_6_.refs_10_.refs_5_.p_ref, f32[1024,4096]{1,0:T(8,128)} %get-tuple-element.239.grad_ref, ...), custom_call_target="tpu_custom_call", output_to_operand_aliasing={{}: (12, {})} | custom-call | flops 1000000000 | bytes 83886080 | tf_op jit(solution)/shard_map/pallas_call | solution.py:411
  (129 shorter events, 197.8 us)
Async XLA Ops:
  14.7 271.5 %collective-permute-start.19 = (bf16[1024,1024]{1,0:T(8,128)(2,1)}, bf16[1024,1024]{1,0:T(8,128)(2,1)}, u32[]{:S(2)}, u32[]{:S(2)}) collective-permute-start(bf16[1024,1024]{1,0:T(8,128)(2,1)} %get-tuple-element.195), channel_id=1, source_target_pairs={{0,2},{2,0},{4,6},{6,4},{1,3},{3,1},{5,7},{7,5}} | collective-permute-start | bytes 6291464 | tf_op jit(solution)/shard_map/ppermute | solution.py:453
  18.0 303.5 %collective-permute-start.20 = (bf16[1024,1024]{1,0:T(8,128)(2,1)}, bf16[1024,1024]{1,0:T(8,128)(2,1)}, u32[]{:S(2)}, u32[]{:S(2)}) collective-permute-start(bf16[1024,1024]{1,0:T(8,128)(2,1)} %get-tuple-element.196), channel_id=1, source_target_pairs={{0,2},{2,0},{4,6},{6,4},{1,3},{3,1},{5,7},{7,5}} | collective-permute-start | bytes 6291464 | tf_op jit(solution)/shard_map/ppermute | solution.py:453
  18.0 305.5 %collective-permute-start.21 = (bf16[1024,1024]{1,0:T(8,128)(2,1)}, bf16[1024,1024]{1,0:T(8,128)(2,1)}, u32[]{:S(2)}, u32[]{:S(2)}) collective-permute-start(bf16[1024,1024]{1,0:T(8,128)(2,1)} %get-tuple-element.197), channel_id=1, source_target_pairs={{0,2},{2,0},{4,6},{6,4},{1,3},{3,1},{5,7},{7,5}} | collective-permute-start | bytes 6291464 | tf_op jit(solution)/shard_map/ppermute | solution.py:453
  20.0 303.5 %collective-permute-start.22 = (bf16[1024,1024]{1,0:T(8,128)(2,1)}, bf16[1024,1024]{1,0:T(8,128)(2,1)}, u32[]{:S(2)}, u32[]{:S(2)}) collective-permute-start(bf16[1024,1024]{1,0:T(8,128)(2,1)} %get-tuple-element.198), channel_id=1, source_target_pairs={{0,2},{2,0},{4,6},{6,4},{1,3},{3,1},{5,7},{7,5}} | collective-permute-start | bytes 6291464 | tf_op jit(solution)/shard_map/ppermute | solution.py:453
  34.3 291.3 %collective-permute-start.33 = (bf16[1024,1024]{1,0:T(8,128)(2,1)}, bf16[1024,1024]{1,0:T(8,128)(2,1)}, u32[]{:S(2)}, u32[]{:S(2)}) collective-permute-start(bf16[1024,1024]{1,0:T(8,128)(2,1)} %get-tuple-element.206), channel_id=1, source_target_pairs={{0,2},{2,0},{4,6},{6,4},{1,3},{3,1},{5,7},{7,5}} | collective-permute-start | bytes 6291464 | tf_op jit(solution)/shard_map/ppermute | solution.py:453
  323.5 101.4 %collective-permute-start.29 = (bf16[1024,1024]{1,0:T(8,128)(2,1)}, bf16[1024,1024]{1,0:T(8,128)(2,1)}, u32[]{:S(2)}, u32[]{:S(2)}) collective-permute-start(bf16[1024,1024]{1,0:T(8,128)(2,1)} %get-tuple-element.204), channel_id=1, source_target_pairs={{0,2},{2,0},{4,6},{6,4},{1,3},{3,1},{5,7},{7,5}} | collective-permute-start | bytes 6291464 | tf_op jit(solution)/shard_map/ppermute | solution.py:453
  323.5 146.3 %collective-permute-start.11 = (bf16[256,4096]{1,0:T(8,128)(2,1)}, bf16[256,4096]{1,0:T(8,128)(2,1)}, u32[]{:S(2)}, u32[]{:S(2)}) collective-permute-start(bf16[256,4096]{1,0:T(8,128)(2,1)} %get-tuple-element.187), channel_id=1, source_target_pairs={{0,2},{2,0},{4,6},{6,4},{1,3},{3,1},{5,7},{7,5}} | collective-permute-start | bytes 6291464 | tf_op jit(solution)/shard_map/ppermute | solution.py:453
  325.5 189.2 %collective-permute-start.12 = (bf16[256,4096]{1,0:T(8,128)(2,1)}, bf16[256,4096]{1,0:T(8,128)(2,1)}, u32[]{:S(2)}, u32[]{:S(2)}) collective-permute-start(bf16[256,4096]{1,0:T(8,128)(2,1)} %get-tuple-element.188), channel_id=1, source_target_pairs={{0,2},{2,0},{4,6},{6,4},{1,3},{3,1},{5,7},{7,5}} | collective-permute-start | bytes 6291464 | tf_op jit(solution)/shard_map/ppermute | solution.py:453
  335.0 224.7 %collective-permute-start.13 = (bf16[256,4096]{1,0:T(8,128)(2,1)}, bf16[256,4096]{1,0:T(8,128)(2,1)}, u32[]{:S(2)}, u32[]{:S(2)}) collective-permute-start(bf16[256,4096]{1,0:T(8,128)(2,1)} %get-tuple-element.189), channel_id=1, source_target_pairs={{0,2},{2,0},{4,6},{6,4},{1,3},{3,1},{5,7},{7,5}} | collective-permute-start | bytes 6291464 | tf_op jit(solution)/shard_map/ppermute | solution.py:453
  379.9 237.7 %collective-permute-start.10 = (bf16[256,4096]{1,0:T(8,128)(2,1)}, bf16[256,4096]{1,0:T(8,128)(2,1)}, u32[]{:S(2)}, u32[]{:S(2)}) collective-permute-start(bf16[256,4096]{1,0:T(8,128)(2,1)} %get-tuple-element.186), channel_id=1, source_target_pairs={{0,2},{2,0},{4,6},{6,4},{1,3},{3,1},{5,7},{7,5}} | collective-permute-start | bytes 6291464 | tf_op jit(solution)/shard_map/ppermute | solution.py:453
  424.9 224.7 %collective-permute-start.1 = (bf16[256,4096]{1,0:T(8,128)(2,1)}, bf16[256,4096]{1,0:T(8,128)(2,1)}, u32[]{:S(2)}, u32[]{:S(2)}) collective-permute-start(bf16[256,4096]{1,0:T(8,128)(2,1)} %get-tuple-element.174), channel_id=1, source_target_pairs={{0,2},{2,0},{4,6},{6,4},{1,3},{3,1},{5,7},{7,5}} | collective-permute-start | bytes 6291464 | tf_op jit(solution)/shard_map/ppermute | solution.py:453
  469.8 224.7 %collective-permute-start.2 = (bf16[256,4096]{1,0:T(8,128)(2,1)}, bf16[256,4096]{1,0:T(8,128)(2,1)}, u32[]{:S(2)}, u32[]{:S(2)}) collective-permute-start(bf16[256,4096]{1,0:T(8,128)(2,1)} %get-tuple-element.175), channel_id=1, source_target_pairs={{0,2},{2,0},{4,6},{6,4},{1,3},{3,1},{5,7},{7,5}} | collective-permute-start | bytes 6291464 | tf_op jit(solution)/shard_map/ppermute | solution.py:453
  514.7 224.7 %collective-permute-start.3 = (bf16[256,4096]{1,0:T(8,128)(2,1)}, bf16[256,4096]{1,0:T(8,128)(2,1)}, u32[]{:S(2)}, u32[]{:S(2)}) collective-permute-start(bf16[256,4096]{1,0:T(8,128)(2,1)} %get-tuple-element.176), channel_id=1, source_target_pairs={{0,2},{2,0},{4,6},{6,4},{1,3},{3,1},{5,7},{7,5}} | collective-permute-start | bytes 6291464 | tf_op jit(solution)/shard_map/ppermute | solution.py:453
  559.7 222.2 %collective-permute-start.4 = (bf16[256,4096]{1,0:T(8,128)(2,1)}, bf16[256,4096]{1,0:T(8,128)(2,1)}, u32[]{:S(2)}, u32[]{:S(2)}) collective-permute-start(bf16[256,4096]{1,0:T(8,128)(2,1)} %get-tuple-element.177), channel_id=1, source_target_pairs={{0,2},{2,0},{4,6},{6,4},{1,3},{3,1},{5,7},{7,5}} | collective-permute-start | bytes 6291464 | tf_op jit(solution)/shard_map/ppermute | solution.py:453
  617.7 225.7 %collective-permute-start.23 = (bf16[1024,1024]{1,0:T(8,128)(2,1)}, bf16[1024,1024]{1,0:T(8,128)(2,1)}, u32[]{:S(2)}, u32[]{:S(2)}) collective-permute-start(bf16[1024,1024]{1,0:T(8,128)(2,1)} %collective-permute-done.19.refs_0_), channel_id=1, source_target_pairs={{0,4},{2,6},{4,0},{6,2},{1,5},{3,7},{5,1},{7,3}} | collective-permute-start | bytes 6291464 | tf_op jit(solution)/shard_map/ppermute | solution.py:454
  649.6 193.9 %collective-permute-start.24 = (bf16[1024,1024]{1,0:T(8,128)(2,1)}, bf16[1024,1024]{1,0:T(8,128)(2,1)}, u32[]{:S(2)}, u32[]{:S(2)}) collective-permute-start(bf16[1024,1024]{1,0:T(8,128)(2,1)} %collective-permute-done.20.refs_1_), channel_id=1, source_target_pairs={{0,4},{2,6},{4,0},{6,2},{1,5},{3,7},{5,1},{7,3}} | collective-permute-start | bytes 6291464 | tf_op jit(solution)/shard_map/ppermute | solution.py:454
  694.5 149.4 %collective-permute-start.25 = (bf16[1024,1024]{1,0:T(8,128)(2,1)}, bf16[1024,1024]{1,0:T(8,128)(2,1)}, u32[]{:S(2)}, u32[]{:S(2)}) collective-permute-start(bf16[1024,1024]{1,0:T(8,128)(2,1)} %collective-permute-done.21.refs_2_), channel_id=1, source_target_pairs={{0,4},{2,6},{4,0},{6,2},{1,5},{3,7},{5,1},{7,3}} | collective-permute-start | bytes 6291464 | tf_op jit(solution)/shard_map/ppermute | solution.py:454
  739.5 105.0 %collective-permute-start.26 = (bf16[1024,1024]{1,0:T(8,128)(2,1)}, bf16[1024,1024]{1,0:T(8,128)(2,1)}, u32[]{:S(2)}, u32[]{:S(2)}) collective-permute-start(bf16[1024,1024]{1,0:T(8,128)(2,1)} %collective-permute-done.22.refs_3_), channel_id=1, source_target_pairs={{0,4},{2,6},{4,0},{6,2},{1,5},{3,7},{5,1},{7,3}} | collective-permute-start | bytes 6291464 | tf_op jit(solution)/shard_map/ppermute | solution.py:454
  843.4 312.7 %collective-permute-start.18 = (bf16[4096,1024]{1,0:T(8,128)(2,1)}, bf16[4096,1024]{1,0:T(8,128)(2,1)}, u32[]{:S(2)}, u32[]{:S(2)}) collective-permute-start(bf16[4096,1024]{1,0:T(8,128)(2,1)} %get-tuple-element.137.w2_hbm.refs_4_), channel_id=1, source_target_pairs={{0,1},{1,0},{2,3},{3,2},{4,5},{5,4},{6,7},{7,6}} | collective-permute-start | bytes 25165832 | tf_op jit(solution)/shard_map/ppermute | solution.py:458
  843.4 241.8 %collective-permute-start.9 = (bf16[1024,4096]{1,0:T(8,128)(2,1)}, bf16[1024,4096]{1,0:T(8,128)(2,1)}, u32[]{:S(2)}, u32[]{:S(2)}) collective-permute-start(bf16[1024,4096]{1,0:T(8,128)(2,1)} %get-tuple-element.135.w1_ref), channel_id=1, source_target_pairs={{0,1},{1,0},{2,3},{3,2},{4,5},{5,4},{6,7},{7,6}} | collective-permute-start | bytes 25165832 | tf_op jit(solution)/shard_map/ppermute | solution.py:458
  844.4 93.2 %collective-permute-start.15 = (bf16[256,4096]{1,0:T(8,128)(2,1)}, bf16[256,4096]{1,0:T(8,128)(2,1)}, u32[]{:S(2)}, u32[]{:S(2)}) collective-permute-start(bf16[256,4096]{1,0:T(8,128)(2,1)} %collective-permute-done.11.refs_1_), channel_id=1, source_target_pairs={{0,4},{2,6},{4,0},{6,2},{1,5},{3,7},{5,1},{7,3}} | collective-permute-start | bytes 6291464 | tf_op jit(solution)/shard_map/ppermute | solution.py:454
  846.0 135.7 %collective-permute-start.16 = (bf16[256,4096]{1,0:T(8,128)(2,1)}, bf16[256,4096]{1,0:T(8,128)(2,1)}, u32[]{:S(2)}, u32[]{:S(2)}) collective-permute-start(bf16[256,4096]{1,0:T(8,128)(2,1)} %collective-permute-done.12.refs_2_), channel_id=1, source_target_pairs={{0,4},{2,6},{4,0},{6,2},{1,5},{3,7},{5,1},{7,3}} | collective-permute-start | bytes 6291464 | tf_op jit(solution)/shard_map/ppermute | solution.py:454
  894.8 330.7 %collective-permute-start.27 = (bf16[4096,1024]{1,0:T(8,128)(2,1)}, bf16[4096,1024]{1,0:T(8,128)(2,1)}, u32[]{:S(2)}, u32[]{:S(2)}) collective-permute-start(bf16[4096,1024]{1,0:T(8,128)(2,1)} %get-tuple-element.141.w2_hbm.refs_4_), channel_id=1, source_target_pairs={{0,1},{1,0},{2,3},{3,2},{4,5},{5,4},{6,7},{7,6}} | collective-permute-start | bytes 25165832 | tf_op jit(solution)/shard_map/ppermute | solution.py:458
  937.7 331.5 %collective-permute-start = (bf16[1024,4096]{1,0:T(8,128)(2,1)}, bf16[1024,4096]{1,0:T(8,128)(2,1)}, u32[]{:S(2)}, u32[]{:S(2)}) collective-permute-start(bf16[1024,4096]{1,0:T(8,128)(2,1)} %get-tuple-element.138.w1_ref.refs_5_), channel_id=1, source_target_pairs={{0,1},{1,0},{2,3},{3,2},{4,5},{5,4},{6,7},{7,6}} | collective-permute-start | bytes 25165832 | tf_op jit(solution)/shard_map/ppermute | solution.py:458
  1083.8 70.8 %collective-permute-start.5 = (bf16[256,4096]{1,0:T(8,128)(2,1)}, bf16[256,4096]{1,0:T(8,128)(2,1)}, u32[]{:S(2)}, u32[]{:S(2)}) collective-permute-start(bf16[256,4096]{1,0:T(8,128)(2,1)} %collective-permute-done.1.refs_0_), channel_id=1, source_target_pairs={{0,4},{2,6},{4,0},{6,2},{1,5},{3,7},{5,1},{7,3}} | collective-permute-start | bytes 6291464 | tf_op jit(solution)/shard_map/ppermute | solution.py:454
  1085.3 138.6 %collective-permute-start.6 = (bf16[256,4096]{1,0:T(8,128)(2,1)}, bf16[256,4096]{1,0:T(8,128)(2,1)}, u32[]{:S(2)}, u32[]{:S(2)}) collective-permute-start(bf16[256,4096]{1,0:T(8,128)(2,1)} %collective-permute-done.2.refs_1_), channel_id=1, source_target_pairs={{0,4},{2,6},{4,0},{6,2},{1,5},{3,7},{5,1},{7,3}} | collective-permute-start | bytes 6291464 | tf_op jit(solution)/shard_map/ppermute | solution.py:454
  1154.6 112.6 %collective-permute-start.7 = (bf16[256,4096]{1,0:T(8,128)(2,1)}, bf16[256,4096]{1,0:T(8,128)(2,1)}, u32[]{:S(2)}, u32[]{:S(2)}) collective-permute-start(bf16[256,4096]{1,0:T(8,128)(2,1)} %collective-permute-done.3.refs_2_), channel_id=1, source_target_pairs={{0,4},{2,6},{4,0},{6,2},{1,5},{3,7},{5,1},{7,3}} | collective-permute-start | bytes 6291464 | tf_op jit(solution)/shard_map/ppermute | solution.py:454
  1156.1 111.5 %collective-permute-start.8 = (bf16[256,4096]{1,0:T(8,128)(2,1)}, bf16[256,4096]{1,0:T(8,128)(2,1)}, u32[]{:S(2)}, u32[]{:S(2)}) collective-permute-start(bf16[256,4096]{1,0:T(8,128)(2,1)} %collective-permute-done.4.refs_3_), channel_id=1, source_target_pairs={{0,4},{2,6},{4,0},{6,2},{1,5},{3,7},{5,1},{7,3}} | collective-permute-start | bytes 6291464 | tf_op jit(solution)/shard_map/ppermute | solution.py:454
  1223.9 113.2 %collective-permute-start.30 = (bf16[1024,1024]{1,0:T(8,128)(2,1)}, bf16[1024,1024]{1,0:T(8,128)(2,1)}, u32[]{:S(2)}, u32[]{:S(2)}) collective-permute-start(bf16[1024,1024]{1,0:T(8,128)(2,1)} %collective-permute-done.28.refs_0_), channel_id=1, source_target_pairs={{0,4},{2,6},{4,0},{6,2},{1,5},{3,7},{5,1},{7,3}} | collective-permute-start | bytes 6291464 | tf_op jit(solution)/shard_map/ppermute | solution.py:454
  1225.5 128.9 %collective-permute-start.31 = (bf16[1024,1024]{1,0:T(8,128)(2,1)}, bf16[1024,1024]{1,0:T(8,128)(2,1)}, u32[]{:S(2)}, u32[]{:S(2)}) collective-permute-start(bf16[1024,1024]{1,0:T(8,128)(2,1)} %collective-permute-done.29.refs_1_), channel_id=1, source_target_pairs={{0,4},{2,6},{4,0},{6,2},{1,5},{3,7},{5,1},{7,3}} | collective-permute-start | bytes 6291464 | tf_op jit(solution)/shard_map/ppermute | solution.py:454
  1267.2 180.0 %collective-permute-start.64 = (bf16[1024,1024]{1,0:T(8,128)(2,1)}, bf16[1024,1024]{1,0:T(8,128)(2,1)}, u32[]{:S(2)}, u32[]{:S(2)}) collective-permute-start(bf16[1024,1024]{1,0:T(8,128)(2,1)} %get-tuple-element.262), channel_id=1, source_target_pairs={{0,2},{2,0},{4,6},{6,4},{1,3},{3,1},{5,7},{7,5}} | collective-permute-start | bytes 6291464 | tf_op jit(solution)/shard_map/ppermute | solution.py:453
  1267.6 181.3 %collective-permute-start.65 = (bf16[1024,1024]{1,0:T(8,128)(2,1)}, bf16[1024,1024]{1,0:T(8,128)(2,1)}, u32[]{:S(2)}, u32[]{:S(2)}) collective-permute-start(bf16[1024,1024]{1,0:T(8,128)(2,1)} %get-tuple-element.263), channel_id=1, source_target_pairs={{0,2},{2,0},{4,6},{6,4},{1,3},{3,1},{5,7},{7,5}} | collective-permute-start | bytes 6291464 | tf_op jit(solution)/shard_map/ppermute | solution.py:453
  1269.2 180.0 %collective-permute-start.66 = (bf16[1024,1024]{1,0:T(8,128)(2,1)}, bf16[1024,1024]{1,0:T(8,128)(2,1)}, u32[]{:S(2)}, u32[]{:S(2)}) collective-permute-start(bf16[1024,1024]{1,0:T(8,128)(2,1)} %get-tuple-element.264), channel_id=1, source_target_pairs={{0,2},{2,0},{4,6},{6,4},{1,3},{3,1},{5,7},{7,5}} | collective-permute-start | bytes 6291464 | tf_op jit(solution)/shard_map/ppermute | solution.py:453
  1337.1 113.7 %collective-permute-start.67 = (bf16[1024,1024]{1,0:T(8,128)(2,1)}, bf16[1024,1024]{1,0:T(8,128)(2,1)}, u32[]{:S(2)}, u32[]{:S(2)}) collective-permute-start(bf16[1024,1024]{1,0:T(8,128)(2,1)} %get-tuple-element.265), channel_id=1, source_target_pairs={{0,2},{2,0},{4,6},{6,4},{1,3},{3,1},{5,7},{7,5}} | collective-permute-start | bytes 6291464 | tf_op jit(solution)/shard_map/ppermute | solution.py:453
  1354.4 151.8 %collective-permute-start.61 = (bf16[1024,1024]{1,0:T(8,128)(2,1)}, bf16[1024,1024]{1,0:T(8,128)(2,1)}, u32[]{:S(2)}, u32[]{:S(2)}) collective-permute-start(bf16[1024,1024]{1,0:T(8,128)(2,1)} %get-tuple-element.260), channel_id=1, source_target_pairs={{0,2},{2,0},{4,6},{6,4},{1,3},{3,1},{5,7},{7,5}} | collective-permute-start | bytes 6291464 | tf_op jit(solution)/shard_map/ppermute | solution.py:453
  1447.2 93.6 %collective-permute-start.59 = (bf16[1024,1024]{1,0:T(8,128)(2,1)}, bf16[1024,1024]{1,0:T(8,128)(2,1)}, u32[]{:S(2)}, u32[]{:S(2)}) collective-permute-start(bf16[1024,1024]{1,0:T(8,128)(2,1)} %get-tuple-element.259), channel_id=1, source_target_pairs={{0,2},{2,0},{4,6},{6,4},{1,3},{3,1},{5,7},{7,5}} | collective-permute-start | bytes 6291464 | tf_op jit(solution)/shard_map/ppermute | solution.py:453
  1448.8 136.9 %collective-permute-start.57 = (bf16[1024,1024]{1,0:T(8,128)(2,1)}, bf16[1024,1024]{1,0:T(8,128)(2,1)}, u32[]{:S(2)}, u32[]{:S(2)}) collective-permute-start(bf16[1024,1024]{1,0:T(8,128)(2,1)} %get-tuple-element.258), channel_id=1, source_target_pairs={{0,2},{2,0},{4,6},{6,4},{1,3},{3,1},{5,7},{7,5}} | collective-permute-start | bytes 6291464 | tf_op jit(solution)/shard_map/ppermute | solution.py:453
  1449.2 181.4 %collective-permute-start.55 = (bf16[1024,1024]{1,0:T(8,128)(2,1)}, bf16[1024,1024]{1,0:T(8,128)(2,1)}, u32[]{:S(2)}, u32[]{:S(2)}) collective-permute-start(bf16[1024,1024]{1,0:T(8,128)(2,1)} %get-tuple-element.257), channel_id=1, source_target_pairs={{0,2},{2,0},{4,6},{6,4},{1,3},{3,1},{5,7},{7,5}} | collective-permute-start | bytes 6291464 | tf_op jit(solution)/shard_map/ppermute | solution.py:453
  1450.9 224.7 %collective-permute-start.46 = (bf16[256,4096]{1,0:T(8,128)(2,1)}, bf16[256,4096]{1,0:T(8,128)(2,1)}, u32[]{:S(2)}, u32[]{:S(2)}) collective-permute-start(bf16[256,4096]{1,0:T(8,128)(2,1)} %get-tuple-element.252), channel_id=1, source_target_pairs={{0,2},{2,0},{4,6},{6,4},{1,3},{3,1},{5,7},{7,5}} | collective-permute-start | bytes 6291464 | tf_op jit(solution)/shard_map/ppermute | solution.py:453
  1506.1 233.2 %collective-permute-start.47 = (bf16[256,4096]{1,0:T(8,128)(2,1)}, bf16[256,4096]{1,0:T(8,128)(2,1)}, u32[]{:S(2)}, u32[]{:S(2)}) collective-permute-start(bf16[256,4096]{1,0:T(8,128)(2,1)} %get-tuple-element.253), channel_id=1, source_target_pairs={{0,2},{2,0},{4,6},{6,4},{1,3},{3,1},{5,7},{7,5}} | collective-permute-start | bytes 6291464 | tf_op jit(solution)/shard_map/ppermute | solution.py:453
  1540.7 224.7 %collective-permute-start.48 = (bf16[256,4096]{1,0:T(8,128)(2,1)}, bf16[256,4096]{1,0:T(8,128)(2,1)}, u32[]{:S(2)}, u32[]{:S(2)}) collective-permute-start(bf16[256,4096]{1,0:T(8,128)(2,1)} %get-tuple-element.254), channel_id=1, source_target_pairs={{0,2},{2,0},{4,6},{6,4},{1,3},{3,1},{5,7},{7,5}} | collective-permute-start | bytes 6291464 | tf_op jit(solution)/shard_map/ppermute | solution.py:453
  1585.7 224.7 %collective-permute-start.49 = (bf16[256,4096]{1,0:T(8,128)(2,1)}, bf16[256,4096]{1,0:T(8,128)(2,1)}, u32[]{:S(2)}, u32[]{:S(2)}) collective-permute-start(bf16[256,4096]{1,0:T(8,128)(2,1)} %get-tuple-element.255), channel_id=1, source_target_pairs={{0,2},{2,0},{4,6},{6,4},{1,3},{3,1},{5,7},{7,5}} | collective-permute-start | bytes 6291464 | tf_op jit(solution)/shard_map/ppermute | solution.py:453
  1630.6 224.7 %collective-permute-start.37 = (bf16[256,4096]{1,0:T(8,128)(2,1)}, bf16[256,4096]{1,0:T(8,128)(2,1)}, u32[]{:S(2)}, u32[]{:S(2)}) collective-permute-start(bf16[256,4096]{1,0:T(8,128)(2,1)} %get-tuple-element.240), channel_id=1, source_target_pairs={{0,2},{2,0},{4,6},{6,4},{1,3},{3,1},{5,7},{7,5}} | collective-permute-start | bytes 6291464 | tf_op jit(solution)/shard_map/ppermute | solution.py:453
  1675.6 224.7 %collective-permute-start.38 = (bf16[256,4096]{1,0:T(8,128)(2,1)}, bf16[256,4096]{1,0:T(8,128)(2,1)}, u32[]{:S(2)}, u32[]{:S(2)}) collective-permute-start(bf16[256,4096]{1,0:T(8,128)(2,1)} %get-tuple-element.241), channel_id=1, source_target_pairs={{0,2},{2,0},{4,6},{6,4},{1,3},{3,1},{5,7},{7,5}} | collective-permute-start | bytes 6291464 | tf_op jit(solution)/shard_map/ppermute | solution.py:453
  1739.4 220.3 %collective-permute-start.39 = (bf16[256,4096]{1,0:T(8,128)(2,1)}, bf16[256,4096]{1,0:T(8,128)(2,1)}, u32[]{:S(2)}, u32[]{:S(2)}) collective-permute-start(bf16[256,4096]{1,0:T(8,128)(2,1)} %get-tuple-element.242), channel_id=1, source_target_pairs={{0,2},{2,0},{4,6},{6,4},{1,3},{3,1},{5,7},{7,5}} | collective-permute-start | bytes 6291464 | tf_op jit(solution)/shard_map/ppermute | solution.py:453
  1765.5 220.1 %collective-permute-start.40 = (bf16[256,4096]{1,0:T(8,128)(2,1)}, bf16[256,4096]{1,0:T(8,128)(2,1)}, u32[]{:S(2)}, u32[]{:S(2)}) collective-permute-start(bf16[256,4096]{1,0:T(8,128)(2,1)} %get-tuple-element.243), channel_id=1, source_target_pairs={{0,2},{2,0},{4,6},{6,4},{1,3},{3,1},{5,7},{7,5}} | collective-permute-start | bytes 6291464 | tf_op jit(solution)/shard_map/ppermute | solution.py:453
  1810.4 176.7 %collective-permute-start.68 = (bf16[1024,1024]{1,0:T(8,128)(2,1)}, bf16[1024,1024]{1,0:T(8,128)(2,1)}, u32[]{:S(2)}, u32[]{:S(2)}) collective-permute-start(bf16[1024,1024]{1,0:T(8,128)(2,1)} %collective-permute-done.64.refs_0_), channel_id=1, source_target_pairs={{0,4},{2,6},{4,0},{6,2},{1,5},{3,7},{5,1},{7,3}} | collective-permute-start | bytes 6291464 | tf_op jit(solution)/shard_map/ppermute | solution.py:454
  1855.3 132.2 %collective-permute-start.69 = (bf16[1024,1024]{1,0:T(8,128)(2,1)}, bf16[1024,1024]{1,0:T(8,128)(2,1)}, u32[]{:S(2)}, u32[]{:S(2)}) collective-permute-start(bf16[1024,1024]{1,0:T(8,128)(2,1)} %collective-permute-done.65.refs_1_), channel_id=1, source_target_pairs={{0,4},{2,6},{4,0},{6,2},{1,5},{3,7},{5,1},{7,3}} | collective-permute-start | bytes 6291464 | tf_op jit(solution)/shard_map/ppermute | solution.py:454
  1900.3 88.8 %collective-permute-start.70 = (bf16[1024,1024]{1,0:T(8,128)(2,1)}, bf16[1024,1024]{1,0:T(8,128)(2,1)}, u32[]{:S(2)}, u32[]{:S(2)}) collective-permute-start(bf16[1024,1024]{1,0:T(8,128)(2,1)} %collective-permute-done.66.refs_2_), channel_id=1, source_target_pairs={{0,4},{2,6},{4,0},{6,2},{1,5},{3,7},{5,1},{7,3}} | collective-permute-start | bytes 6291464 | tf_op jit(solution)/shard_map/ppermute | solution.py:454
  1959.7 89.8 %collective-permute-start.71 = (bf16[1024,1024]{1,0:T(8,128)(2,1)}, bf16[1024,1024]{1,0:T(8,128)(2,1)}, u32[]{:S(2)}, u32[]{:S(2)}) collective-permute-start(bf16[1024,1024]{1,0:T(8,128)(2,1)} %collective-permute-done.67.refs_3_), channel_id=1, source_target_pairs={{0,4},{2,6},{4,0},{6,2},{1,5},{3,7},{5,1},{7,3}} | collective-permute-start | bytes 6291464 | tf_op jit(solution)/shard_map/ppermute | solution.py:454
  1985.5 68.0 %collective-permute-start.62 = (bf16[1024,1024]{1,0:T(8,128)(2,1)}, bf16[1024,1024]{1,0:T(8,128)(2,1)}, u32[]{:S(2)}, u32[]{:S(2)}) collective-permute-start(bf16[1024,1024]{1,0:T(8,128)(2,1)} %collective-permute-done.61.refs_0_), channel_id=1, source_target_pairs={{0,4},{2,6},{4,0},{6,2},{1,5},{3,7},{5,1},{7,3}} | collective-permute-start | bytes 6291464 | tf_op jit(solution)/shard_map/ppermute | solution.py:454
  1987.1 111.4 %collective-permute-start.60 = (bf16[1024,1024]{1,0:T(8,128)(2,1)}, bf16[1024,1024]{1,0:T(8,128)(2,1)}, u32[]{:S(2)}, u32[]{:S(2)}) collective-permute-start(bf16[1024,1024]{1,0:T(8,128)(2,1)} %collective-permute-done.59.refs_0_), channel_id=1, source_target_pairs={{0,4},{2,6},{4,0},{6,2},{1,5},{3,7},{5,1},{7,3}} | collective-permute-start | bytes 6291464 | tf_op jit(solution)/shard_map/ppermute | solution.py:454
  1987.6 155.8 %collective-permute-start.58 = (bf16[1024,1024]{1,0:T(8,128)(2,1)}, bf16[1024,1024]{1,0:T(8,128)(2,1)}, u32[]{:S(2)}, u32[]{:S(2)}) collective-permute-start(bf16[1024,1024]{1,0:T(8,128)(2,1)} %collective-permute-done.57.refs_0_), channel_id=1, source_target_pairs={{0,4},{2,6},{4,0},{6,2},{1,5},{3,7},{5,1},{7,3}} | collective-permute-start | bytes 6291464 | tf_op jit(solution)/shard_map/ppermute | solution.py:454
  1989.1 199.2 %collective-permute-start.56 = (bf16[1024,1024]{1,0:T(8,128)(2,1)}, bf16[1024,1024]{1,0:T(8,128)(2,1)}, u32[]{:S(2)}, u32[]{:S(2)}) collective-permute-start(bf16[1024,1024]{1,0:T(8,128)(2,1)} %collective-permute-done.55.refs_0_), channel_id=1, source_target_pairs={{0,4},{2,6},{4,0},{6,2},{1,5},{3,7},{5,1},{7,3}} | collective-permute-start | bytes 6291464 | tf_op jit(solution)/shard_map/ppermute | solution.py:454
  2049.5 321.8 %collective-permute-start.63 = (bf16[4096,1024]{1,0:T(8,128)(2,1)}, bf16[4096,1024]{1,0:T(8,128)(2,1)}, u32[]{:S(2)}, u32[]{:S(2)}) collective-permute-start(bf16[4096,1024]{1,0:T(8,128)(2,1)} %get-tuple-element.199.w2_hbm.refs_4_), channel_id=1, source_target_pairs={{0,1},{1,0},{2,3},{3,2},{4,5},{5,4},{6,7},{7,6}} | collective-permute-start | bytes 25165832 | tf_op jit(solution)/shard_map/ppermute | solution.py:458
  2053.5 317.8 %collective-permute-start.54 = (bf16[4096,1024]{1,0:T(8,128)(2,1)}, bf16[4096,1024]{1,0:T(8,128)(2,1)}, u32[]{:S(2)}, u32[]{:S(2)}) collective-permute-start(bf16[4096,1024]{1,0:T(8,128)(2,1)} %get-tuple-element.210.w2_hbm.refs_4_), channel_id=1, source_target_pairs={{0,1},{1,0},{2,3},{3,2},{4,5},{5,4},{6,7},{7,6}} | collective-permute-start | bytes 25165832 | tf_op jit(solution)/shard_map/ppermute | solution.py:458
  2098.4 274.9 %collective-permute-start.45 = (bf16[1024,4096]{1,0:T(8,128)(2,1)}, bf16[1024,4096]{1,0:T(8,128)(2,1)}, u32[]{:S(2)}, u32[]{:S(2)}) collective-permute-start(bf16[1024,4096]{1,0:T(8,128)(2,1)} %get-tuple-element.192.w1_ref), channel_id=1, source_target_pairs={{0,1},{1,0},{2,3},{3,2},{4,5},{5,4},{6,7},{7,6}} | collective-permute-start | bytes 25165832 | tf_op jit(solution)/shard_map/ppermute | solution.py:458
  2143.4 93.8 %collective-permute-start.50 = (bf16[256,4096]{1,0:T(8,128)(2,1)}, bf16[256,4096]{1,0:T(8,128)(2,1)}, u32[]{:S(2)}, u32[]{:S(2)}) collective-permute-start(bf16[256,4096]{1,0:T(8,128)(2,1)} %collective-permute-done.46.refs_0_), channel_id=1, source_target_pairs={{0,4},{2,6},{4,0},{6,2},{1,5},{3,7},{5,1},{7,3}} | collective-permute-start | bytes 6291464 | tf_op jit(solution)/shard_map/ppermute | solution.py:454
  2188.3 86.9 %collective-permute-start.51 = (bf16[256,4096]{1,0:T(8,128)(2,1)}, bf16[256,4096]{1,0:T(8,128)(2,1)}, u32[]{:S(2)}, u32[]{:S(2)}) collective-permute-start(bf16[256,4096]{1,0:T(8,128)(2,1)} %collective-permute-done.47.refs_1_), channel_id=1, source_target_pairs={{0,4},{2,6},{4,0},{6,2},{1,5},{3,7},{5,1},{7,3}} | collective-permute-start | bytes 6291464 | tf_op jit(solution)/shard_map/ppermute | solution.py:454
  2237.1 302.8 %collective-permute-start.36 = (bf16[1024,4096]{1,0:T(8,128)(2,1)}, bf16[1024,4096]{1,0:T(8,128)(2,1)}, u32[]{:S(2)}, u32[]{:S(2)}) collective-permute-start(bf16[1024,4096]{1,0:T(8,128)(2,1)} %get-tuple-element.200.w1_ref.refs_5_), channel_id=1, source_target_pairs={{0,1},{1,0},{2,3},{3,2},{4,5},{5,4},{6,7},{7,6}} | collective-permute-start | bytes 25165832 | tf_op jit(solution)/shard_map/ppermute | solution.py:458
  2368.8 125.8 %collective-permute-start.41 = (bf16[256,4096]{1,0:T(8,128)(2,1)}, bf16[256,4096]{1,0:T(8,128)(2,1)}, u32[]{:S(2)}, u32[]{:S(2)}) collective-permute-start(bf16[256,4096]{1,0:T(8,128)(2,1)} %collective-permute-done.37.refs_0_), channel_id=1, source_target_pairs={{0,4},{2,6},{4,0},{6,2},{1,5},{3,7},{5,1},{7,3}} | collective-permute-start | bytes 6291464 | tf_op jit(solution)/shard_map/ppermute | solution.py:454
  2371.3 123.3 %collective-permute-start.42 = (bf16[256,4096]{1,0:T(8,128)(2,1)}, bf16[256,4096]{1,0:T(8,128)(2,1)}, u32[]{:S(2)}, u32[]{:S(2)}) collective-permute-start(bf16[256,4096]{1,0:T(8,128)(2,1)} %collective-permute-done.38.refs_1_), channel_id=1, source_target_pairs={{0,4},{2,6},{4,0},{6,2},{1,5},{3,7},{5,1},{7,3}} | collective-permute-start | bytes 6291464 | tf_op jit(solution)/shard_map/ppermute | solution.py:454
  2371.3 136.7 %collective-permute-start.43 = (bf16[256,4096]{1,0:T(8,128)(2,1)}, bf16[256,4096]{1,0:T(8,128)(2,1)}, u32[]{:S(2)}, u32[]{:S(2)}) collective-permute-start(bf16[256,4096]{1,0:T(8,128)(2,1)} %collective-permute-done.39.refs_2_), channel_id=1, source_target_pairs={{0,4},{2,6},{4,0},{6,2},{1,5},{3,7},{5,1},{7,3}} | collective-permute-start | bytes 6291464 | tf_op jit(solution)/shard_map/ppermute | solution.py:454
  2373.4 166.6 %collective-permute-start.44 = (bf16[256,4096]{1,0:T(8,128)(2,1)}, bf16[256,4096]{1,0:T(8,128)(2,1)}, u32[]{:S(2)}, u32[]{:S(2)}) collective-permute-start(bf16[256,4096]{1,0:T(8,128)(2,1)} %collective-permute-done.40.refs_3_), channel_id=1, source_target_pairs={{0,4},{2,6},{4,0},{6,2},{1,5},{3,7},{5,1},{7,3}} | collective-permute-start | bytes 6291464 | tf_op jit(solution)/shard_map/ppermute | solution.py:454
  (8 other events, 417.9 us)
